TPU v7x, 32 devices: a whole 2x2x4 slice. The times are simulated.
32 devices in a mesh: section: 2 (over x), ctx: 4 (over z), tp: 4 (over y, core).
Axes of the slice: x: 2, y: 2, z: 4, core: 2. Of those that a mesh axis runs over, the one named last changes fastest.
Arguments:
- boundary: bfloat16 [2, 2, 1024, 2048], P('section', None, 'ctx', 'tp'), may hold values from -6 to 6
- doc_ids: int32 [2, 1024], replicated, may hold values from 0 to 3, never falling along the last dimension, each value on 1 to 512 neighbouring positions
- qkv_weight: bfloat16 [2, 3, 2048, 2048], P('section', None, 'ctx', 'tp'), may hold values from -0.125 to 0.125
- qkv_bias: bfloat16 [2, 3, 2048], P('section', None, ('tp', 'ctx')), may hold values from -3 to 3
- out_weight: bfloat16 [2, 2048, 2048], P('section', 'tp', 'ctx'), may hold values from -0.5 to 0.5
- out_bias: bfloat16 [2, 2048], P('section', ('tp', 'ctx')), may hold values from -3 to 3
- fc1_weight: bfloat16 [2, 2048, 8192], P('section', 'ctx', 'tp'), may hold values from -0.125 to 0.125
- fc1_bias: bfloat16 [2, 8192], P('section', ('tp', 'ctx')), may hold values from -3 to 3
- fc2_weight: bfloat16 [2, 8192, 2048], P('section', 'tp', 'ctx'), may hold values from -0.0625 to 0.0625
- fc2_bias: bfloat16 [2, 2048], P('section', ('tp', 'ctx')), may hold values from -3 to 3
- norm_gain: bfloat16 [2, 2048], P('section', ('tp', 'ctx')), may hold values from 0.099609375 to 1.8984375
- norm_shift: bfloat16 [2, 2048], P('section', ('tp', 'ctx')), may hold values from -3 to 3
Outputs:
- acts: bfloat16 [2, 2, 1024, 2048], P('section', None, 'ctx', 'tp')
- input_grads: bfloat16 [2, 2, 1024, 2048], P('section', None, 'ctx', 'tp')
- grad_qkv_weight: float32 [2, 3, 2048, 2048], P('section', None, 'ctx', 'tp')
- grad_qkv_bias: float32 [2, 3, 2048], P('section', None, ('tp', 'ctx'))
- grad_out_weight: float32 [2, 2048, 2048], P('section', 'tp', 'ctx')
- grad_out_bias: float32 [2, 2048], P('section', ('tp', 'ctx'))
- grad_fc1_weight: float32 [2, 2048, 8192], P('section', 'ctx', 'tp')
- grad_fc1_bias: float32 [2, 8192], P('section', ('tp', 'ctx'))
- grad_fc2_weight: float32 [2, 8192, 2048], P('section', 'tp', 'ctx')
- grad_fc2_bias: float32 [2, 2048], P('section', ('tp', 'ctx'))
- grad_norm_gain: float32 [2, 2048], P('section', ('tp', 'ctx'))
- grad_norm_shift: float32 [2, 2048], P('section', ('tp', 'ctx'))
Inputs may be any that keep to these rules, and one draw needn't show every extreme that they name: `doc_ids`: in each sequence the ids never fall; every id 0 to 3 covers 1 to 512 consecutive positions, and some id covers exactly 512.
All inputs are finite; a program needn't handle non-finite values.
Results may differ from a plain program's by a relative error of at most 0.024.
Values may be sent and summed in bfloat16 or wider, within the bound.
A program may use at most 320 MiB of HBM per device.

v0:
```python
import jax
import jax.numpy as jnp
from jax import lax
from jax.sharding import PartitionSpec as P

D = 2048
HD = 64
ROT = 32


EPS = 1e-05
GELU_C = 0.7978845608028654
GELU_K = 0.044715


def from_behind(value, axis, steps):
    count = lax.axis_size(axis)
    leading, last = (max(0, -steps), min(count, count - steps))
    return lax.ppermute(value, axis, [(source, source + steps) for source in range(leading, last)])


def gelu(value):
    inner = jnp.tanh(GELU_C * (value + GELU_K * value * value * value))
    return 0.5 * value * (1.0 + inner)


def gelu_slope(value):
    inner = jnp.tanh(GELU_C * (value + GELU_K * value * value * value))
    return 0.5 * (1.0 + inner) + 0.5 * value * (1.0 - inner * inner) * GELU_C * (
        1.0 + 3.0 * GELU_K * value * value
    )


def rope_tables(positions):
    half = ROT // 2
    freq = 10000.0 ** (-(jnp.arange(half).astype(jnp.float32) * 2.0 / ROT))
    angle = positions.astype(jnp.float32)[:, None] * freq[None, :]
    return (jnp.cos(angle), jnp.sin(angle))


def rotate(field, cosine, sine, sign):
    half = ROT // 2
    first = field[..., :half]
    second = field[..., half:ROT]
    cosine = cosine[:, None, :]
    sine = sine[:, None, :] * sign
    return jnp.concatenate(
        [first * cosine - second * sine, second * cosine + first * sine, field[..., ROT:]], axis=-1
    )


def local_layout(ids_full, ctx_index, tokens):
    length = ids_full.shape[0]
    local_ids = lax.dynamic_slice_in_dim(ids_full, ctx_index * tokens, tokens)
    start = jnp.sum((ids_full[None, :] < local_ids[:, None]).astype(jnp.int32), axis=1)
    query_at = ctx_index * tokens + jnp.arange(tokens, dtype=jnp.int32)
    key_at = jnp.arange(length, dtype=jnp.int32)
    allowed = (key_at[None, :] <= query_at[:, None]) & (ids_full[None, :] == local_ids[:, None])
    return (query_at - start, allowed)


def score_block(query, keys):
    return jnp.einsum("thd,shd->hts", query, keys, preferred_element_type=jnp.float32) * HD ** (
        -0.5
    )


def forward_layer(layer_in, ids_full, params, ctx_index):
    w_qkv, b_qkv, w_out, b_out, w_up, b_up, w_down, b_down, gain, shift = params
    tokens = layer_in.shape[0]
    heads = w_qkv.shape[2] // HD
    wide_in = layer_in.astype(jnp.float32)
    row_sums = lax.psum((jnp.sum(wide_in, axis=1), jnp.sum(wide_in * wide_in, axis=1)), "tp")
    row_mean = row_sums[0] / D
    variance = row_sums[1] / D - row_mean * row_mean
    inverse_std = lax.rsqrt(variance + EPS)
    centered = (wide_in - row_mean[:, None]) * inverse_std[:, None]
    normed_part = (centered * gain.astype(jnp.float32) + shift.astype(jnp.float32)).astype(
        jnp.bfloat16
    )
    normed = lax.all_gather(normed_part, "tp", axis=1, tiled=True)
    positions, allowed = local_layout(ids_full, ctx_index, tokens)
    cosine, sine = rope_tables(positions)
    projected = (
        jnp.einsum("td,cde->cte", normed, w_qkv, preferred_element_type=jnp.float32)
        + b_qkv.astype(jnp.float32)[:, None, :]
    )
    query = rotate(projected[0].reshape(tokens, heads, HD), cosine, sine, 1.0).astype(jnp.bfloat16)
    key_rot = rotate(projected[1].reshape(tokens, heads, HD), cosine, sine, 1.0).astype(
        jnp.bfloat16
    )
    value_part = projected[2].reshape(tokens, heads, HD).astype(jnp.bfloat16)
    key_all, value_all = (
        lax.all_gather(key_rot, "ctx", axis=0, tiled=True),
        lax.all_gather(value_part, "ctx", axis=0, tiled=True),
    )
    scores = score_block(query, key_all)
    totals = jnp.sum(jnp.where(allowed[None], jnp.exp(scores), 0.0), axis=2)
    log_total = jnp.log(totals)
    probs = jnp.where(allowed[None], jnp.exp(scores - log_total[:, :, None]), 0.0).astype(
        jnp.bfloat16
    )
    attended = (
        jnp.einsum("hts,shd->thd", probs, value_all, preferred_element_type=jnp.float32)
        .astype(jnp.bfloat16)
        .reshape(tokens, heads * HD)
    )
    hidden_pre = jnp.dot(normed, w_up, preferred_element_type=jnp.float32) + b_up.astype(
        jnp.float32
    )
    hidden = gelu(hidden_pre).astype(jnp.bfloat16)
    summands = jnp.dot(attended, w_out, preferred_element_type=jnp.float32) + jnp.dot(
        hidden, w_down, preferred_element_type=jnp.float32
    )
    mixed = lax.psum_scatter(summands, "tp", scatter_dimension=1, tiled=True)
    layer_out = (wide_in + mixed + b_out.astype(jnp.float32) + b_down.astype(jnp.float32)).astype(
        jnp.bfloat16
    )
    kept = (key_rot, value_part)
    return (
        layer_out,
        (centered, inverse_std, normed, query, kept, attended, log_total, hidden_pre, hidden),
    )


def backward_layer(incoming, saved, ids_full, params, ctx_index):
    w_qkv, b_qkv, w_out, b_out, w_up, b_up, w_down, b_down, gain, shift = params
    centered, inverse_std, normed, query, kept, attended, log_total, hidden_pre, hidden = saved
    tokens = query.shape[0]
    heads = query.shape[1]
    wide_grad = incoming.astype(jnp.float32)
    grad_rows = lax.all_gather(incoming, "tp", axis=1, tiled=True)
    grad_out_bias = jnp.sum(wide_grad, axis=0)
    grad_out = jnp.einsum("tk,te->ke", attended, grad_rows, preferred_element_type=jnp.float32)
    d_attended = jnp.einsum(
        "te,ke->tk", grad_rows, w_out, preferred_element_type=jnp.float32
    ).astype(jnp.bfloat16)
    grad_down = jnp.einsum("tf,te->fe", hidden, grad_rows, preferred_element_type=jnp.float32)
    d_pre = jnp.einsum(
        "te,fe->tf", grad_rows, w_down, preferred_element_type=jnp.float32
    ) * gelu_slope(hidden_pre)
    grad_up_bias = jnp.sum(d_pre, axis=0)
    d_hidden = d_pre.astype(jnp.bfloat16)
    grad_up = jnp.einsum("td,tf->df", normed, d_hidden, preferred_element_type=jnp.float32)
    key_all, value_all = (
        lax.all_gather(kept[0], "ctx", axis=0, tiled=True),
        lax.all_gather(kept[1], "ctx", axis=0, tiled=True),
    )
    positions, allowed = local_layout(ids_full, ctx_index, tokens)
    cosine, sine = rope_tables(positions)
    d_heads = d_attended.reshape(tokens, heads, HD)
    out_heads = attended.reshape(tokens, heads, HD)
    delta = jnp.sum(d_heads.astype(jnp.float32) * out_heads.astype(jnp.float32), axis=2)
    scores = score_block(query, key_all)
    probs = jnp.where(allowed[None], jnp.exp(scores - log_total[:, :, None]), 0.0)
    d_probs = jnp.einsum("thd,shd->hts", d_heads, value_all, preferred_element_type=jnp.float32)
    d_scores = (probs * (d_probs - delta.T[:, :, None]) * HD ** (-0.5)).astype(jnp.bfloat16)
    d_query = jnp.einsum("hts,shd->thd", d_scores, key_all, preferred_element_type=jnp.float32)
    key_terms = jnp.einsum("hts,thd->shd", d_scores, query, preferred_element_type=jnp.float32)
    value_terms = jnp.einsum(
        "hts,thd->shd", probs.astype(jnp.bfloat16), d_heads, preferred_element_type=jnp.float32
    )
    d_key, d_value = (
        lax.psum_scatter(
            key_terms.astype(jnp.bfloat16), "ctx", scatter_dimension=0, tiled=True
        ).astype(jnp.float32),
        lax.psum_scatter(
            value_terms.astype(jnp.bfloat16), "ctx", scatter_dimension=0, tiled=True
        ).astype(jnp.float32),
    )
    d_projected = jnp.stack(
        [rotate(d_query, cosine, sine, -1.0), rotate(d_key, cosine, sine, -1.0), d_value]
    ).reshape(3, tokens, heads * HD)
    grad_qkv_bias = jnp.sum(d_projected, axis=1)
    d_qkv = d_projected.astype(jnp.bfloat16)
    grad_qkv = jnp.einsum("td,cte->cde", normed, d_qkv, preferred_element_type=jnp.float32)
    normed_terms = jnp.einsum("cte,cde->td", d_qkv, w_qkv, preferred_element_type=jnp.float32)
    normed_terms = normed_terms + jnp.einsum(
        "tf,df->td", d_hidden, w_up, preferred_element_type=jnp.float32
    )
    d_normed = lax.psum_scatter(
        normed_terms.astype(jnp.bfloat16), "tp", scatter_dimension=1, tiled=True
    ).astype(jnp.float32)
    grad_gain = jnp.sum(d_normed * centered, axis=0)
    grad_shift = jnp.sum(d_normed, axis=0)
    scaled = d_normed * gain.astype(jnp.float32)
    row_terms = lax.psum((jnp.sum(scaled, axis=1), jnp.sum(scaled * centered, axis=1)), "tp")
    grad_in = wide_grad + inverse_std[:, None] * (
        scaled - row_terms[0][:, None] / D - centered * (row_terms[1][:, None] / D)
    )
    grads = (
        grad_qkv,
        grad_qkv_bias,
        grad_out,
        grad_out_bias,
        grad_up,
        grad_up_bias,
        grad_down,
        grad_out_bias,
        grad_gain,
        grad_shift,
    )
    return (grad_in.astype(jnp.bfloat16), grads)


def shards(
    boundary,
    doc_ids,
    qkv_weight,
    qkv_bias,
    out_weight,
    out_bias,
    fc1_weight,
    fc1_bias,
    fc2_weight,
    fc2_bias,
    norm_gain,
    norm_shift,
):
    section = lax.axis_index("section")
    ctx_index = lax.axis_index("ctx")
    micro = boundary.shape[1]
    tokens = boundary.shape[2]
    width_part = boundary.shape[3]
    params = (
        lax.all_gather(qkv_weight[0], "ctx", axis=1, tiled=True),
        lax.all_gather(qkv_bias[0], "ctx", axis=1, tiled=True),
        lax.all_gather(out_weight[0], "ctx", axis=1, tiled=True),
        lax.all_gather(out_bias[0], "ctx", axis=0, tiled=True),
        lax.all_gather(fc1_weight[0], "ctx", axis=0, tiled=True),
        lax.all_gather(fc1_bias[0], "ctx", axis=0, tiled=True),
        lax.all_gather(fc2_weight[0], "ctx", axis=1, tiled=True),
        lax.all_gather(fc2_bias[0], "ctx", axis=0, tiled=True),
        lax.all_gather(norm_gain[0], "ctx", axis=0, tiled=True),
        lax.all_gather(norm_shift[0], "ctx", axis=0, tiled=True),
    )
    inputs = boundary[0]
    ticks = jnp.arange(micro + 1, dtype=jnp.int32)

    def forward_tick(received, tick):
        index = jnp.clip(tick - section, 0, micro - 1)
        first = lax.dynamic_index_in_dim(inputs, index, 0, keepdims=False)
        layer_in = jnp.where(section == 0, first, received)
        ids_full = lax.dynamic_index_in_dim(doc_ids, index, 0, keepdims=False)
        layer_out, saved = forward_layer(layer_in, ids_full, params, ctx_index)
        passed = from_behind(layer_out, "section", 1)
        return (passed, (layer_out, saved))

    start_zero = jnp.zeros((tokens, width_part), jnp.bfloat16)
    leftover, (outs_all, saved_all) = lax.scan(forward_tick, start_zero, ticks)
    held = lax.optimization_barrier(
        (
            (
                qkv_weight[0],
                qkv_bias[0],
                out_weight[0],
                out_bias[0],
                fc1_weight[0],
                fc1_bias[0],
                fc2_weight[0],
                fc2_bias[0],
                norm_gain[0],
                norm_shift[0],
            ),
            outs_all,
        )
    )[0]
    back_params = (
        lax.all_gather(held[0], "ctx", axis=1, tiled=True),
        lax.all_gather(held[1], "ctx", axis=1, tiled=True),
        lax.all_gather(held[2], "ctx", axis=1, tiled=True),
        lax.all_gather(held[3], "ctx", axis=0, tiled=True),
        lax.all_gather(held[4], "ctx", axis=0, tiled=True),
        lax.all_gather(held[5], "ctx", axis=0, tiled=True),
        lax.all_gather(held[6], "ctx", axis=1, tiled=True),
        lax.all_gather(held[7], "ctx", axis=0, tiled=True),
        lax.all_gather(held[8], "ctx", axis=0, tiled=True),
        lax.all_gather(held[9], "ctx", axis=0, tiled=True),
    )
    zero_grads = tuple((jnp.zeros(weight.shape, jnp.float32) for weight in params))

    def backward_tick(carry, tick):
        received, totals = carry
        raw_index = tick - (1 - section)
        valid = (raw_index >= 0) & (raw_index < micro)
        index = jnp.clip(raw_index, 0, micro - 1)
        cotangent = lax.dynamic_index_in_dim(inputs, index, 0, keepdims=False)
        incoming = jnp.where(section == 1, cotangent, received)
        incoming = jnp.where(valid, incoming, jnp.zeros_like(incoming))
        position_slot = index + section
        saved = jax.tree.map(
            lambda stacked: lax.dynamic_index_in_dim(stacked, position_slot, 0, keepdims=False),
            saved_all,
        )
        ids_full = lax.dynamic_index_in_dim(doc_ids, index, 0, keepdims=False)
        grad_in, terms = backward_layer(incoming, saved, ids_full, back_params, ctx_index)
        totals = tuple((total + term for total, term in zip(totals, terms)))
        passed = from_behind(grad_in, "section", -1)
        return ((passed, totals), grad_in)

    (leftover_grad, totals), grads_all = lax.scan(backward_tick, (start_zero, zero_grads), ticks)
    acts = lax.dynamic_slice_in_dim(outs_all, section, micro, 0)[None]
    input_grads = lax.dynamic_slice_in_dim(grads_all, 1 - section, micro, 0)[None]
    shares = (
        lax.psum_scatter(
            totals[0].astype(jnp.bfloat16), "ctx", scatter_dimension=1, tiled=True
        ).astype(jnp.float32),
        lax.psum_scatter(
            totals[1].astype(jnp.bfloat16), "ctx", scatter_dimension=1, tiled=True
        ).astype(jnp.float32),
        lax.psum_scatter(
            totals[2].astype(jnp.bfloat16), "ctx", scatter_dimension=1, tiled=True
        ).astype(jnp.float32),
        lax.psum_scatter(
            totals[3].astype(jnp.bfloat16), "ctx", scatter_dimension=0, tiled=True
        ).astype(jnp.float32),
        lax.psum_scatter(
            totals[4].astype(jnp.bfloat16), "ctx", scatter_dimension=0, tiled=True
        ).astype(jnp.float32),
        lax.psum_scatter(
            totals[5].astype(jnp.bfloat16), "ctx", scatter_dimension=0, tiled=True
        ).astype(jnp.float32),
        lax.psum_scatter(
            totals[6].astype(jnp.bfloat16), "ctx", scatter_dimension=1, tiled=True
        ).astype(jnp.float32),
        lax.psum_scatter(
            totals[7].astype(jnp.bfloat16), "ctx", scatter_dimension=0, tiled=True
        ).astype(jnp.float32),
        lax.psum_scatter(
            totals[8].astype(jnp.bfloat16), "ctx", scatter_dimension=0, tiled=True
        ).astype(jnp.float32),
        lax.psum_scatter(
            totals[9].astype(jnp.bfloat16), "ctx", scatter_dimension=0, tiled=True
        ).astype(jnp.float32),
    )
    return (
        acts,
        input_grads,
        shares[0][None],
        shares[1][None],
        shares[2][None],
        shares[3][None],
        shares[4][None],
        shares[5][None],
        shares[6][None],
        shares[7][None],
        shares[8][None],
        shares[9][None],
    )


def solution(mesh):
    in_specs = (
        P("section", None, "ctx", "tp"),
        P(),
        P("section", None, "ctx", "tp"),
        P("section", None, ("tp", "ctx")),
        P("section", "tp", "ctx"),
        P("section", ("tp", "ctx")),
        P("section", "ctx", "tp"),
        P("section", ("tp", "ctx")),
        P("section", "tp", "ctx"),
        P("section", ("tp", "ctx")),
        P("section", ("tp", "ctx")),
        P("section", ("tp", "ctx")),
    )
    out_specs = (
        P("section", None, "ctx", "tp"),
        P("section", None, "ctx", "tp"),
        P("section", None, "ctx", "tp"),
        P("section", None, ("tp", "ctx")),
        P("section", "tp", "ctx"),
        P("section", ("tp", "ctx")),
        P("section", "ctx", "tp"),
        P("section", ("tp", "ctx")),
        P("section", "tp", "ctx"),
        P("section", ("tp", "ctx")),
        P("section", ("tp", "ctx")),
        P("section", ("tp", "ctx")),
    )
    return jax.shard_map(shards, mesh=mesh, in_specs=in_specs, out_specs=out_specs, check_vma=False)
```

profile of v0, /device:TPU:0, one launch (start us, length us, event | category | flops | bytes accessed | tf_op | source)
XLA Modules:
  0.0 2482.1 jit_solution(12038437606748546442)
XLA Ops:
  72.4 101.5 %all-gather.42.cloned.1.call-done = bf16[1,3,2048,512]{3,2,1,0:T(8,128)(2,1)} async-done(((bf16[1,3,512,512]{3,2,1,0:T(8,128)(2,1)}), bf16[1,3,2048,512]{3,2,1,0:T(8,128)(2,1)}) %all-gather.42.cloned.1.call-update) | async-done | bytes 6291472 | tf_op jit(solution)/shard_map/all_gather | solution.py:226
  173.9 149.4 %all-gather.46.cloned.1.call-done = bf16[1,2048,2048]{2,1,0:T(8,128)(2,1)} async-done(((bf16[1,512,2048]{2,1,0:T(8,128)(2,1)}), bf16[1,2048,2048]{2,1,0:T(8,128)(2,1)}) %all-gather.46.cloned.1.call-update) | async-done | bytes 8388624 | tf_op jit(solution)/shard_map/all_gather | solution.py:230
  323.3 149.3 %all-gather.48.cloned.1.call-done = bf16[1,2048,2048]{2,1,0:T(8,128)(2,1)} async-done(((bf16[1,2048,512]{2,1,0:T(8,128)(2,1)}), bf16[1,2048,2048]{2,1,0:T(8,128)(2,1)}) %all-gather.48.cloned.1.call-update) | async-done | bytes 8388624 | tf_op jit(solution)/shard_map/all_gather | solution.py:232
  474.0 434.6 %while.71 = (s32[]{:T(128)}, bf16[256,512]{1,0:T(8,128)(2,1)S(1)}, bf16[3,256,512]{2,1,0:T(8,128)(2,1)}, f32[3,256,512]{2,1,0:T(8,128)}, f32[3,256]{1,0:T(4,128)...) while((s32[]{:T(128)}, bf16[256,512]{1,0:T(8,128)(2,1)S(1)}, ...), condition=%wide.region_8.9_spmd, body=%wide.region_0.8_spmd.sunk | while | flops 7012755456 | bytes 142612688 | solution.py:250
  545.3 23.8 all-gather.52.cloned.1.call-done
  587.2 19.3 reduce-scatter.22.cloned.1.call-done
  691.2 23.8 all-gather.52.cloned.1.call-done
  837.1 23.6 all-gather.52.cloned.1.call-done
  878.8 19.3 reduce-scatter.22.cloned.1.call-done
  922.2 35.3 %all-gather.34.cloned.1.call-done = bf16[512,2048]{1,0:T(8,128)(2,1)} async-done(((bf16[512,512]{1,0:T(8,128)(2,1)}), bf16[512,2048]{1,0:T(8,128)(2,1)}) %all-gather.34.cloned.1.call-update) | async-done | bytes 2097168 | tf_op jit(solution)/shard_map/all_gather | solution.py:271
  957.4 115.6 %all-gather.36.cloned.1.call-done = bf16[3,2048,512]{2,1,0:T(8,128)(2,1)} async-done(((bf16[3,512,512]{2,1,0:T(8,128)(2,1)}), bf16[3,2048,512]{2,1,0:T(8,128)(2,1)}) %all-gather.36.cloned.1.call-update) | async-done | bytes 6291472 | tf_op jit(solution)/shard_map/all_gather | solution.py:269
  1073.0 149.4 %all-gather.38.cloned.1.call-done = bf16[2048,2048]{1,0:T(8,128)(2,1)} async-done(((bf16[2048,512]{1,0:T(8,128)(2,1)}), bf16[2048,2048]{1,0:T(8,128)(2,1)}) %all-gather.38.cloned.1.call-update) | async-done | bytes 8388624 | tf_op jit(solution)/shard_map/all_gather | solution.py:275
  1222.4 149.2 %all-gather.40.cloned.1.call-done = bf16[2048,2048]{1,0:T(8,128)(2,1)} async-done(((bf16[512,2048]{1,0:T(8,128)(2,1)}), bf16[2048,2048]{1,0:T(8,128)(2,1)}) %all-gather.40.cloned.1.call-update) | async-done | bytes 8388624 | tf_op jit(solution)/shard_map/all_gather | solution.py:273
  1372.7 625.2 %while.72 = (s32[]{:T(128)}, bf16[256,512]{1,0:T(8,128)(2,1)S(1)}, f32[3,2048,512]{1,2,0:T(8,128)}, f32[3,512]{1,0:T(4,128)S(1)}, f32[512,2048]{1,0:T(8,128)}, /...) while((s32[]{:T(128)}, bf16[256,512]{1,0:T(8,128)(2,1)S(1)}, ...), condition=%wide.region_24.25_spmd.clone, body=%wide.region_9.24_spmd.clone.sunk | while | flops 14296822784 | bytes 286250144 | solution.py:301
  1410.0 29.2 %all-gather.58.cloned.1.call-done = bf16[1,1024,8,64]{1,3,2,0:T(8,128)(2,1)} async-done(((bf16[1,256,8,64]{1,3,2,0:T(8,128)(2,1)}), bf16[1,1024,8,64]{1,3,2,0:T(8,128)(2,1)}) %all-gather.58.cloned.1.call-update) | async-done | bytes 1048592 | tf_op jit(solution)/shard_map/while/body/eval_jaxpr/all_gather | solution.py:146
  1445.0 24.6 all-gather.60.cloned.1.call-done
  1511.1 23.9 reduce-scatter.24.cloned.1.call-done
  1612.0 29.2 %all-gather.58.cloned.1.call-done = bf16[1,1024,8,64]{1,3,2,0:T(8,128)(2,1)} async-done(((bf16[1,256,8,64]{1,3,2,0:T(8,128)(2,1)}), bf16[1,1024,8,64]{1,3,2,0:T(8,128)(2,1)}) %all-gather.58.cloned.1.call-update) | async-done | bytes 1048592 | tf_op jit(solution)/shard_map/while/body/eval_jaxpr/all_gather | solution.py:146
  1647.0 24.6 all-gather.60.cloned.1.call-done
  1815.1 29.2 %all-gather.58.cloned.1.call-done = bf16[1,1024,8,64]{1,3,2,0:T(8,128)(2,1)} async-done(((bf16[1,256,8,64]{1,3,2,0:T(8,128)(2,1)}), bf16[1,1024,8,64]{1,3,2,0:T(8,128)(2,1)}) %all-gather.58.cloned.1.call-update) | async-done | bytes 1048592 | tf_op jit(solution)/shard_map/while/body/eval_jaxpr/all_gather | solution.py:146
  1850.1 24.6 all-gather.60.cloned.1.call-done
  2065.6 110.2 %reduce-scatter.12.cloned.1.call-done = bf16[3,512,512]{2,1,0:T(8,128)(2,1)} async-done(((bf16[3,2048,512]{2,1,0:T(8,128)(2,1)}), bf16[3,512,512]{2,1,0:T(8,128)(2,1)}) %reduce-scatter.12.cloned.1.call-update) | async-done | bytes 1572880 | tf_op jit(solution)/shard_map/reduce_scatter | solution.py:305
  2179.3 144.0 %reduce-scatter.18.cloned.1.call-done = bf16[2048,512]{1,0:T(8,128)(2,1)} async-done(((bf16[2048,2048]{1,0:T(8,128)(2,1)}), bf16[2048,512]{1,0:T(8,128)(2,1)}) %reduce-scatter.18.cloned.1.call-update) | async-done | bytes 2097168 | tf_op jit(solution)/shard_map/reduce_scatter | solution.py:323
  2327.5 143.3 %reduce-scatter.16.cloned.1.call-done = bf16[512,2048]{1,0:T(8,128)(2,1)} async-done(((bf16[2048,2048]{1,0:T(8,128)(2,1)}), bf16[512,2048]{1,0:T(8,128)(2,1)}) %reduce-scatter.16.cloned.1.call-update) | async-done | bytes 2097168 | tf_op jit(solution)/shard_map/reduce_scatter | solution.py:317
  (637 shorter events, 901.6 us)
Async XLA Ops:
  7.2 65.2 %all-gather.44.cloned.1.call-start = ((), (), s32[]{:S(2)}) async-start(), calls=%async_computation.18 | async-start | bytes 2621440 | tf_op jit(solution)/shard_map/all_gather | solution.py:228
  8.0 165.9 %all-gather.42.cloned.1.call-start = ((), (), s32[]{:S(2)}) async-start(), calls=%async_computation.17 | async-start | bytes 7864320 | tf_op jit(solution)/shard_map/all_gather | solution.py:226
  8.7 314.6 %all-gather.46.cloned.1.call-start = ((), (), s32[]{:S(2)}) async-start(), calls=%async_computation.19 | async-start | bytes 10485760 | tf_op jit(solution)/shard_map/all_gather | solution.py:230
  9.5 463.1 %all-gather.48.cloned.1.call-start = ((), (), s32[]{:S(2)}) async-start(), calls=%async_computation.20 | async-start | bytes 10485760 | tf_op jit(solution)/shard_map/all_gather | solution.py:232
  511.3 95.2 %reduce-scatter.22.cloned.1.call-start = ((), (), s32[]{:S(2)}) async-start(), calls=%async_computation.25 | async-start | bytes 2621440 | tf_op jit(solution)/shard_map/while/body/eval_jaxpr/reduce_scatter | solution.py:115
  654.5 60.5 %all-gather.52.cloned.1.call-start = ((), (), s32[]{:S(2)}) async-start(), calls=%async_computation.23 | async-start | bytes 1310720 | tf_op jit(solution)/shard_map/while/body/eval_jaxpr/all_gather | solution.py:95
  657.1 95.3 %reduce-scatter.22.cloned.1.call-start = ((), (), s32[]{:S(2)}) async-start(), calls=%async_computation.25 | async-start | bytes 2621440 | tf_op jit(solution)/shard_map/while/body/eval_jaxpr/reduce_scatter | solution.py:115
  803.0 95.1 %reduce-scatter.22.cloned.1.call-start = ((), (), s32[]{:S(2)}) async-start(), calls=%async_computation.25 | async-start | bytes 2621440 | tf_op jit(solution)/shard_map/while/body/eval_jaxpr/reduce_scatter | solution.py:115
  909.2 163.8 %all-gather.36.cloned.1.call-start = ((), (), s32[]{:S(2)}) async-start(), calls=%async_computation.10 | async-start | bytes 7864320 | tf_op jit(solution)/shard_map/all_gather | solution.py:269
  909.8 312.6 %all-gather.38.cloned.1.call-start = ((), (), s32[]{:S(2)}) async-start(), calls=%async_computation.11 | async-start | bytes 10485760 | tf_op jit(solution)/shard_map/all_gather | solution.py:275
  910.6 461.1 %all-gather.40.cloned.1.call-start = ((), (), s32[]{:S(2)}) async-start(), calls=%async_computation.12 | async-start | bytes 10485760 | tf_op jit(solution)/shard_map/all_gather | solution.py:273
  1393.8 75.8 %all-gather.60.cloned.1.call-start = ((), (), s32[]{:S(2)}) async-start(), calls=%async_computation.29 | async-start | bytes 1310720 | tf_op jit(solution)/shard_map/while/body/eval_jaxpr/all_gather | solution.py:147
  1395.5 113.9 %reduce-scatter.26.cloned.1.call-start = ((), (), s32[]{:S(2)}) async-start(), calls=%async_computation.30 | async-start | bytes 1310720 | tf_op jit(solution)/shard_map/while/body/eval_jaxpr/reduce_scatter | solution.py:164
  1488.2 82.9 %reduce-scatter.28.cloned.1.call-start = ((), (), s32[]{:S(2)}) async-start(), calls=%async_computation.31 | async-start | bytes 1310720 | tf_op jit(solution)/shard_map/while/body/eval_jaxpr/reduce_scatter | solution.py:181
  1594.8 76.7 %all-gather.60.cloned.1.call-start = ((), (), s32[]{:S(2)}) async-start(), calls=%async_computation.29 | async-start | bytes 1310720 | tf_op jit(solution)/shard_map/while/body/eval_jaxpr/all_gather | solution.py:147
  1596.6 122.0 %reduce-scatter.26.cloned.1.call-start = ((), (), s32[]{:S(2)}) async-start(), calls=%async_computation.30 | async-start | bytes 1310720 | tf_op jit(solution)/shard_map/while/body/eval_jaxpr/reduce_scatter | solution.py:164
  1690.2 85.6 %reduce-scatter.28.cloned.1.call-start = ((), (), s32[]{:S(2)}) async-start(), calls=%async_computation.31 | async-start | bytes 1310720 | tf_op jit(solution)/shard_map/while/body/eval_jaxpr/reduce_scatter | solution.py:181
  1799.6 75.1 %all-gather.60.cloned.1.call-start = ((), (), s32[]{:S(2)}) async-start(), calls=%async_computation.29 | async-start | bytes 1310720 | tf_op jit(solution)/shard_map/while/body/eval_jaxpr/all_gather | solution.py:147
  1801.3 120.4 %reduce-scatter.26.cloned.1.call-start = ((), (), s32[]{:S(2)}) async-start(), calls=%async_computation.30 | async-start | bytes 1310720 | tf_op jit(solution)/shard_map/while/body/eval_jaxpr/reduce_scatter | solution.py:164
  1893.3 85.4 %reduce-scatter.28.cloned.1.call-start = ((), (), s32[]{:S(2)}) async-start(), calls=%async_computation.31 | async-start | bytes 1310720 | tf_op jit(solution)/shard_map/while/body/eval_jaxpr/reduce_scatter | solution.py:181
  1998.8 64.7 %reduce-scatter.14.cloned.1.call-start = ((), (), s32[]{:S(2)}) async-start(), calls=%async_computation.14 | async-start | bytes 2621440 | tf_op jit(solution)/shard_map/reduce_scatter | solution.py:311
  2002.7 173.1 %reduce-scatter.12.cloned.1.call-start = ((), (), s32[]{:S(2)}) async-start(), calls=%async_computation.13 | async-start | bytes 7864320 | tf_op jit(solution)/shard_map/reduce_scatter | solution.py:305
  2012.8 310.5 %reduce-scatter.18.cloned.1.call-start = ((), (), s32[]{:S(2)}) async-start(), calls=%async_computation.16 | async-start | bytes 10485760 | tf_op jit(solution)/shard_map/reduce_scatter | solution.py:323
  2022.0 448.8 %reduce-scatter.16.cloned.1.call-start = ((), (), s32[]{:S(2)}) async-start(), calls=%async_computation.15 | async-start | bytes 10485760 | tf_op jit(solution)/shard_map/reduce_scatter | solution.py:317
  (110 other events, 1693.8 us)
Sparse Core Ops, SparseCore 0:
  9.6 48.4 all-gather.43
  59.7 114.1 all-gather.41
  175.5 147.7 all-gather.45
  324.7 147.7 all-gather.47
  508.8 29.8 all-gather.53
  540.8 28.2 all-gather.51
  577.0 29.4 reduce-scatter.21
  654.6 29.9 all-gather.53
  686.7 28.2 all-gather.51
  722.9 29.4 reduce-scatter.21
  800.5 29.9 all-gather.53
  832.4 28.2 all-gather.51
  868.6 29.4 reduce-scatter.21
  910.7 46.6 all-gather.33
  958.9 114.1 all-gather.35
  1074.6 147.7 all-gather.37
  1223.8 147.7 all-gather.39
  1409.2 29.9 all-gather.57
  1611.2 29.9 all-gather.57
  1814.3 29.9 all-gather.57
  2021.1 42.3 reduce-scatter.13
  2065.8 109.9 reduce-scatter.11
  2178.2 145.1 reduce-scatter.17
  2325.5 145.2 reduce-scatter.15
  (19 shorter events, 418.8 us)
where the time goes:
time: 2500 us; the launch traced here: 2480 us
  waiting for transfers between devices  1760 us (70%)
  matrix products  354 us (14%)
  other arithmetic  120 us (5%)
  blocking collectives  117 us (5%)
  local copies, waits for them, and re-layouts  80.9 us (3%)
    all_gather x1, waiting for transfers between devices, shards(): lax.all_gather(fc1_weight[0], 'ctx', axis=0, tiled=True)  149 us
    all_gather x1, waiting for transfers between devices, shards(): lax.all_gather(held[6], 'ctx', axis=1, tiled=True)  149 us
    all_gather x1, waiting for transfers between devices, shards(): lax.all_gather(fc2_weight[0], 'ctx', axis=1, tiled=True)  149 us
    all_gather x1, waiting for transfers between devices, shards(): lax.all_gather(held[4], 'ctx', axis=0, tiled=True)  149 us
    reduce_scatter x1, waiting for transfers between devices, shards(): lax.psum_scatter(totals[6].astype(jnp.bfloat16), 'ctx', scatter_dimension...  144 us
    reduce_scatter x1, waiting for transfers between devices, shards(): lax.psum_scatter(totals[4].astype(jnp.bfloat16), 'ctx', scatter_dimension...  143 us
    all_gather x1, waiting for transfers between devices, shards(): lax.all_gather(held[0], 'ctx', axis=1, tiled=True)  116 us
    reduce_scatter x1, waiting for transfers between devices, shards(): lax.psum_scatter(totals[0].astype(jnp.bfloat16), 'ctx', scatter_dimension...  110 us
  transfers between devices with their start and end apart: 49, of which 42 were waited for; matrix products, arithmetic and copies ran while one was open for 16% of the time, Pallas kernels for 0%

commit v1 on v0

--- a/solution.py
+++ b/solution.py
@@ -6,35 +6,17 @@
 D = 2048
 HD = 64
 ROT = 32
-
-
 EPS = 1e-05
 GELU_C = 0.7978845608028654
 GELU_K = 0.044715
-
-
-def from_behind(value, axis, steps):
-    count = lax.axis_size(axis)
-    leading, last = (max(0, -steps), min(count, count - steps))
-    return lax.ppermute(value, axis, [(source, source + steps) for source in range(leading, last)])
-
-
-def gelu(value):
-    inner = jnp.tanh(GELU_C * (value + GELU_K * value * value * value))
-    return 0.5 * value * (1.0 + inner)
-
-
-def gelu_slope(value):
-    inner = jnp.tanh(GELU_C * (value + GELU_K * value * value * value))
-    return 0.5 * (1.0 + inner) + 0.5 * value * (1.0 - inner * inner) * GELU_C * (
-        1.0 + 3.0 * GELU_K * value * value
-    )
+BF16 = jnp.bfloat16
+F32 = jnp.float32
 
 
 def rope_tables(positions):
     half = ROT // 2
-    freq = 10000.0 ** (-(jnp.arange(half).astype(jnp.float32) * 2.0 / ROT))
-    angle = positions.astype(jnp.float32)[:, None] * freq[None, :]
+    freq = 10000.0 ** (-(jnp.arange(half).astype(F32) * 2.0 / ROT))
+    angle = positions.astype(F32)[:, None] * freq[None, :]
     return (jnp.cos(angle), jnp.sin(angle))
 
 
@@ -46,6 +28,260 @@
     sine = sine[:, None, :] * sign
     return jnp.concatenate(
         [first * cosine - second * sine, second * cosine + first * sine, field[..., ROT:]], axis=-1
+    )
+
+
+def doc_layout(ids):
+    length = ids.shape[0]
+    start = jnp.sum((ids[None, :] < ids[:, None]).astype(jnp.int32), axis=1)
+    at = jnp.arange(length, dtype=jnp.int32)
+    allowed = (at[None, :] <= at[:, None]) & (ids[None, :] == ids[:, None])
+    cosine, sine = rope_tables(at - start)
+    return (allowed, cosine, sine)
+
+
+def gather_rows(block):
+    return lax.all_gather(
+        lax.all_gather(block, "ctx", axis=0, tiled=True), "tp", axis=1, tiled=True
+    )
+
+
+def scatter_rows(partial):
+    return lax.psum_scatter(
+        lax.psum_scatter(partial, "tp", scatter_dimension=1, tiled=True),
+        "ctx",
+        scatter_dimension=0,
+        tiled=True,
+    )
+
+
+def swap_section(value):
+    return lax.ppermute(value, "section", [(0, 1), (1, 0)])
+
+
+def both_layers(own):
+    first = lax.axis_index("section") == 0
+    other = swap_section(own)
+    return (jnp.where(first, own, other), jnp.where(first, other, own))
+
+
+def forward(x_full, layout, params):
+    w_qkv, b_qkv, w_out, w_up, b_up, w_down, gain, shift = params
+    allowed, cosine, sine = layout
+    tokens = x_full.shape[0]
+    heads = w_qkv.shape[2] // HD
+    wide = x_full.astype(F32)
+    mean = jnp.mean(wide, axis=1, keepdims=True)
+    variance = jnp.mean(wide * wide, axis=1, keepdims=True) - mean * mean
+    inverse_std = lax.rsqrt(variance + EPS)
+    normed = (
+        (wide - mean) * inverse_std * gain.astype(F32)[None] + shift.astype(F32)[None]
+    ).astype(BF16)
+    projected = (
+        jnp.einsum("td,cde->cte", normed, w_qkv, preferred_element_type=F32)
+        + b_qkv.astype(F32)[:, None, :]
+    )
+    query = rotate(projected[0].reshape(tokens, heads, HD), cosine, sine, 1.0).astype(BF16)
+    key = rotate(projected[1].reshape(tokens, heads, HD), cosine, sine, 1.0).astype(BF16)
+    value = projected[2].reshape(tokens, heads, HD).astype(BF16)
+    scores = jnp.einsum("thd,shd->hts", query, key, preferred_element_type=F32) * HD ** (-0.5)
+    totals = jnp.sum(jnp.where(allowed[None], jnp.exp(scores), 0.0), axis=2)
+    log_total = jnp.log(totals)
+    probs = jnp.where(allowed[None], jnp.exp(scores - log_total[:, :, None]), 0.0).astype(BF16)
+    attended = (
+        jnp.einsum("hts,shd->thd", probs, value, preferred_element_type=F32)
+        .astype(BF16)
+        .reshape(tokens, heads * HD)
+    )
+    hidden_pre = jnp.dot(normed, w_up, preferred_element_type=F32) + b_up.astype(F32)
+    inner = jnp.tanh(GELU_C * (hidden_pre + GELU_K * hidden_pre * hidden_pre * hidden_pre))
+    hidden = (0.5 * hidden_pre * (1.0 + inner)).astype(BF16)
+    partial = jnp.dot(attended, w_out, preferred_element_type=F32) + jnp.dot(
+        hidden, w_down, preferred_element_type=F32
+    )
+    saved = (mean, inverse_std, normed, query, key, value, attended, log_total, hidden_pre, hidden)
+    return (partial.astype(BF16), saved)
+
+
+def backward(g_full, saved, layout, params):
+    w_qkv, b_qkv, w_out, w_up, b_up, w_down, gain, shift = params
+    mean, inverse_std, normed, query, key, value, attended, log_total, hidden_pre, hidden = saved
+    allowed, cosine, sine = layout
+    tokens, heads = query.shape[:2]
+    grad_out = jnp.einsum("tk,te->ke", attended, g_full, preferred_element_type=F32)
+    d_attended = jnp.einsum("te,ke->tk", g_full, w_out, preferred_element_type=F32).astype(BF16)
+    grad_down = jnp.einsum("tf,te->fe", hidden, g_full, preferred_element_type=F32)
+    inner = jnp.tanh(GELU_C * (hidden_pre + GELU_K * hidden_pre * hidden_pre * hidden_pre))
+    slope = 0.5 * (1.0 + inner) + 0.5 * hidden_pre * (1.0 - inner * inner) * GELU_C * (
+        1.0 + 3.0 * GELU_K * hidden_pre * hidden_pre
+    )
+    d_pre = jnp.einsum("te,fe->tf", g_full, w_down, preferred_element_type=F32) * slope
+    grad_up_bias = jnp.sum(d_pre, axis=0)
+    d_hidden = d_pre.astype(BF16)
+    grad_up = jnp.einsum("td,tf->df", normed, d_hidden, preferred_element_type=F32)
+    d_heads = d_attended.reshape(tokens, heads, HD)
+    out_heads = attended.reshape(tokens, heads, HD)
+    delta = jnp.sum(d_heads.astype(F32) * out_heads.astype(F32), axis=2)
+    scores = jnp.einsum("thd,shd->hts", query, key, preferred_element_type=F32) * HD ** (-0.5)
+    probs = jnp.where(allowed[None], jnp.exp(scores - log_total[:, :, None]), 0.0)
+    d_probs = jnp.einsum("thd,shd->hts", d_heads, value, preferred_element_type=F32)
+    d_scores = (probs * (d_probs - delta.T[:, :, None]) * HD ** (-0.5)).astype(BF16)
+    d_query = jnp.einsum("hts,shd->thd", d_scores, key, preferred_element_type=F32)
+    d_key = jnp.einsum("hts,thd->shd", d_scores, query, preferred_element_type=F32)
+    d_value = jnp.einsum("hts,thd->shd", probs.astype(BF16), d_heads, preferred_element_type=F32)
+    d_projected = jnp.stack(
+        [rotate(d_query, cosine, sine, -1.0), rotate(d_key, cosine, sine, -1.0), d_value]
+    ).reshape(3, tokens, heads * HD)
+    grad_qkv_bias = jnp.sum(d_projected, axis=1)
+    d_qkv = d_projected.astype(BF16)
+    grad_qkv = jnp.einsum("td,cte->cde", normed, d_qkv, preferred_element_type=F32)
+    partial = jnp.einsum("cte,cde->td", d_qkv, w_qkv, preferred_element_type=F32) + jnp.einsum(
+        "tf,df->td", d_hidden, w_up, preferred_element_type=F32
+    )
+    return (partial.astype(BF16), (grad_qkv, grad_qkv_bias, grad_out, grad_up, grad_up_bias, grad_down))
+
+
+def shards(
+    boundary,
+    doc_ids,
+    qkv_weight,
+    qkv_bias,
+    out_weight,
+    out_bias,
+    fc1_weight,
+    fc1_bias,
+    fc2_weight,
+    fc2_bias,
+    norm_gain,
+    norm_shift,
+):
+    section = lax.axis_index("section")
+    ctx = lax.axis_index("ctx")
+    tp = lax.axis_index("tp")
+    first = section == 0
+    tokens, part = boundary.shape[2], boundary.shape[3]
+    n_ctx = lax.axis_size("ctx")
+    own = boundary[0]
+    mine = lax.dynamic_index_in_dim(own, section, 0, keepdims=False)
+    theirs = swap_section(lax.dynamic_index_in_dim(own, 1 - section, 0, keepdims=False))
+    x_block = jnp.where(first, mine, theirs)
+    cotangent = jnp.where(first, theirs, mine)
+    ids = lax.dynamic_index_in_dim(doc_ids, section, 0, keepdims=False)
+    layout = doc_layout(ids)
+
+    def turn(weight, split, join):
+        return both_layers(
+            lax.all_to_all(weight, "ctx", split_axis=split, concat_axis=join, tiled=True)
+        )
+
+    w_qkv = turn(qkv_weight[0], 2, 1)
+    w_out = turn(out_weight[0], 0, 1)
+    w_up = turn(fc1_weight[0], 1, 0)
+    w_down = turn(fc2_weight[0], 0, 1)
+    b_qkv = both_layers(qkv_bias[0])
+    b_up = both_layers(fc1_bias[0])
+    vectors = jnp.concatenate([out_bias, fc2_bias, norm_gain, norm_shift], axis=0)
+    vectors = both_layers(
+        lax.all_gather(
+            lax.all_gather(vectors, "ctx", axis=1, tiled=True), "tp", axis=1, tiled=True
+        )
+    )
+    params = [
+        (w_qkv[l], b_qkv[l], w_out[l], w_up[l], b_up[l], w_down[l], vectors[l][2], vectors[l][3])
+        for l in (0, 1)
+    ]
+
+    def own_part(vector):
+        return lax.dynamic_slice_in_dim(vector, tp * part, part)
+
+    def add_up(block, partial, layer):
+        bias = own_part(vectors[layer][0]).astype(F32) + own_part(vectors[layer][1]).astype(F32)
+        return (block.astype(F32) + scatter_rows(partial).astype(F32) + bias).astype(BF16)
+
+    def rows_of(array):
+        return lax.dynamic_slice_in_dim(array, ctx * tokens, tokens)
+
+    def step_back(g_block, x_block, partial, saved, layer):
+        d_normed = scatter_rows(partial).astype(F32)
+        mean, inverse_std = (rows_of(saved[0]), rows_of(saved[1]))
+        centered = (x_block.astype(F32) - mean) * inverse_std
+        scaled = d_normed * own_part(vectors[layer][2]).astype(F32)
+        terms = lax.psum((jnp.sum(scaled, axis=1), jnp.sum(scaled * centered, axis=1)), "tp")
+        width = part * lax.axis_size("tp")
+        grad = g_block.astype(F32) + inverse_std * (
+            scaled - terms[0][:, None] / width - centered * (terms[1][:, None] / width)
+        )
+        return (grad.astype(BF16), jnp.sum(d_normed * centered, axis=0), jnp.sum(d_normed, axis=0))
+
+    x_full = gather_rows(x_block)
+    g_full = gather_rows(cotangent)
+    partial, saved0 = forward(x_full, layout, params[0])
+    act0 = add_up(x_block, partial, 0)
+    x1_full = gather_rows(act0)
+    partial, saved1 = forward(x1_full, layout, params[1])
+    act1 = add_up(act0, partial, 1)
+    partial, grads1 = backward(g_full, saved1, layout, params[1])
+    grad1, gain1, shift1 = step_back(cotangent, act0, partial, saved1, 1)
+    g1_full = gather_rows(grad1)
+    partial, grads0 = backward(g1_full, saved0, layout, params[0])
+    grad0, gain0, shift0 = step_back(grad1, x_block, partial, saved0, 0)
+
+    def home(zero, one):
+        sent = swap_section(jnp.where(first, one, zero).astype(BF16))
+        return jnp.where(first, zero, one) + sent.astype(F32)
+
+    def back(zero, one, split, join):
+        total = home(zero, one)
+        return lax.all_to_all(
+            total.astype(BF16), "ctx", split_axis=split, concat_axis=join, tiled=True
+        ).astype(F32)
+
+    def pair(zero, one):
+        sent = swap_section(jnp.where(first, one, zero))
+        kept = jnp.where(first, zero, one)
+        return jnp.where(first, jnp.stack([kept, sent]), jnp.stack([sent, kept]))[None]
+
+    def column_sum(full):
+        slab = lax.dynamic_slice_in_dim(
+            full, tp * part + ctx * (part // n_ctx), part // n_ctx, axis=1
+        )
+        return jnp.sum(slab.astype(F32), axis=0)
+
+    def over_ctx(zero, one):
+        return lax.psum_scatter(home(zero, one), "ctx", scatter_dimension=0, tiled=True)
+
+    bias_out = home(column_sum(g1_full), column_sum(g_full))[None]
+    return (
+        pair(act0, act1),
+        pair(grad0, grad1),
+        back(grads0[0], grads1[0], 1, 2)[None],
+        home(grads0[1], grads1[1])[None],
+        back(grads0[2], grads1[2], 1, 0)[None],
+        bias_out,
+        back(grads0[3], grads1[3], 0, 1)[None],
+        home(grads0[4], grads1[4])[None],
+        back(grads0[5], grads1[5], 1, 0)[None],
+        bias_out,
+        over_ctx(gain0, gain1)[None],
+        over_ctx(shift0, shift1)[None],
+    )
+
+
+def from_behind(value, axis, steps):
+    count = lax.axis_size(axis)
+    leading, last = (max(0, -steps), min(count, count - steps))
+    return lax.ppermute(value, axis, [(source, source + steps) for source in range(leading, last)])
+
+
+def gelu(value):
+    inner = jnp.tanh(GELU_C * (value + GELU_K * value * value * value))
+    return 0.5 * value * (1.0 + inner)
+
+
+def gelu_slope(value):
+    inner = jnp.tanh(GELU_C * (value + GELU_K * value * value * value))
+    return 0.5 * (1.0 + inner) + 0.5 * value * (1.0 - inner * inner) * GELU_C * (
+        1.0 + 3.0 * GELU_K * value * value
     )
 
 
@@ -203,7 +439,7 @@
     return (grad_in.astype(jnp.bfloat16), grads)
 
 
-def shards(
+def base_shards(
     boundary,
     doc_ids,
     qkv_weight,
@@ -350,32 +586,21 @@
 
 
 def solution(mesh):
-    in_specs = (
-        P("section", None, "ctx", "tp"),
-        P(),
-        P("section", None, "ctx", "tp"),
-        P("section", None, ("tp", "ctx")),
-        P("section", "tp", "ctx"),
-        P("section", ("tp", "ctx")),
-        P("section", "ctx", "tp"),
-        P("section", ("tp", "ctx")),
-        P("section", "tp", "ctx"),
-        P("section", ("tp", "ctx")),
-        P("section", ("tp", "ctx")),
-        P("section", ("tp", "ctx")),
-    )
-    out_specs = (
-        P("section", None, "ctx", "tp"),
-        P("section", None, "ctx", "tp"),
-        P("section", None, "ctx", "tp"),
-        P("section", None, ("tp", "ctx")),
-        P("section", "tp", "ctx"),
-        P("section", ("tp", "ctx")),
-        P("section", "ctx", "tp"),
-        P("section", ("tp", "ctx")),
-        P("section", "tp", "ctx"),
-        P("section", ("tp", "ctx")),
-        P("section", ("tp", "ctx")),
-        P("section", ("tp", "ctx")),
-    )
-    return jax.shard_map(shards, mesh=mesh, in_specs=in_specs, out_specs=out_specs, check_vma=False)
+    specs = {
+        "token": P("section", None, "ctx", "tp"),
+        "rows": P("section", "tp", "ctx"),
+        "columns": P("section", "ctx", "tp"),
+        "vector": P("section", ("tp", "ctx")),
+        "vectors": P("section", None, ("tp", "ctx")),
+    }
+    weights = ("token", "vectors", "rows", "vector", "columns", "vector", "rows", "vector", "vector", "vector")
+    placed = tuple(specs[name] for name in weights)
+    heads = D // HD
+    whole_heads = heads % (mesh.shape["tp"] * mesh.shape["ctx"]) == 0
+    return jax.shard_map(
+        shards if whole_heads and mesh.shape["section"] == 2 else base_shards,
+        mesh=mesh,
+        in_specs=(specs["token"], P(), *placed),
+        out_specs=(specs["token"], specs["token"], *placed),
+        check_vma=False,
+    )

time: 2500 us -> 1130 us (0.45)
  waiting for transfers between devices: 1760 us -> 698 us
  matrix products: 354 us -> 147 us
  other arithmetic: 120 us -> 65.8 us
  starting transfers between devices: 15.6 us -> 66.5 us
  blocking collectives: 117 us -> 66.8 us
    all_gather x26 -> x8, waiting for transfers between devices: 1180 us -> 177 us  [the longest x4 103 us: gather_rows(): lax.all_gather(lax.all_gather(block, 'ctx', axis=0, tiled=True), 'tp', ax...]
    reduce_scatter x16 -> x8, waiting for transfers between devices: 533 us -> 195 us  [the longest x4 139 us: scatter_rows(): lax.psum_scatter(partial, 'tp', scatter_dimension=1, tiled=True)]
    dot_general x57 -> x34, matrix products: 354 us -> 129 us  [the longest x2 14.8 us: backward(): jnp.einsum('td,tf->df', normed, d_hidden, preferred_element_type=F32)]
    ppermute x6 -> x19, waiting for transfers between devices: 36.8 us -> 187 us  [swap_section(): return lax.ppermute(value, 'section', [(0, 1), (1, 0)])]
    all_to_all x0 -> x8, waiting for transfers between devices: none -> 138 us  [the longest x4 105 us: turn(): lax.all_to_all(weight, 'ctx', split_axis=split, concat_axis=join, tiled=T...]
    all_to_all x0 -> x8, starting transfers between devices: none -> 37.1 us  [the longest x4 18.8 us: back(): lax.all_to_all(total.astype(BF16), 'ctx', split_axis=split, concat_axis=j...]
    dynamic_slice x30 -> x1, local copies, waits for them, and re-layouts: 29.3 us -> 0.01 us  [shards(): ids = lax.dynamic_index_in_dim(doc_ids, section, 0, keepdims=False)]
    dynamic_update_slice x15 -> x0, other arithmetic: 25.4 us -> none  [shards(): leftover, (outs_all, saved_all) = lax.scan(forward_tick, start_zero, ticks)]
  transfers between devices with their start and end apart: 49 -> 43, of which waited for: 42 -> 24; matrix products, arithmetic and copies ran while one was open for 16% -> 18% of each run, Pallas kernels for 0% -> 0%
where the time goes in v1:
time: 1130 us
  waiting for transfers between devices  698 us (62%)
  matrix products  147 us (13%)
  blocking collectives  66.8 us (6%)
  starting transfers between devices  66.5 us (6%)
  local copies, waits for them, and re-layouts  66.2 us (6%)
  other arithmetic  65.8 us (6%)
  between operations  16.2 us (1%)
    ppermute x19, waiting for transfers between devices, swap_section(): return lax.ppermute(value, 'section', [(0, 1), (1, 0)])  187 us
    reduce_scatter x4, waiting for transfers between devices, scatter_rows(): lax.psum_scatter(partial, 'tp', scatter_dimension=1, tiled=True)  139 us
    all_to_all x4, waiting for transfers between devices, turn(): lax.all_to_all(weight, 'ctx', split_axis=split, concat_axis=join, tiled=T...  105 us
    all_gather x4, waiting for transfers between devices, gather_rows(): lax.all_gather(lax.all_gather(block, 'ctx', axis=0, tiled=True), 'tp', ax...  103 us
    all_gather x4, waiting for transfers between devices, gather_rows(): lax.all_gather(block, 'ctx', axis=0, tiled=True)  73.5 us
    reduce_scatter x4, waiting for transfers between devices, scatter_rows(): lax.psum_scatter(lax.psum_scatter(partial, 'tp', scatter_dimension=1, til...  56 us
    all_gather x1, blocking collectives, shards(): lax.all_gather(vectors, 'ctx', axis=1, tiled=True)  39.2 us
    all_to_all x4, waiting for transfers between devices, back(): lax.all_to_all(total.astype(BF16), 'ctx', split_axis=split, concat_axis=j...  33 us
  transfers between devices with their start and end apart: 43, of which 24 were waited for; matrix products, arithmetic and copies ran while one was open for 18% of the time, Pallas kernels for 0%

profile of v1, /device:TPU:0, one launch (start us, length us, event | category | flops | bytes accessed | tf_op | source)
XLA Modules:
  0.0 1126.7 jit_solution(15091445721323376209)
XLA Ops:
  17.9 10.1 all-to-all-done.1
  48.8 47.6 %all-to-all-done = bf16[3,512,512]{1,0,2:T(4,128)(2,1)S(1)} async-done(((bf16[3,512,512]{1,0,2:T(4,128)(2,1)}), bf16[3,512,512]{1,0,2:T(4,128)(2,1)S(1)}, u32[]{:S(2)}, u32[]{:S(2)}) %all-to-all-start) | async-done | bytes 1572896 | tf_op jit(solution)/shard_map/all_to_all | solution.py:174
  102.1 47.0 %all-to-all-done.2 = bf16[512,4,512]{2,0,1:T(8,128)(2,1)S(1)} async-done(((bf16[512,4,512]{2,0,1:T(8,128)(2,1)}), bf16[512,4,512]{2,0,1:T(8,128)(2,1)S(1)}, u32[]{:S(2)}, u32[]{:S(2)}) %all-to-all-start.2) | async-done | bytes 2097184 | tf_op jit(solution)/shard_map/all_to_all | solution.py:174
  153.8 39.2 %all_gather.32 = bf16[4,512]{1,0:T(4,128)(2,1)S(1)} all-gather(bf16[4,128]{1,0:T(4,128)(2,1)S(1)} %pad_maximum_fusion.10), channel_id=1, replica_groups=mesh['section'=2,'ctx'=4,'tp'=4] {'ctx'}, dimensions={1}, use_global_device_ids=true | all-gather | bytes 5120 | tf_op jit(solution)/shard_map/all_gather | solution.py:186
  223.9 23.9 %collective-permute-done.1 = bf16[3,2048,128]{2,1,0:T(8,128)(2,1)} collective-permute-done((bf16[3,2048,128]{2,1,0:T(8,128)(2,1)}, bf16[3,2048,128]{2,1,0:T(8,128)(2,1)}, u32[]{:S(2)}, u32[]{:S(2)}) %collective-permute-start.1) | collective-permute-done | bytes 1572896 | tf_op jit(solution)/shard_map/ppermute | solution.py:59
  250.9 53.1 %collective-permute-done.5 = bf16[2048,512]{1,0:T(8,128)(2,1)} collective-permute-done((bf16[2048,512]{1,0:T(8,128)(2,1)S(1)}, bf16[2048,512]{1,0:T(8,128)(2,1)}, u32[]{:S(2)}, u32[]{:S(2)}) %collective-permute-start.5) | collective-permute-done | bytes 2097184 | tf_op jit(solution)/shard_map/ppermute | solution.py:59
  316.7 30.8 %collective-permute-done.7 = bf16[512,2048]{1,0:T(8,128)(2,1)} collective-permute-done((bf16[512,2048]{1,0:T(8,128)(2,1)}, bf16[512,2048]{1,0:T(8,128)(2,1)}, u32[]{:S(2)}, u32[]{:S(2)}) %collective-permute-start.7) | collective-permute-done | bytes 2097184 | tf_op jit(solution)/shard_map/ppermute | solution.py:59
  358.6 53.2 %reduce-scatter.9.cloned.1.call-done = bf16[1024,512]{1,0:T(8,128)(2,1)} async-done(((bf16[1024,2048]{1,0:T(8,128)(2,1)}), bf16[1024,512]{1,0:T(8,128)(2,1)}) %reduce-scatter.9.cloned.1.call-update) | async-done | bytes 1048592 | tf_op jit(solution)/shard_map/reduce_scatter | solution.py:51
  413.1 28.1 %reduce-scatter.11.cloned.1.call-done = bf16[256,512]{1,0:T(8,128)(2,1)} async-done(((bf16[1024,512]{1,0:T(8,128)(2,1)}), bf16[256,512]{1,0:T(8,128)(2,1)}) %reduce-scatter.11.cloned.1.call-update) | async-done | bytes 262160 | tf_op jit(solution)/shard_map/reduce_scatter | solution.py:50
  443.1 26.1 %all-gather.17.cloned.1.call-done = bf16[1024,512]{1,0:T(8,128)(2,1)} async-done(((bf16[256,512]{1,0:T(8,128)(2,1)}), bf16[1024,512]{1,0:T(8,128)(2,1)}) %all-gather.17.cloned.1.call-update) | async-done | bytes 1048592 | tf_op jit(solution)/shard_map/all_gather | solution.py:45
  469.3 28.7 %all-gather.13.cloned.1.call-done = bf16[1024,512]{1,0:T(8,128)(2,1)} async-done(((bf16[256,512]{1,0:T(8,128)(2,1)}), bf16[1024,512]{1,0:T(8,128)(2,1)}) %all-gather.13.cloned.1.call-update) | async-done | bytes 1048592 | tf_op jit(solution)/shard_map/all_gather | solution.py:45
  498.1 35.4 %all-gather.19.cloned.1.call-done = bf16[1024,2048]{1,0:T(8,128)(2,1)} async-done(((bf16[1024,512]{1,0:T(8,128)(2,1)}), bf16[1024,2048]{1,0:T(8,128)(2,1)}) %all-gather.19.cloned.1.call-update) | async-done | bytes 4194320 | tf_op jit(solution)/shard_map/all_gather | solution.py:44
  537.2 32.3 %all-gather.15.cloned.1.call-done = bf16[1024,2048]{1,0:T(8,128)(2,1)} async-done(((bf16[1024,512]{1,0:T(8,128)(2,1)}), bf16[1024,2048]{1,0:T(8,128)(2,1)}) %all-gather.15.cloned.1.call-update) | async-done | bytes 4194320 | tf_op jit(solution)/shard_map/all_gather | solution.py:44
  581.2 9.1 fusion.13
  631.7 43.6 %reduce-scatter.17.cloned.1.call-done = bf16[1024,512]{1,0:T(8,128)(2,1)} async-done(((bf16[1024,2048]{1,0:T(8,128)(2,1)}), bf16[1024,512]{1,0:T(8,128)(2,1)}) %reduce-scatter.17.cloned.1.call-update) | async-done | bytes 1048592 | tf_op jit(solution)/shard_map/reduce_scatter | solution.py:51
  676.9 27.9 %reduce-scatter.19.cloned.1.call-done = bf16[256,512]{1,0:T(8,128)(2,1)} async-done(((bf16[1024,512]{1,0:T(8,128)(2,1)}), bf16[256,512]{1,0:T(8,128)(2,1)}) %reduce-scatter.19.cloned.1.call-update) | async-done | bytes 262160 | tf_op jit(solution)/shard_map/reduce_scatter | solution.py:50
  722.5 18.6 %all-gather.21.cloned.1.call-done = bf16[1024,512]{1,0:T(8,128)(2,1)} async-done(((bf16[256,512]{1,0:T(8,128)(2,1)}), bf16[1024,512]{1,0:T(8,128)(2,1)}) %all-gather.21.cloned.1.call-update) | async-done | bytes 1048592 | tf_op jit(solution)/shard_map/all_gather | solution.py:45
  745.8 42.2 %reduce-scatter.13.cloned.1.call-done = bf16[1024,512]{1,0:T(8,128)(2,1)} async-done(((bf16[1024,2048]{1,0:T(8,128)(2,1)}), bf16[1024,512]{1,0:T(8,128)(2,1)}) %reduce-scatter.13.cloned.1.call-update) | async-done | bytes 1048592 | tf_op jit(solution)/shard_map/reduce_scatter | solution.py:51
  788.2 35.8 %all-gather.23.cloned.1.call-done = bf16[1024,2048]{1,0:T(8,128)(2,1)} async-done(((bf16[1024,512]{1,0:T(8,128)(2,1)}), bf16[1024,2048]{1,0:T(8,128)(2,1)}) %all-gather.23.cloned.1.call-update) | async-done | bytes 4194320 | tf_op jit(solution)/shard_map/all_gather | solution.py:44
  921.8 24.6 %collective-permute-done.14 = bf16[2048,512]{1,0:T(8,128)(2,1)} collective-permute-done((bf16[2048,512]{1,0:T(8,128)(2,1)}, bf16[2048,512]{1,0:T(8,128)(2,1)}, u32[]{:S(2)}, u32[]{:S(2)}) %collective-permute-start.14) | collective-permute-done | bytes 2097184 | tf_op jit(solution)/shard_map/ppermute | solution.py:59
  950.7 11.1 all-to-all-done.4
  974.7 44.9 %collective-permute-done.16 = bf16[512,2048]{1,0:T(8,128)(2,1)S(1)} collective-permute-done((bf16[512,2048]{1,0:T(8,128)(2,1)S(1)}, bf16[512,2048]{1,0:T(8,128)(2,1)S(1)}, u32[]{:S(2)}, u32[]{:S(2)}) %collective-permute-start.16) | collective-permute-done | bytes 2097184 | tf_op jit(solution)/shard_map/ppermute | solution.py:59
  1069.3 21.9 %all-to-all-done.7 = bf16[512,4,512]{2,0,1:T(8,128)(2,1)} async-done(((bf16[512,4,512]{2,0,1:T(8,128)(2,1)}), bf16[512,4,512]{2,0,1:T(8,128)(2,1)}, u32[]{:S(2)}, u32[]{:S(2)}) %all-to-all-start.7) | async-done | bytes 2097184 | tf_op jit(solution)/shard_map/all_to_all | solution.py:235
  1107.6 9.8 all-reduce.4
  (417 shorter events, 365.4 us)
Async XLA Ops:
  28.0 68.3 %all-to-all-start = ((bf16[3,512,512]{1,0,2:T(4,128)(2,1)}), bf16[3,512,512]{1,0,2:T(4,128)(2,1)S(1)}, u32[]{:S(2)}, u32[]{:S(2)}) async-start(bf16[3,512,512]{1,0,2:T(4,128)(2,1)} %bitcast.188), calls=%async_computation | async-start | bytes 4194304 | tf_op jit(solution)/shard_map/all_to_all | solution.py:174
  31.8 69.6 %all-gather.9.cloned.1.call-start = ((), (), s32[]{:S(2)}) async-start(), calls=%async_computation.16 | async-start | bytes 1310720 | tf_op jit(solution)/shard_map/all_gather | solution.py:45
  101.3 117.0 %all-gather.11.cloned.1.call-start = ((), (), s32[]{:S(2)}) async-start(), calls=%async_computation.17 | async-start | bytes 5242880 | tf_op jit(solution)/shard_map/all_gather | solution.py:44
  149.1 64.6 %all-to-all-start.3 = ((bf16[4,512,512]{2,1,0:T(8,128)(2,1)}), bf16[4,512,512]{2,1,0:T(8,128)(2,1)}, u32[]{:S(2)}, u32[]{:S(2)}) async-start(bf16[4,512,512]{2,1,0:T(8,128)(2,1)} %bitcast.208), calls=%async_computation.3 | async-start | bytes 4194304 | tf_op jit(solution)/shard_map/all_to_all | solution.py:174
  153.7 258.1 %reduce-scatter.9.cloned.1.call-start = ((), (), s32[]{:S(2)}) async-start(), calls=%async_computation.18 | async-start | bytes 5242880 | tf_op jit(solution)/shard_map/reduce_scatter | solution.py:51
  211.6 142.9 %collective-permute-start.4 = (bf16[128,2048]{1,0:T(8,128)(2,1)S(1)}, bf16[128,2048]{1,0:T(8,128)(2,1)S(1)}, u32[]{:S(2)}, u32[]{:S(2)}) collective-permute-start(bf16[128,2048]{1,0:T(8,128)(2,1)S(1)} %bitcast.190), channel_id=1, source_target_pairs={{0,16},{16,0},{1,17},{17,1},{2,18},{18,2},{3,19},{19,3},{4,20},{20... | collective-permute-start | bytes 1572872 | tf_op jit(solution)/shard_map/ppermute | solution.py:59
  213.1 90.9 %collective-permute-start.5 = (bf16[2048,512]{1,0:T(8,128)(2,1)S(1)}, bf16[2048,512]{1,0:T(8,128)(2,1)}, u32[]{:S(2)}, u32[]{:S(2)}) collective-permute-start(bf16[2048,512]{1,0:T(8,128)(2,1)S(1)} %bitcast.174), channel_id=1, source_target_pairs={{0,16},{16,0},{1,17},{17,1},{2,18},{18,2},{3,19},{19,3},{4,20},{20... | collective-permute-start | bytes 6291464 | tf_op jit(solution)/shard_map/ppermute | solution.py:59
  216.8 130.7 %collective-permute-start.7 = (bf16[512,2048]{1,0:T(8,128)(2,1)}, bf16[512,2048]{1,0:T(8,128)(2,1)}, u32[]{:S(2)}, u32[]{:S(2)}) collective-permute-start(bf16[512,2048]{1,0:T(8,128)(2,1)} %bitcast.89), channel_id=1, source_target_pairs={{0,16},{16,0},{1,17},{17,1},{2,18},{18,2},{3,19},{19,3},{4,20},{20... | collective-permute-start | bytes 6291464 | tf_op jit(solution)/shard_map/ppermute | solution.py:59
  358.5 82.8 %reduce-scatter.11.cloned.1.call-start = ((), (), s32[]{:S(2)}) async-start(), calls=%async_computation.19 | async-start | bytes 1310720 | tf_op jit(solution)/shard_map/reduce_scatter | solution.py:50
  411.8 57.4 %all-gather.17.cloned.1.call-start = ((), (), s32[]{:S(2)}) async-start(), calls=%async_computation.24 | async-start | bytes 1310720 | tf_op jit(solution)/shard_map/all_gather | solution.py:45
  412.4 85.6 %all-gather.13.cloned.1.call-start = ((), (), s32[]{:S(2)}) async-start(), calls=%async_computation.20 | async-start | bytes 1310720 | tf_op jit(solution)/shard_map/all_gather | solution.py:45
  443.0 90.4 %all-gather.19.cloned.1.call-start = ((), (), s32[]{:S(2)}) async-start(), calls=%async_computation.25 | async-start | bytes 5242880 | tf_op jit(solution)/shard_map/all_gather | solution.py:44
  469.2 100.3 %all-gather.15.cloned.1.call-start = ((), (), s32[]{:S(2)}) async-start(), calls=%async_computation.21 | async-start | bytes 5242880 | tf_op jit(solution)/shard_map/all_gather | solution.py:44
  498.0 177.3 %reduce-scatter.17.cloned.1.call-start = ((), (), s32[]{:S(2)}) async-start(), calls=%async_computation.26 | async-start | bytes 5242880 | tf_op jit(solution)/shard_map/reduce_scatter | solution.py:51
  631.7 73.1 %reduce-scatter.19.cloned.1.call-start = ((), (), s32[]{:S(2)}) async-start(), calls=%async_computation.27 | async-start | bytes 1310720 | tf_op jit(solution)/shard_map/reduce_scatter | solution.py:50
  675.4 65.8 %all-gather.21.cloned.1.call-start = ((), (), s32[]{:S(2)}) async-start(), calls=%async_computation.28 | async-start | bytes 1310720 | tf_op jit(solution)/shard_map/all_gather | solution.py:45
  714.8 73.2 %reduce-scatter.13.cloned.1.call-start = ((), (), s32[]{:S(2)}) async-start(), calls=%async_computation.22 | async-start | bytes 5242880 | tf_op jit(solution)/shard_map/reduce_scatter | solution.py:51
  722.5 101.5 %all-gather.23.cloned.1.call-start = ((), (), s32[]{:S(2)}) async-start(), calls=%async_computation.29 | async-start | bytes 5242880 | tf_op jit(solution)/shard_map/all_gather | solution.py:44
  741.2 287.1 %reduce-scatter.15.cloned.1.call-start = ((), (), s32[]{:S(2)}) async-start(), calls=%async_computation.23 | async-start | bytes 1310720 | tf_op jit(solution)/shard_map/reduce_scatter | solution.py:50
  787.9 251.6 %reduce-scatter.21.cloned.1.call-start = ((), (), s32[]{:S(2)}) async-start(), calls=%async_computation.30 | async-start | bytes 5242880 | tf_op jit(solution)/shard_map/reduce_scatter | solution.py:51
  909.1 52.7 %all-to-all-start.4 = ((bf16[3,2048,128]{2,0,1:T(4,128)(2,1)}), bf16[3,2048,128]{2,0,1:T(4,128)(2,1)S(1)}, u32[]{:S(2)}, u32[]{:S(2)}) async-start(bf16[3,2048,128]{2,0,1:T(4,128)(2,1)} %copy.77), calls=%async_computation.12 | async-start | bytes 4194304 | tf_op jit(solution)/shard_map/all_to_all | solution.py:235
  961.8 60.6 %all-to-all-start.6 = ((bf16[4,512,512]{2,1,0:T(8,128)(2,1)}), bf16[4,512,512]{2,1,0:T(8,128)(2,1)}, u32[]{:S(2)}, u32[]{:S(2)}) async-start(bf16[4,512,512]{2,1,0:T(8,128)(2,1)} %bitcast.185), calls=%async_computation.14 | async-start | bytes 4194304 | tf_op jit(solution)/shard_map/all_to_all | solution.py:235
  1022.5 68.7 %all-to-all-start.7 = ((bf16[512,4,512]{2,0,1:T(8,128)(2,1)}), bf16[512,4,512]{2,0,1:T(8,128)(2,1)}, u32[]{:S(2)}, u32[]{:S(2)}) async-start(bf16[512,4,512]{2,0,1:T(8,128)(2,1)} %bitcast.189), calls=%async_computation.15 | async-start | bytes 4194304 | tf_op jit(solution)/shard_map/all_to_all | solution.py:235
  1027.3 68.1 %reduce-scatter.23.cloned.1.call-start = ((), (), s32[]{:S(2)}) async-start(), calls=%async_computation.31 | async-start | bytes 1310720 | tf_op jit(solution)/shard_map/reduce_scatter | solution.py:50
  (114 other events, 3070.4 us)
Sparse Core Ops, SparseCore 0:
  41.1 48.5 all-gather.8
  103.7 35.8 all-gather.10
  358.6 53.0 reduce-scatter.8
  413.9 27.3 reduce-scatter.10
  442.7 26.4 all-gather.16
  470.6 27.3 all-gather.12
  499.6 33.8 all-gather.18
  535.0 34.4 all-gather.14
  631.8 43.4 reduce-scatter.16
  677.5 27.2 reduce-scatter.18
  714.9 26.2 all-gather.20
  744.1 43.7 reduce-scatter.12
  789.5 34.4 all-gather.22
  826.1 27.2 reduce-scatter.14
  874.0 46.7 reduce-scatter.20
  1039.6 45.6 reduce-scatter.22

commit v2 on v1

--- a/solution.py
+++ b/solution.py
@@ -1,6 +1,11 @@
+import functools
+import itertools
+
 import jax
 import jax.numpy as jnp
 from jax import lax
+from jax.experimental import pallas as pl
+from jax.experimental.pallas import tpu as pltpu
 from jax.sharding import PartitionSpec as P
 
 D = 2048
@@ -40,29 +45,637 @@
     return (allowed, cosine, sine)
 
 
-def gather_rows(block):
-    return lax.all_gather(
-        lax.all_gather(block, "ctx", axis=0, tiled=True), "tp", axis=1, tiled=True
-    )
-
-
-def scatter_rows(partial):
-    return lax.psum_scatter(
-        lax.psum_scatter(partial, "tp", scatter_dimension=1, tiled=True),
-        "ctx",
-        scatter_dimension=0,
-        tiled=True,
-    )
-
-
-def swap_section(value):
-    return lax.ppermute(value, "section", [(0, 1), (1, 0)])
-
-
-def both_layers(own):
-    first = lax.axis_index("section") == 0
-    other = swap_section(own)
-    return (jnp.where(first, own, other), jnp.where(first, other, own))
+MESH = pl.DeviceIdType.MESH
+FWD, BWD, LAST, START = 0, 1, 2, 3
+
+
+class Wire:
+    def __init__(self, send_sems, recv_sems):
+        self.send_sems, self.recv_sems = send_sems, recv_sems
+        self.copies = []
+        self.section = lax.axis_index("section")
+        self.c = lax.axis_index("ctx")
+        self.t = lax.axis_index("tp")
+        self.y = self.t // 2
+        self.k = self.t % 2
+        self.c_up = (self.c + 1) % 4
+        self.c_far = (self.c + 2) % 4
+        self.c_down = (self.c + 3) % 4
+        self.t_y = (self.t + 2) % 4
+        self.t_core = self.t + 1 - 2 * self.k
+        self.up = {"ctx": self.c_up}
+        self.down = {"ctx": self.c_down}
+        self.beside = {"tp": self.t_y}
+        self.core = {"tp": self.t_core}
+        self.across = {"section": 1 - self.section}
+        self.others = [(2, self.c_far), (1, self.c_up), (3, self.c_down)]
+
+    def greet(self, targets):
+        barrier = pltpu.get_barrier_semaphore()
+        for target in targets:
+            pl.semaphore_signal(barrier, inc=1, device_id=target, device_id_type=MESH)
+        pl.semaphore_wait(barrier, len(targets))
+
+    def send(self, source, target, device):
+        index = len(self.copies)
+        copy = pltpu.make_async_remote_copy(
+            src_ref=source,
+            dst_ref=target,
+            send_sem=self.send_sems.at[index],
+            recv_sem=self.recv_sems.at[index],
+            device_id=device,
+            device_id_type=MESH,
+        )
+        copy.start()
+        self.copies.append(copy)
+        return copy
+
+    def send_one_of(self, first, source, other_source, target, device):
+        index = len(self.copies)
+        copies = [
+            pltpu.make_async_remote_copy(
+                src_ref=ref,
+                dst_ref=target,
+                send_sem=self.send_sems.at[index],
+                recv_sem=self.recv_sems.at[index],
+                device_id=device,
+                device_id_type=MESH,
+            )
+            for ref in (source, other_source)
+        ]
+        pl.when(first)(copies[0].start)
+        pl.when(jnp.logical_not(first))(copies[1].start)
+        self.copies.append(copies[0])
+        return copies[0]
+
+    def drain(self):
+        for copy in self.copies:
+            copy.wait_send()
+
+
+class Gather:
+    def __init__(self, wire, full, rows, part):
+        self.w, self.full, self.rows, self.part = wire, full, rows, part
+        self.far, self.beside, self.core = {}, {}, []
+
+    def region(self, c, t, group):
+        size = self.rows // 2
+        return self.full.at[
+            pl.ds(pl.multiple_of(c * self.rows + group * size, 16), size),
+            pl.ds(pl.multiple_of(t * self.part, 128), self.part),
+        ]
+
+    def pass_on(self, device, c, t, group):
+        spot = self.region(c, t, group)
+        return self.w.send(spot, spot, device)
+
+    def begin(self, group):
+        w = self.w
+        for step, place in w.others:
+            self.far[group, step] = self.pass_on({"ctx": place}, w.c, w.t, group)
+        self.beside[group, 0] = self.pass_on(w.beside, w.c, w.t, group)
+        self.core.append(self.pass_on(w.core, w.c, w.t, group))
+
+    def finish(self):
+        w = self.w
+        steps = [(step, group) for group in (0, 1) for step in (1, 3, 2)]
+        for step, group in steps:
+            source = (w.c + 4 - step) % 4
+            self.far[group, step].wait_recv()
+            self.beside[group, step] = self.pass_on(w.beside, source, w.t, group)
+            self.core.append(self.pass_on(w.core, source, w.t, group))
+        for step, group in [(0, 0), (0, 1)] + steps:
+            self.beside[group, step].wait_recv()
+            self.core.append(self.pass_on(w.core, (w.c + 4 - step) % 4, w.t_y, group))
+        for copy in self.core:
+            copy.wait_recv()
+
+
+def scatter_scratch(rows, part):
+    return [
+        pltpu.VMEM((2, 4 * rows, part), BF16),
+        pltpu.VMEM((2, 4 * rows, part), BF16),
+        pltpu.VMEM((4 * rows, part), BF16),
+        pltpu.VMEM((3, rows, part), BF16),
+    ]
+
+
+class Scatter:
+    def __init__(self, wire, partial, scratch, rows, part):
+        self.w, self.partial, self.rows, self.part = wire, partial, rows, part
+        self.theirs, self.chip, self.from_y, self.from_far = scratch
+        w = wire
+        self.places = [(2, w.c_far), (1, w.c_up), (3, w.c_down), (0, w.c)]
+        self.order = [
+            (group, c, y)
+            for group in (0, 1)
+            for y in (1 - w.y, w.y)
+            for _, c in self.places
+        ]
+        self.far = {}
+
+    def span(self, group, c):
+        size = self.rows // 2
+        return pl.ds(pl.multiple_of(c * self.rows + group * size, 16), size)
+
+    def begin(self):
+        w = self.w
+        self.cores = []
+        for group, c, y in self.order:
+            columns = pl.ds(pl.multiple_of((2 * y + 1 - w.k) * self.part, 128), self.part)
+            self.cores.append(
+                w.send(
+                    self.partial.at[self.span(group, c), columns],
+                    self.theirs.at[y, self.span(group, c)],
+                    w.core,
+                )
+            )
+
+    def take(self, index):
+        group, c, y = self.order[index]
+        self.cores[index].wait_recv()
+        rows = self.span(group, c)
+        columns = pl.ds(pl.multiple_of((2 * y + self.w.k) * self.part, 128), self.part)
+        return self.partial[rows, columns].astype(F32) + self.theirs[y, rows].astype(F32)
+
+    def run(self):
+        for _ in self.steps():
+            pass
+
+    def steps(self):
+        w = self.w
+        half = self.rows // 2
+        beside = {}
+        for group in (0, 1):
+            for slot, (_, c) in enumerate(self.places):
+                rows = self.span(group, c)
+                self.chip[1 - w.y, rows] = self.take(8 * group + slot).astype(BF16)
+                beside[group, slot] = w.send(
+                    self.chip.at[1 - w.y, rows], self.from_y.at[rows], w.beside
+                )
+                yield
+        for group in (0, 1):
+            for slot, (step, c) in enumerate(self.places):
+                rows = self.span(group, c)
+                value = self.take(8 * group + 4 + slot)
+                beside[group, slot].wait_recv()
+                self.chip[w.y, rows] = (value + self.from_y[rows].astype(F32)).astype(BF16)
+                if step:
+                    self.far[group, step] = w.send(
+                        self.chip.at[w.y, rows],
+                        self.from_far.at[step - 1, pl.ds(group * half, half)],
+                        {"ctx": c},
+                    )
+                yield
+
+    def total(self, group):
+        half = self.rows // 2
+        value = self.chip[self.w.y, self.span(group, self.w.c)].astype(F32)
+        for step in (1, 3, 2):
+            self.far[group, step].wait_recv()
+            value += self.from_far[step - 1, pl.ds(group * half, half)].astype(F32)
+        return value
+
+
+def neighbours(w):
+    return [{"ctx": place} for _, place in w.others] + [w.beside, w.core]
+
+
+def next_layer_kernel(rows, part, partial, block, bias, act, full, *rest):
+    *scratch, send_sems, recv_sems = rest
+    w = Wire(send_sems, recv_sems)
+    w.greet(neighbours(w))
+    scatter = Scatter(w, partial, scratch, rows, part)
+    scatter.begin()
+    scatter.run()
+    gather = Gather(w, full, rows, part)
+    half = rows // 2
+    for group in (0, 1):
+        own = slice(group * half, (group + 1) * half)
+        value = (block[own].astype(F32) + scatter.total(group) + bias[...]).astype(BF16)
+        act[own] = value
+        gather.region(w.c, w.t, group)[...] = value
+        gather.begin(group)
+    gather.finish()
+    w.drain()
+
+
+def next_layer(partial, block, bias):
+    rows, part = block.shape
+    vmem = pl.BlockSpec(memory_space=pltpu.VMEM)
+    return pl.pallas_call(
+        functools.partial(next_layer_kernel, rows, part),
+        out_shape=(
+            jax.ShapeDtypeStruct((rows, part), BF16),
+            jax.ShapeDtypeStruct((4 * rows, 4 * part), BF16),
+        ),
+        in_specs=[vmem] * 3,
+        out_specs=(vmem, vmem),
+        scratch_shapes=scatter_scratch(rows, part)
+        + [pltpu.SemaphoreType.DMA((80,)), pltpu.SemaphoreType.DMA((80,))],
+        compiler_params=pltpu.CompilerParams(
+            collective_id=FWD, has_side_effects=True, vmem_limit_bytes=40 << 20
+        ),
+        name="next_layer",
+    )(partial, block, bias)
+
+
+def diagonal(w):
+    return {"tp": (w.t_core + 2) % 4}
+
+
+def back_scratch(rows, part):
+    return [
+        pltpu.VMEM((rows, part), F32),
+        pltpu.VMEM((2, 8, 128), F32),
+        pltpu.VMEM((2, 3, 8, 128), F32),
+    ]
+
+
+def norm_back(w, scatter, blocks, scratch, rows, part, grad, sums, done):
+    g_block, x_block, mean, inverse_std, gain = blocks
+    d_normed, row_out, row_in = scratch
+    half = rows // 2
+    width = 4 * part
+    lane = lax.broadcasted_iota(jnp.int32, (half, 128), 1)
+    sent = []
+    gain_sum = jnp.zeros((1, part), F32)
+    shift_sum = jnp.zeros((1, part), F32)
+    for group in (0, 1):
+        own = slice(group * half, (group + 1) * half)
+        value = scatter.total(group)
+        d_normed[own] = value
+        centered = (x_block[own].astype(F32) - mean[own]) * inverse_std[own]
+        weighted = value * centered
+        gain_sum += jnp.sum(weighted, axis=0, keepdims=True)
+        shift_sum += jnp.sum(value, axis=0, keepdims=True)
+        first = jnp.sum(value * gain[...], axis=1, keepdims=True)
+        second = jnp.sum(weighted * gain[...], axis=1, keepdims=True)
+        packed = jnp.where(lane == 0, first, jnp.where(lane == 1, second, 0.0))
+        row_out[group] = packed.T[:8]
+        sent.append(
+            [
+                w.send(row_out.at[group], row_in.at[group, slot], peer)
+                for slot, peer in enumerate((w.beside, w.core, diagonal(w)))
+            ]
+        )
+    sums[...] = jnp.concatenate(
+        [gain_sum, shift_sum, jnp.zeros((6, part), F32)], axis=0
+    )
+    for group in (0, 1):
+        own = slice(group * half, (group + 1) * half)
+        for copy in sent[group]:
+            copy.wait_recv()
+        rows_sum = row_out[group] + row_in[group, 0] + row_in[group, 1] + row_in[group, 2]
+        columns = jnp.concatenate([rows_sum, jnp.zeros((half - 8, 128), F32)], axis=0).T
+        centered = (x_block[own].astype(F32) - mean[own]) * inverse_std[own]
+        scaled = d_normed[own] * gain[...]
+        value = g_block[own].astype(F32) + inverse_std[own] * (
+            scaled - columns[:, 0:1] / width - centered * (columns[:, 1:2] / width)
+        )
+        grad[own] = value.astype(BF16)
+        done(group)
+
+
+def previous_layer_kernel(
+    rows, part, partial, g_block, x_block, mean, inverse_std, gain, grad, full, sums, *rest
+):
+    *scratch, send_sems, recv_sems = rest
+    w = Wire(send_sems, recv_sems)
+    w.greet(neighbours(w) + [diagonal(w)])
+    scatter = Scatter(w, partial, scratch[:4], rows, part)
+    scatter.begin()
+    scatter.run()
+    gather = Gather(w, full, rows, part)
+    half = rows // 2
+
+    def done(group):
+        gather.region(w.c, w.t, group)[...] = grad[group * half : (group + 1) * half]
+        gather.begin(group)
+
+    norm_back(
+        w, scatter, (g_block, x_block, mean, inverse_std, gain), scratch[4:], rows, part, grad, sums, done
+    )
+    gather.finish()
+    w.drain()
+
+
+def previous_layer(partial, g_block, x_block, mean, inverse_std, gain):
+    rows, part = g_block.shape
+    vmem = pl.BlockSpec(memory_space=pltpu.VMEM)
+    return pl.pallas_call(
+        functools.partial(previous_layer_kernel, rows, part),
+        out_shape=(
+            jax.ShapeDtypeStruct((rows, part), BF16),
+            jax.ShapeDtypeStruct((4 * rows, 4 * part), BF16),
+            jax.ShapeDtypeStruct((8, part), F32),
+        ),
+        in_specs=[vmem] * 6,
+        out_specs=(vmem,) * 3,
+        scratch_shapes=scatter_scratch(rows, part)
+        + back_scratch(rows, part)
+        + [pltpu.SemaphoreType.DMA((90,)), pltpu.SemaphoreType.DMA((90,))],
+        compiler_params=pltpu.CompilerParams(
+            collective_id=BWD, has_side_effects=True, vmem_limit_bytes=44 << 20
+        ),
+        name="previous_layer",
+    )(partial, g_block, x_block, mean, inverse_std, gain)
+
+
+def whole(size, start=0):
+    return pl.ds(start, size)
+
+
+class Turn:
+    def __init__(self, d_part, e_part, f_part):
+        self.d, self.e, self.f = d_part, e_part, f_part
+
+    def rows(self, name):
+        return {"qkv": self.d, "out": self.e, "up": self.d, "down": self.f}[name]
+
+    def inner(self, name, half):
+        size = self.rows(name)
+        return (0, size) if half is None else (half * size // 2, size // 2)
+
+    def shard(self, name, ref, c, half=None):
+        start, size = self.inner(name, half)
+        if name == "qkv":
+            return ref.at[:, pl.ds(start, size), pl.ds(pl.multiple_of(c * self.e, 128), self.e)]
+        if name == "up":
+            return ref.at[pl.ds(start, size), pl.ds(pl.multiple_of(c * self.f, 128), self.f)]
+        stride = self.e if name == "out" else self.f
+        return ref.at[pl.ds(pl.multiple_of(c * stride + start, 16), size)]
+
+    def turned(self, name, ref, c, half=None):
+        start, size = self.inner(name, half)
+        if name == "qkv":
+            return ref.at[:, pl.ds(pl.multiple_of(c * self.d + start, 16), size)]
+        if name == "up":
+            return ref.at[pl.ds(pl.multiple_of(c * self.d + start, 16), size)]
+        return ref.at[pl.ds(start, size), pl.ds(pl.multiple_of(c * self.d, 128), self.d)]
+
+    def piece_shape(self, name, halved=False):
+        size = self.rows(name) // (2 if halved else 1)
+        return {
+            "qkv": (3, size, self.e),
+            "out": (size, self.d),
+            "up": (size, self.f),
+            "down": (size, self.d),
+        }[name]
+
+    def turned_shape(self, name):
+        return {
+            "qkv": (3, 4 * self.d, self.e),
+            "out": (self.e, 4 * self.d),
+            "up": (4 * self.d, self.f),
+            "down": (self.f, 4 * self.d),
+        }[name]
+
+
+NAMES = ("qkv", "out", "up", "down")
+
+
+def everyone(w):
+    return [
+        {"section": (w.section + ds) % 2, "ctx": (w.c + dc) % 4, "tp": (w.t + dt) % 4}
+        for ds in range(2)
+        for dc in range(4)
+        for dt in range(4)
+        if (ds, dc, dt) != (0, 0, 0)
+    ]
+
+
+def begin_kernel(turn, rows, part, own, vector, *rest):
+    shards = dict(zip(NAMES, rest[:4]))
+    turned = dict(zip(NAMES, rest[4:8]))
+    x_full, g_full, x_block, g_block, vectors = rest[8:13]
+    bounce = dict(zip(NAMES, rest[13:17]))
+    other, local_sems, send_sems, recv_sems = rest[17:]
+    w = Wire(send_sems, recv_sems)
+    s = w.section
+    peers = everyone(w)
+    w.greet(peers)
+    mine = {name: turned[name].at[s] for name in NAMES}
+    swap = w.send(own.at[1 - s], other, w.across)
+    vectors[s, w.c, w.t] = vector[...]
+    told = [w.send(vector, vectors.at[s, w.c, w.t], peer) for peer in peers]
+    local, far, across = {}, {}, []
+    for i, name in enumerate(NAMES):
+        own_piece = turn.shard(name, shards[name], w.c)
+        across.append(w.send(own_piece, turn.turned(name, mine[name], w.c), w.across))
+        local[name] = pltpu.make_async_copy(own_piece, bounce[name], local_sems.at[i])
+        local[name].start()
+        for step, place in w.others:
+            far[name, step] = w.send(
+                turn.shard(name, shards[name], place),
+                turn.turned(name, mine[name], w.c),
+                {"ctx": place},
+            )
+    swap.wait_recv()
+    mine_block = own[s]
+    x_block[...] = jnp.where(s == 0, mine_block, other[...])
+    g_block[...] = jnp.where(s == 0, other[...], mine_block)
+    half = rows // 2
+    gathers = [Gather(w, x_full, rows, part), Gather(w, g_full, rows, part)]
+    for gather, block in zip(gathers, (x_block, g_block)):
+        for group in (0, 1):
+            gather.region(w.c, w.t, group)[...] = block[group * half : (group + 1) * half]
+            gather.begin(group)
+    puts = []
+    for i, name in enumerate(NAMES):
+        local[name].wait()
+        puts.append(
+            pltpu.make_async_copy(bounce[name], turn.turned(name, mine[name], w.c), local_sems.at[4 + i])
+        )
+        puts[-1].start()
+    for name in NAMES:
+        for step in (1, 3, 2):
+            far[name, step].wait_recv()
+            spot = turn.turned(name, mine[name], (w.c + 4 - step) % 4)
+            across.append(w.send(spot, spot, w.across))
+    for gather in gathers:
+        gather.finish()
+    for copy in told + across:
+        copy.wait_recv()
+    for put in puts:
+        put.wait()
+    w.drain()
+
+
+def begin(own, vector, shards):
+    _, rows, part = own.shape
+    turn = Turn(shards["qkv"].shape[1], shards["qkv"].shape[2] // 4, shards["up"].shape[1] // 4)
+    vmem = pl.BlockSpec(memory_space=pltpu.VMEM)
+    hbm = pl.BlockSpec(memory_space=pl.ANY)
+    shape = jax.ShapeDtypeStruct
+    full = shape((4 * rows, 4 * part), BF16)
+    block = shape((rows, part), BF16)
+    return pl.pallas_call(
+        functools.partial(begin_kernel, turn, rows, part),
+        out_shape=tuple(shape((2,) + turn.turned_shape(name), BF16) for name in NAMES)
+        + (full, full, block, block, shape((2, 4, 4) + vector.shape, F32)),
+        in_specs=[vmem, vmem] + [hbm] * 4,
+        out_specs=(hbm,) * 4 + (vmem,) * 5,
+        scratch_shapes=[pltpu.VMEM(turn.piece_shape(name), BF16) for name in NAMES]
+        + [
+            pltpu.VMEM((rows, part), BF16),
+            pltpu.SemaphoreType.DMA((8,)),
+            pltpu.SemaphoreType.DMA((200,)),
+            pltpu.SemaphoreType.DMA((200,)),
+        ],
+        compiler_params=pltpu.CompilerParams(
+            collective_id=START, has_side_effects=True, vmem_limit_bytes=40 << 20
+        ),
+        name="begin",
+    )(own, vector, *(shards[name] for name in NAMES))
+
+
+SENT = ("down", "out", "up", "qkv")
+
+
+def end_kernel(turn, rows, part, *refs):
+    grads0, grads1 = dict(zip(NAMES, refs[:4])), dict(zip(NAMES, refs[4:8]))
+    partial_x, block, bias = refs[8:11]
+    partial_g, *blocks = refs[11:17]
+    small, sums1 = refs[17:19]
+    outs = dict(zip(NAMES, refs[19:23]))
+    act, grad, small_sum, norm_sum = refs[23:27]
+    rest = refs[27:]
+    kept, arrived = dict(zip(NAMES, rest[:4])), dict(zip(NAMES, rest[4:8]))
+    landed = dict(zip(NAMES, rest[8:12]))
+    scratch_x, scratch_g, scratch_n = rest[12:16], rest[16:20], rest[20:23]
+    small_in, sums0, norm_out, norm_in = rest[23:27]
+    local_sems, send_sems, recv_sems = rest[27:]
+    w = Wire(send_sems, recv_sems)
+    s = w.section
+    half = rows // 2
+    moves = [(ds, dc) for ds in (0, 1) for dc in range(4) if (ds, dc) != (0, 0)]
+
+    def away(ds, dc):
+        return {"section": (s + ds) % 2, "ctx": (w.c + dc) % 4}
+
+    w.greet([away(*move) for move in moves] + [w.beside, w.core, diagonal(w)])
+    places = [(2, w.c_far), (1, w.c_up), (3, w.c_down), (0, w.c)]
+    small_copy = w.send(small.at[1 - s], small_in, w.across)
+    across = {}
+    for i, name in enumerate(SENT):
+        for layer, grads in ((0, grads0), (1, grads1)):
+            keep = pltpu.make_async_copy(grads[name], kept[name], local_sems.at[i])
+            pl.when(s == layer)(keep.start)
+        for step, c in places:
+            target = turn.turned(name, arrived[name], c)
+            across[name, step] = w.send_one_of(
+                s == 0,
+                turn.turned(name, grads1[name], c),
+                turn.turned(name, grads0[name], c),
+                target,
+                w.across,
+            )
+    scatter_x = Scatter(w, partial_x, scratch_x, rows, part)
+    scatter_g = Scatter(w, partial_g, scratch_g, rows, part)
+    scatter_x.begin()
+    scatter_g.begin()
+    work = itertools.chain(scatter_x.steps(), scatter_g.steps())
+    home = {}
+    for i, name in enumerate(SENT):
+        pltpu.make_async_copy(grads0[name], kept[name], local_sems.at[i]).wait()
+        for step, c in places:
+            across[name, step].wait_recv()
+            mine = turn.turned(name, kept[name], c)
+            theirs = turn.turned(name, arrived[name], c)
+            total = mine[...].astype(F32) + theirs[...].astype(F32)
+            if step:
+                theirs[...] = total.astype(BF16)
+                home[name, step] = w.send(theirs, landed[name].at[step - 1], {"ctx": c})
+            else:
+                turn.shard(name, outs[name], w.c)[...] = total
+            for _ in range(5):
+                next(work, None)
+    for _ in work:
+        pass
+    for group in (0, 1):
+        own = slice(group * half, (group + 1) * half)
+        value = block[own].astype(F32) + scatter_x.total(group) + bias[...]
+        act[own] = value.astype(BF16)
+    norm_back(w, scatter_g, blocks, scratch_n, rows, part, grad, sums0, lambda group: None)
+    for layer, sums in ((0, sums0), (1, sums1)):
+        for c in range(4):
+            norm_out[layer, c] = sums[:, c * 128 : (c + 1) * 128]
+    told = []
+    for slot, (ds, dc) in enumerate(moves):
+        told.append(
+            w.send(
+                norm_out.at[(s + ds) % 2, (w.c + dc) % 4], norm_in.at[slot], away(ds, dc)
+            )
+        )
+    small_copy.wait_recv()
+    small_sum[...] = small[s] + small_in[...]
+    for name in SENT:
+        for step in (1, 3, 2):
+            home[name, step].wait_recv()
+            spot = turn.shard(name, outs[name], (w.c + 4 - step) % 4)
+            spot[...] = landed[name][step - 1].astype(F32)
+    total = norm_out[s, w.c]
+    for slot, copy in enumerate(told):
+        copy.wait_recv()
+        total += norm_in[slot]
+    norm_sum[...] = total
+    w.drain()
+
+
+def end(grads0, grads1, partial_x, block, bias, partial_g, blocks, small, sums1):
+    rows, part = block.shape
+    d_part = grads0["qkv"].shape[1] // 4
+    turn = Turn(d_part, grads0["qkv"].shape[2], grads0["up"].shape[1])
+    shape = jax.ShapeDtypeStruct
+    vmem = pl.BlockSpec(memory_space=pltpu.VMEM)
+    hbm = pl.BlockSpec(memory_space=pl.ANY)
+    e, f = 4 * turn.e, 4 * turn.f
+    homes = {
+        "qkv": (3, d_part, e),
+        "out": (e, d_part),
+        "up": (d_part, f),
+        "down": (f, d_part),
+    }
+    return pl.pallas_call(
+        functools.partial(end_kernel, turn, rows, part),
+        out_shape=tuple(shape(homes[name], F32) for name in NAMES)
+        + (
+            shape((rows, part), BF16),
+            shape((rows, part), BF16),
+            shape(small.shape[1:], F32),
+            shape((8, 128), F32),
+        ),
+        in_specs=[hbm] * 8 + [vmem] * 11,
+        out_specs=(vmem,) * 8,
+        scratch_shapes=[pltpu.VMEM(turn.turned_shape(name), BF16) for name in NAMES] * 2
+        + [pltpu.VMEM((3,) + turn.piece_shape(name), BF16) for name in NAMES]
+        + scatter_scratch(rows, part) * 2
+        + back_scratch(rows, part)
+        + [
+            pltpu.VMEM(small.shape[1:], F32),
+            pltpu.VMEM((8, part), F32),
+            pltpu.VMEM((2, 4, 8, 128), F32),
+            pltpu.VMEM((7, 8, 128), F32),
+            pltpu.SemaphoreType.DMA((4,)),
+            pltpu.SemaphoreType.DMA((120,)),
+            pltpu.SemaphoreType.DMA((120,)),
+        ],
+        compiler_params=pltpu.CompilerParams(
+            collective_id=LAST, has_side_effects=True, vmem_limit_bytes=63 << 20
+        ),
+        name="end",
+    )(
+        *(grads0[name] for name in NAMES),
+        *(grads1[name] for name in NAMES),
+        partial_x,
+        block,
+        bias,
+        partial_g,
+        *blocks,
+        small,
+        sums1,
+    )
 
 
 def forward(x_full, layout, params):
@@ -138,7 +751,13 @@
     partial = jnp.einsum("cte,cde->td", d_qkv, w_qkv, preferred_element_type=F32) + jnp.einsum(
         "tf,df->td", d_hidden, w_up, preferred_element_type=F32
     )
-    return (partial.astype(BF16), (grad_qkv, grad_qkv_bias, grad_out, grad_up, grad_up_bias, grad_down))
+    grads = {
+        "qkv": grad_qkv.astype(BF16),
+        "out": grad_out.astype(BF16),
+        "up": grad_up.astype(BF16),
+        "down": grad_down.astype(BF16),
+    }
+    return (partial.astype(BF16), grads, (grad_qkv_bias, grad_up_bias))
 
 
 def shards(
@@ -158,112 +777,99 @@
     section = lax.axis_index("section")
     ctx = lax.axis_index("ctx")
     tp = lax.axis_index("tp")
+    rows, part = boundary.shape[2:]
+    slab = out_bias.shape[1]
+    layout = doc_layout(lax.dynamic_index_in_dim(doc_ids, section, 0, keepdims=False))
+    n_up = fc1_bias.shape[1] // slab
+    vector = jnp.concatenate(
+        [
+            (out_bias.astype(F32) + fc2_bias.astype(F32)),
+            norm_gain.astype(F32),
+            norm_shift.astype(F32),
+            qkv_bias[0].astype(F32),
+            fc1_bias.astype(F32).reshape(n_up, slab),
+        ]
+    )
+    vector = jnp.pad(vector, ((0, 16 - vector.shape[0]), (0, 0)))
+    shard_of = {"qkv": qkv_weight[0], "out": out_weight[0], "up": fc1_weight[0], "down": fc2_weight[0]}
+    *turned, x_full, g_full, x_block, g_block, vectors = begin(boundary[0], vector, shard_of)
+    turned = dict(zip(NAMES, turned))
+    wide = vectors.transpose(0, 3, 2, 1, 4).reshape(2, 16, -1)
+    local = lax.dynamic_index_in_dim(
+        lax.dynamic_index_in_dim(vectors, ctx, 1, keepdims=False), tp, 1, keepdims=False
+    )
+    params = [
+        (
+            turned["qkv"][layer],
+            local[layer, 3:6],
+            turned["out"][layer],
+            turned["up"][layer],
+            local[layer, 6 : 6 + n_up].reshape(-1),
+            turned["down"][layer],
+            wide[layer, 1],
+            wide[layer, 2],
+        )
+        for layer in (0, 1)
+    ]
+    own = lax.dynamic_slice_in_dim(wide, tp * part, part, axis=2)
+    bias = own[:, 0:1]
+    gain = own[:, 1:2]
+
+    def norm_rows(saved):
+        return tuple(lax.dynamic_slice_in_dim(array, ctx * rows, rows) for array in saved[:2])
+
+    partial, saved0 = forward(x_full, layout, params[0])
+    act0, x1_full = next_layer(partial, x_block, bias[0])
+    partial_x, saved1 = forward(x1_full, layout, params[1])
+    partial, grads1, small1 = backward(g_full, saved1, layout, params[1])
+    grad1, g1_full, sums1 = previous_layer(
+        partial, g_block, act0, *norm_rows(saved1), gain[1]
+    )
+    partial_g, grads0, small0 = backward(g1_full, saved0, layout, params[0])
+
+    def column_sum(full):
+        start = tp * part + ctx * slab
+        return jnp.sum(lax.dynamic_slice_in_dim(full, start, slab, axis=1).astype(F32), axis=0)
+
+    small = jnp.stack(
+        [
+            jnp.concatenate([grad[0], grad[1].reshape(n_up, slab), column_sum(full)[None]])
+            for grad, full in ((small0, g1_full), (small1, g_full))
+        ]
+    )
+    *weight_grads, act1, grad0, small, norms = end(
+        grads0,
+        grads1,
+        partial_x,
+        act0,
+        bias[1],
+        partial_g,
+        (grad1, x_block, *norm_rows(saved0), gain[0]),
+        small,
+        sums1,
+    )
+    g_qkv, g_out, g_up, g_down = weight_grads
     first = section == 0
-    tokens, part = boundary.shape[2], boundary.shape[3]
-    n_ctx = lax.axis_size("ctx")
-    own = boundary[0]
-    mine = lax.dynamic_index_in_dim(own, section, 0, keepdims=False)
-    theirs = swap_section(lax.dynamic_index_in_dim(own, 1 - section, 0, keepdims=False))
-    x_block = jnp.where(first, mine, theirs)
-    cotangent = jnp.where(first, theirs, mine)
-    ids = lax.dynamic_index_in_dim(doc_ids, section, 0, keepdims=False)
-    layout = doc_layout(ids)
-
-    def turn(weight, split, join):
-        return both_layers(
-            lax.all_to_all(weight, "ctx", split_axis=split, concat_axis=join, tiled=True)
-        )
-
-    w_qkv = turn(qkv_weight[0], 2, 1)
-    w_out = turn(out_weight[0], 0, 1)
-    w_up = turn(fc1_weight[0], 1, 0)
-    w_down = turn(fc2_weight[0], 0, 1)
-    b_qkv = both_layers(qkv_bias[0])
-    b_up = both_layers(fc1_bias[0])
-    vectors = jnp.concatenate([out_bias, fc2_bias, norm_gain, norm_shift], axis=0)
-    vectors = both_layers(
-        lax.all_gather(
-            lax.all_gather(vectors, "ctx", axis=1, tiled=True), "tp", axis=1, tiled=True
-        )
-    )
-    params = [
-        (w_qkv[l], b_qkv[l], w_out[l], w_up[l], b_up[l], w_down[l], vectors[l][2], vectors[l][3])
-        for l in (0, 1)
-    ]
-
-    def own_part(vector):
-        return lax.dynamic_slice_in_dim(vector, tp * part, part)
-
-    def add_up(block, partial, layer):
-        bias = own_part(vectors[layer][0]).astype(F32) + own_part(vectors[layer][1]).astype(F32)
-        return (block.astype(F32) + scatter_rows(partial).astype(F32) + bias).astype(BF16)
-
-    def rows_of(array):
-        return lax.dynamic_slice_in_dim(array, ctx * tokens, tokens)
-
-    def step_back(g_block, x_block, partial, saved, layer):
-        d_normed = scatter_rows(partial).astype(F32)
-        mean, inverse_std = (rows_of(saved[0]), rows_of(saved[1]))
-        centered = (x_block.astype(F32) - mean) * inverse_std
-        scaled = d_normed * own_part(vectors[layer][2]).astype(F32)
-        terms = lax.psum((jnp.sum(scaled, axis=1), jnp.sum(scaled * centered, axis=1)), "tp")
-        width = part * lax.axis_size("tp")
-        grad = g_block.astype(F32) + inverse_std * (
-            scaled - terms[0][:, None] / width - centered * (terms[1][:, None] / width)
-        )
-        return (grad.astype(BF16), jnp.sum(d_normed * centered, axis=0), jnp.sum(d_normed, axis=0))
-
-    x_full = gather_rows(x_block)
-    g_full = gather_rows(cotangent)
-    partial, saved0 = forward(x_full, layout, params[0])
-    act0 = add_up(x_block, partial, 0)
-    x1_full = gather_rows(act0)
-    partial, saved1 = forward(x1_full, layout, params[1])
-    act1 = add_up(act0, partial, 1)
-    partial, grads1 = backward(g_full, saved1, layout, params[1])
-    grad1, gain1, shift1 = step_back(cotangent, act0, partial, saved1, 1)
-    g1_full = gather_rows(grad1)
-    partial, grads0 = backward(g1_full, saved0, layout, params[0])
-    grad0, gain0, shift0 = step_back(grad1, x_block, partial, saved0, 0)
-
-    def home(zero, one):
-        sent = swap_section(jnp.where(first, one, zero).astype(BF16))
-        return jnp.where(first, zero, one) + sent.astype(F32)
-
-    def back(zero, one, split, join):
-        total = home(zero, one)
-        return lax.all_to_all(
-            total.astype(BF16), "ctx", split_axis=split, concat_axis=join, tiled=True
-        ).astype(F32)
 
     def pair(zero, one):
-        sent = swap_section(jnp.where(first, one, zero))
+        sent = lax.ppermute(jnp.where(first, one, zero), "section", [(0, 1), (1, 0)])
         kept = jnp.where(first, zero, one)
         return jnp.where(first, jnp.stack([kept, sent]), jnp.stack([sent, kept]))[None]
 
-    def column_sum(full):
-        slab = lax.dynamic_slice_in_dim(
-            full, tp * part + ctx * (part // n_ctx), part // n_ctx, axis=1
-        )
-        return jnp.sum(slab.astype(F32), axis=0)
-
-    def over_ctx(zero, one):
-        return lax.psum_scatter(home(zero, one), "ctx", scatter_dimension=0, tiled=True)
-
-    bias_out = home(column_sum(g1_full), column_sum(g_full))[None]
+    bias_out = small[3 + n_up][None]
     return (
         pair(act0, act1),
         pair(grad0, grad1),
-        back(grads0[0], grads1[0], 1, 2)[None],
-        home(grads0[1], grads1[1])[None],
-        back(grads0[2], grads1[2], 1, 0)[None],
+        g_qkv[None],
+        small[None, :3],
+        g_out[None],
         bias_out,
-        back(grads0[3], grads1[3], 0, 1)[None],
-        home(grads0[4], grads1[4])[None],
-        back(grads0[5], grads1[5], 1, 0)[None],
+        g_up[None],
+        small[3 : 3 + n_up].reshape(1, -1),
+        g_down[None],
         bias_out,
-        over_ctx(gain0, gain1)[None],
-        over_ctx(shift0, shift1)[None],
+        norms[0:1],
+        norms[1:2],
     )
 
 
@@ -596,9 +1202,10 @@
     weights = ("token", "vectors", "rows", "vector", "columns", "vector", "rows", "vector", "vector", "vector")
     placed = tuple(specs[name] for name in weights)
     heads = D // HD
+    place = {"section": 2, "ctx": 4, "tp": 4}
     whole_heads = heads % (mesh.shape["tp"] * mesh.shape["ctx"]) == 0
     return jax.shard_map(
-        shards if whole_heads and mesh.shape["section"] == 2 else base_shards,
+        shards if whole_heads and dict(mesh.shape) == place else base_shards,
         mesh=mesh,
         in_specs=(specs["token"], P(), *placed),
         out_specs=(specs["token"], specs["token"], *placed),

time: 1130 us -> 817 us (0.72)
  waiting for transfers between devices: 698 us -> 5.08 us
  Pallas kernels: 0 us -> 570 us
  blocking collectives: 66.8 us -> 0 us
  starting transfers between devices: 66.5 us -> 2.16 us
  other arithmetic: 65.8 us -> 30.1 us
  local copies, waits for them, and re-layouts: 66.2 us -> 51.7 us
  between operations: 16.2 us -> 2.12 us
    pallas_call x0 -> x4, Pallas kernels: none -> 570 us  [the longest x1 217 us: end(): pl.pallas_call(functools.partial(end_kernel, turn, rows, part), out_shape...]
    reduce_scatter x8 -> x0, waiting for transfers between devices: 195 us -> none  [the longest x4 139 us: scatter_rows(): lax.psum_scatter(partial, 'tp', scatter_dimension=1, tiled=True)]
    ppermute x19 -> x2, waiting for transfers between devices: 187 us -> 5.08 us  [pair(): lax.ppermute(jnp.where(first, one, zero), 'section', [(0, 1), (1, 0)])]
    all_gather x8 -> x0, waiting for transfers between devices: 177 us -> none  [the longest x4 103 us: gather_rows(): lax.all_gather(lax.all_gather(block, 'ctx', axis=0, tiled=True), 'tp', ax...]
    all_to_all x8 -> x0, waiting for transfers between devices: 138 us -> none  [the longest x4 105 us: turn(): lax.all_to_all(weight, 'ctx', split_axis=split, concat_axis=join, tiled=T...]
    all_gather x2 -> x0, blocking collectives: 45 us -> none  [the longest x1 39.2 us: shards(): lax.all_gather(vectors, 'ctx', axis=1, tiled=True)]
    all_to_all x8 -> x0, starting transfers between devices: 37.1 us -> none  [the longest x4 18.8 us: back(): lax.all_to_all(total.astype(BF16), 'ctx', split_axis=split, concat_axis=j...]
    ppermute x19 -> x2, starting transfers between devices: 28.5 us -> 2.16 us  [pair(): lax.ppermute(jnp.where(first, one, zero), 'section', [(0, 1), (1, 0)])]
  transfers between devices with their start and end apart: 43 -> 2, of which waited for: 24 -> 2; matrix products, arithmetic and copies ran while one was open for 18% -> 1% of each run, Pallas kernels for 0% -> 0%
where the time goes in v2:
time: 817 us; the launch traced here: 807 us
  Pallas kernels  570 us (70%)
  matrix products  145 us (18%)
  local copies, waits for them, and re-layouts  51.7 us (6%)
  other arithmetic  30.1 us (4%)
    pallas_call x1, Pallas kernels, end(): pl.pallas_call(functools.partial(end_kernel, turn, rows, part), out_shape...  217 us
    pallas_call x1, Pallas kernels, begin(): pl.pallas_call(functools.partial(begin_kernel, turn, rows, part), out_sha...  215 us
    pallas_call x1, Pallas kernels, previous_layer(): pl.pallas_call(functools.partial(previous_layer_kernel, rows, part), out_...  68.8 us
    pallas_call x1, Pallas kernels, next_layer(): pl.pallas_call(functools.partial(next_layer_kernel, rows, part), out_shap...  68.5 us
    unnamed x202, local copies, waits for them, and re-layouts  25 us
    reduce_sum x2, matrix products, forward(): totals = jnp.sum(jnp.where(allowed[None], jnp.exp(scores), 0.0), axis=2)  18.1 us
  transfers between devices with their start and end apart: 2, of which 2 were waited for; matrix products, arithmetic and copies ran while one was open for 1% of the time, Pallas kernels for 0%

profile of v2, /device:TPU:0, one launch (start us, length us, event | category | flops | bytes accessed | tf_op | source)
XLA Modules:
  0.0 806.6 jit_solution(16682619200551841836)
XLA Ops:
  12.9 215.3 %begin.1 = (bf16[2,3,2048,128]{3,2,1,0:T(8,128)(2,1)S(1)}, bf16[2,128,2048]{2,1,0:T(8,128)(2,1)S(1)}, bf16[2,2048,512]{2,1,0:T(8,128)(2,1)}, bf16[2,512,2048]{2,...) custom-call(bf16[2,256,512]{2,1,0:T(8,128)(2,1)S(1)} %bitcast.223, ...), custom_call_target="tpu_custom_call" | custom-call | tf_op jit(solution)/shard_map/begin/pallas_call | solution.py:513
  246.3 3.7 fusion.81
  252.7 9.1 %fusion.15 = f32[2,1024,1024]{1,2,0:T(8,128)} fusion(pred[1024,1024]{0,1:T(8,128)(4,1)} %fusion.40, bf16[1024,2,32]{0,2,1:T(8,128)(2,1)S(1)} %slice.385, bf16[1024,2,16]{0,2,1:T(8,128)(2,1)} %get-tuple-element.122, bf16[1024,2,16]{0,2,1:T(8,128)(2,1)} %get-tuple-element.123, bf16[1024,2,32]{0,2,1:T(8,128)(2,1)S(1)} %slice.386, ...), kind=kOutput, calls=%fused_computation.23 | convolution fusion | flops 550505472 | bytes 9961472 | tf_op jit(solution)/shard_map/reduce_sum | solution.py:701
  261.9 4.4 fusion.119
  267.7 4.9 fusion.77
  273.9 68.5 %next_layer.1 = (bf16[256,512]{1,0:T(8,128)(2,1)S(1)}, bf16[1024,2048]{1,0:T(8,128)(2,1)S(1)}) custom-call(bf16[1024,2048]{1,0:T(8,128)(2,1)S(1)} %add_convert_fusion.1.partial, bf16[256,512]{1,0:T(8,128)(2,1)S(1)} %copy-done.10, f32[1,512]{1,0:T(1,128)S(1)} %get-tuple-element.111.bias), custom_call_target="tpu_custom_call" | custom-call | tf_op jit(solution)/shard_map/next_layer/pallas_call | solution.py:266
  352.9 9.0 %fusion.13 = f32[2,1024,1024]{1,2,0:T(8,128)} fusion(pred[1024,1024]{0,1:T(8,128)(4,1)} %fusion.40, bf16[1024,2,32]{0,2,1:T(8,128)(2,1)} %slice.383, bf16[1024,2,16]{0,2,1:T(8,128)(2,1)} %get-tuple-element.120, bf16[1024,2,16]{0,2,1:T(8,128)(2,1)} %get-tuple-element.121, bf16[1024,2,32]{0,2,1:T(8,128)(2,1)} %slice.384, ...), kind=kOutput, calls=%fused_computation.20 | convolution fusion | flops 550505472 | bytes 9961472 | tf_op jit(solution)/shard_map/reduce_sum | solution.py:701
  362.0 5.1 multiply_reduce_fusion.1
  391.6 7.7 fusion.157
  399.3 5.7 fusion.67
  405.9 6.7 fusion.17.partial
  412.7 68.8 %previous_layer.1 = (bf16[256,512]{1,0:T(8,128)(2,1)S(1)}, bf16[1024,2048]{1,0:T(8,128)(2,1)S(1)}, f32[8,512]{1,0:T(8,128)S(1)}) custom-call(bf16[1024,2048]{1,0:T(8,128)(2,1)S(1)} %fusion.17.partial, bf16[256,512]{1,0:T(8,128)(2,1)S(1)} %copy-done.21, bf16[256,512]{1,0:T(8,128)(2,1)S(1)} %get-tuple-element.41.x_block.refs_9_, f32[256,1]{1,0:T(8,128)S(1)} %copy.56.mean, ...), custom_call_target="tpu_custom_call" | custom-call | tf_op jit(solution)/shard_map/previous_layer/pallas_call | solution.py:366
  483.1 4.8 multiply_convert_fusion
  494.4 5.1 fusion.158
  503.7 8.3 %fusion.71 = f32[1024,2048]{1,0:T(8,128)} fusion(bf16[2,512,2048]{2,1,0:T(8,128)(2,1)} %get-tuple-element.39, f32[1024,512]{1,0:T(8,128)} %fusion.69, f32[512]{0:T(512)S(1)} %copy-done.79), kind=kOutput, calls=%fused_computation.87 | convolution fusion | flops 2152726528 | bytes 12584960 | tf_op jit(solution)/shard_map/dot_general | solution.py:712
  512.1 3.8 convolution_convert_fusion.1.refs_6_
  519.4 4.1 convolution_convert_fusion.2.refs_3_
  523.6 5.7 fusion.79
  529.3 3.8 convolution_convert_fusion.3.refs_2_
  534.9 3.8 fusion.52.refs_0_
  538.7 4.0 convolution_convert_fusion.refs_7_
  544.3 8.4 %fusion.16.refs_11_ = bf16[1024,2048]{1,0:T(8,128)(2,1)} fusion(f32[1024,2048]{1,0:T(8,128)} %fusion.79, bf16[2,3,2048,128]{3,2,1,0:T(8,128)(2,1)S(1)} %get-tuple-element.34, f32[1,1024,128]{1,2,0:T(8,128)} %bitcast.228, f32[1,1024,128]{1,2,0:T(8,128)} %bitcast.236, f32[1,1024,128]{1,2,0:T(8,128)} %bitcast.233), kind=kOutput, calls=%fused_computation.25 | convolution fusion | flops 1615593472 | bytes 15728640 | tf_op jit(solution)/shard_map/cte,cde->td/dot_general | solution.py:751
  554.2 6.7 add_convert_fusion.refs_8_
  563.2 217.5 %end.1 = (f32[3,512,512]{2,1,0:T(8,128)}, f32[512,512]{1,0:T(8,128)}, f32[512,2048]{1,0:T(8,128)}, f32[2048,512]{1,0:T(8,128)}, bf16[256,512]{1,0:T(8,128)(2,1)}...) custom-call(bf16[3,2048,128]{2,1,0:T(8,128)(2,1)} %fusion.52.refs_0_, ...), custom_call_target="tpu_custom_call" | custom-call | tf_op jit(solution)/shard_map/end/pallas_call | solution.py:640
  (292 shorter events, 119.7 us)
Async XLA Ops:
  250.9 132.4 %copy-start.50 = (f32[1024,16]{0,1:T(8,128)}, f32[1024,16]{0,1:T(8,128)S(1)}, u32[]{:S(2)}) copy-start(f32[1024,16]{0,1:T(8,128)S(1)} %get-tuple-element.130) | copy-start | bytes 196612
  273.9 69.8 %copy-start.72 = (f32[1,1,2048]{2,1,0:T(1,128)S(1)}, f32[1,1,2048]{2,1,0:T(1,128)}, u32[]{:S(2)}) copy-start(f32[1,1,2048]{2,1,0:T(1,128)} %get-tuple-element.113) | copy-start | bytes 24580
  342.4 70.2 %copy-start.4 = (bf16[256,512]{1,0:T(8,128)(2,1)}, bf16[256,512]{1,0:T(8,128)(2,1)S(1)}, u32[]{:S(2)}) copy-start(bf16[256,512]{1,0:T(8,128)(2,1)S(1)} %get-tuple-element.41.x_block.refs_9_) | copy-start | bytes 786436
  391.6 7.7 copy-start.85
  412.6 68.9 %copy-start.15 = (bf16[2,128,2048]{2,1,0:T(8,128)(2,1)S(1)}, bf16[2,128,2048]{2,1,0:T(8,128)(2,1)}, u32[]{:S(2)}) copy-start(bf16[2,128,2048]{2,1,0:T(8,128)(2,1)} %copy-done.13) | copy-start | bytes 3145732
  412.7 68.9 %copy-start.43 = (bf16[2,64,1024]{2,1,0:T(8,128)(2,1)S(1)}, bf16[2,64,1024]{2,1,0:T(8,128)(2,1)}, u32[]{:S(2)}) copy-start(bf16[2,64,1024]{2,1,0:T(8,128)(2,1)} %copy-done.42) | copy-start | bytes 786436
  481.5 12.0 %copy-start.2 = (bf16[1024,2048]{1,0:T(8,128)(2,1)}, bf16[1024,2048]{1,0:T(8,128)(2,1)S(1)}, u32[]{:S(2)}) copy-start(bf16[1024,2048]{1,0:T(8,128)(2,1)S(1)} %get-tuple-element.45) | copy-start | bytes 12582916
  483.1 8.2 %slice-start = ((s8[8388608]{0:T(1024)(128)(4,1)}), s8[4194304]{0:T(1024)(128)(4,1)S(1)}, s32[]{:S(2)}) async-start(s8[8388608]{0:T(1024)(128)(4,1)} %bitcast.226), calls=%async_computation | async-start | bytes 8388608
  483.1 8.1 %slice-start.1 = ((s8[8388608]{0:T(1024)(128)(4,1)}), s8[4194304]{0:T(1024)(128)(4,1)S(1)}, s32[]{:S(2)}) async-start(s8[8388608]{0:T(1024)(128)(4,1)} %bitcast.226), calls=%async_computation.1 | async-start | bytes 8388608
  494.4 9.4 %copy-start.79 = (f32[512]{0:T(512)S(1)}, f32[512]{0:T(512)}, u32[]{:S(2)}) copy-start(f32[512]{0:T(512)} %get-tuple-element.126) | copy-start | bytes 6148
  503.7 8.3 %copy-start.38 = (bf16[1024,2048]{1,0:T(8,128)(2,1)S(1)}, bf16[1024,2048]{1,0:T(8,128)(2,1)}, u32[]{:S(2)}) copy-start(bf16[1024,2048]{1,0:T(8,128)(2,1)} %copy-done.36) | copy-start | bytes 12582916
  503.7 8.3 %copy-start.90 = (bf16[1024,512]{1,0:T(8,128)(2,1)S(1)}, bf16[1024,512]{1,0:T(8,128)(2,1)}, u32[]{:S(2)}) copy-start(bf16[1024,512]{1,0:T(8,128)(2,1)} %copy-done.89) | copy-start | bytes 3145732
  544.2 8.5 %copy-start.26 = (bf16[1024,2048]{1,0:T(8,128)(2,1)S(1)}, bf16[1024,2048]{1,0:T(8,128)(2,1)}, u32[]{:S(2)}) copy-start(bf16[1024,2048]{1,0:T(8,128)(2,1)} %get-tuple-element.43) | copy-start | bytes 12582916
  544.2 8.5 %copy-start.46 = (bf16[2,64,1024]{2,1,0:T(8,128)(2,1)S(1)}, bf16[2,64,1024]{2,1,0:T(8,128)(2,1)}, u32[]{:S(2)}) copy-start(bf16[2,64,1024]{2,1,0:T(8,128)(2,1)} %get-tuple-element.138) | copy-start | bytes 786436
  554.2 8.3 %copy-start.76 = (f32[128]{0:T(128)S(1)}, f32[128]{0:T(128)}, u32[]{:S(2)}) copy-start(f32[128]{0:T(128)} %convert_reduce_fusion.4) | copy-start | bytes 1540
  554.2 8.3 %copy-start.78 = (f32[512]{0:T(512)S(1)}, f32[512]{0:T(512)}, u32[]{:S(2)}) copy-start(f32[512]{0:T(512)} %get-tuple-element.143) | copy-start | bytes 6148
  554.2 8.3 %copy-start.77 = (f32[512]{0:T(512)S(1)}, f32[512]{0:T(512)}, u32[]{:S(2)}) copy-start(f32[512]{0:T(512)} %get-tuple-element.141) | copy-start | bytes 6148
  563.2 217.5 %copy-start.12 = (bf16[256,512]{1,0:T(8,128)(2,1)S(1)}, bf16[256,512]{1,0:T(8,128)(2,1)}, u32[]{:S(2)}) copy-start(bf16[256,512]{1,0:T(8,128)(2,1)} %copy-done.11) | copy-start | bytes 786436
  563.2 219.5 %copy-start.5 = (bf16[256,512]{1,0:T(8,128)(2,1)S(1)}, bf16[256,512]{1,0:T(8,128)(2,1)}, u32[]{:S(2)}) copy-start(bf16[256,512]{1,0:T(8,128)(2,1)} %copy-done.4) | copy-start | bytes 786436
  780.6 16.1 %copy-start.41 = (f32[3,512,512]{2,1,0:T(8,128)S(1)}, f32[3,512,512]{2,1,0:T(8,128)}, u32[]{:S(2)}) copy-start(f32[3,512,512]{2,1,0:T(8,128)} %get-tuple-element.50) | copy-start | bytes 9437188
  781.8 9.2 %collective-permute-start.1 = (bf16[256,512]{1,0:T(8,128)(2,1)S(1)}, bf16[256,512]{1,0:T(8,128)(2,1)S(1)}, u32[]{:S(2)}, u32[]{:S(2)}) collective-permute-start(bf16[256,512]{1,0:T(8,128)(2,1)S(1)} %get-tuple-element.105), channel_id=1, source_target_pairs={{0,16},{16,0},{1,17},{17,1},{2,18},{18,2},{3,19},{19,3},{4,20},{20... | collective-permute-start | bytes 786440 | tf_op jit(solution)/shard_map/ppermute | solution.py:855
  783.6 11.7 %collective-permute-start = (bf16[256,512]{1,0:T(8,128)(2,1)S(1)}, bf16[256,512]{1,0:T(8,128)(2,1)S(1)}, u32[]{:S(2)}, u32[]{:S(2)}) collective-permute-start(bf16[256,512]{1,0:T(8,128)(2,1)S(1)} %get-tuple-element.107), channel_id=1, source_target_pairs={{0,16},{16,0},{1,17},{17,1},{2,18},{18,2},{3,19},{19,3},{4,20},{20... | collective-permute-start | bytes 786440 | tf_op jit(solution)/shard_map/ppermute | solution.py:855
  787.6 10.8 %copy-start.88 = (f32[1,128]{1,0:T(1,128)}, f32[1,128]{1,0:T(1,128)S(1)}, u32[]{:S(2)}) copy-start(f32[1,128]{1,0:T(1,128)S(1)} %slice.228) | copy-start | bytes 1540
  791.0 7.4 copy-start.54
  (77 other events, 249.5 us)

commit v3 on v0

v3 whole, which is shorter than its diff:
```python
import functools
import itertools

import jax
import jax.numpy as jnp
from jax import lax
from jax.experimental import pallas as pl
from jax.experimental.pallas import tpu as pltpu
from jax.sharding import PartitionSpec as P

D = 2048
HD = 64
ROT = 32
EPS = 1e-05
GELU_C = 0.7978845608028654
GELU_K = 0.044715
ACT = "act"
ACTS = "acts"
ARRIVED = "arrived_"
ATT = "att"
BOUNCE = "bounce_"
B_QKV = "b_qkv"
B_UP = "b_up"
COLUMNS = "columns"
CORES = "cores"
COSINE = "cosine"
CTX = "ctx"
DOWN = "down"
D_W = "d_w_"
G = "g"
G1 = "g1"
GAIN = "gain"
GAIN_BLOCK = "gain_block"
GRAD = "grad"
GRADS = "grads"
G_BLOCK = "g_block"
HEADS_EQ = "hts,shd->thd"
HIDDEN = "hidden"
HOME = "home_"
INVERSE_STD = "inverse_std"
KEPT = "kept_"
KEYS_EQ = "hts,thd->shd"
LSE = "lse"
MEAN = "mean"
MEAN_BLOCK = "mean_block"
NORMED = "normed"
NORM_SUM = "norm_sum"
N_START = "start"
ONE = "one_"
OUT = "out"
PARTIAL = "partial"
QKV = "qkv"
ROWS = "rows"
SCORES_EQ = "thd,shd->hts"
SECTION = "section"
SHARD = "shard_"
SHIFT = "shift"
SINE = "sine"
SLOPE = "slope"
SMALL_SUM = "small_sum"
STD_BLOCK = "std_block"
SUMS = "sums"
TOKEN = "token"
TP = "tp"
TURNED = "turned_"
UP = "up"
VECTOR = "vector"
VECTORS = "vectors"
W = "w_"
X = "x"
X1 = "x1"
X_BLOCK = "x_block"
BF16 = jnp.bfloat16
F32 = jnp.float32


def rope_tables(positions):
    half = ROT // 2
    freq = 10000.0 ** (-(jnp.arange(half).astype(F32) * 2.0 / ROT))
    angle = positions.astype(F32)[:, None] * freq[None, :]
    return (jnp.cos(angle), jnp.sin(angle))


def rotate(field, cosine, sine, sign):
    half = ROT // 2
    first = field[..., :half]
    second = field[..., half:ROT]
    cosine = cosine[:, None, :]
    sine = sine[:, None, :] * sign
    return jnp.concatenate(
        [first * cosine - second * sine, second * cosine + first * sine, field[..., ROT:]], axis=-1
    )


def doc_tables(ids, heads):
    length = ids.shape[0]
    start = jnp.sum((ids[None, :] < ids[:, None]).astype(jnp.int32), axis=1)
    cosine, sine = rope_tables(jnp.arange(length, dtype=jnp.int32) - start)
    still = jnp.ones((length, HD - ROT), F32)
    cosine = jnp.tile(jnp.concatenate([cosine, cosine, still], axis=1), (1, heads))
    sine = jnp.tile(jnp.concatenate([-sine, sine, 0.0 * still], axis=1), (1, heads))
    return {N_START: start[:, None], COSINE: cosine, SINE: sine}


MESH = pl.DeviceIdType.MESH
FWD, BWD, LAST, START = 0, 1, 2, 3
GROUPS = 2


class Wire:
    def __init__(self, send_sems, recv_sems):
        self.send_sems, self.recv_sems = send_sems, recv_sems
        self.copies = []
        self.section = lax.axis_index(SECTION)
        self.c = lax.axis_index(CTX)
        self.t = lax.axis_index(TP)
        self.y = self.t // 2
        self.k = self.t % 2
        self.c_up = (self.c + 1) % 4
        self.c_far = (self.c + 2) % 4
        self.c_down = (self.c + 3) % 4
        self.t_y = (self.t + 2) % 4
        self.t_core = self.t + 1 - 2 * self.k
        self.up = {CTX: jnp.minimum(self.c + 1, 3)}
        self.down = {CTX: jnp.maximum(self.c - 1, 0)}
        self.beside = {TP: self.t_y}
        self.core = {TP: self.t_core}
        self.across = {SECTION: 1 - self.section}
        self.others = [(2, self.c_far), (1, self.c_up), (3, self.c_down)]

    def greet(self, targets):
        barrier = pltpu.get_barrier_semaphore()
        for target in targets:
            pl.semaphore_signal(barrier, inc=1, device_id=target, device_id_type=MESH)
        pl.semaphore_wait(barrier, len(targets))

    def send(self, source, target, device, when=None):
        index = len(self.copies)
        copy = pltpu.make_async_remote_copy(
            src_ref=source,
            dst_ref=target,
            send_sem=self.send_sems.at[index],
            recv_sem=self.recv_sems.at[index],
            device_id=device,
            device_id_type=MESH,
        )
        if when is None:
            copy.start()
        else:
            pl.when(when)(copy.start)
        self.copies.append((copy, when))
        return copy

    def send_one_of(self, first, source, other_source, target, device):
        index = len(self.copies)
        copies = [
            pltpu.make_async_remote_copy(
                src_ref=ref,
                dst_ref=target,
                send_sem=self.send_sems.at[index],
                recv_sem=self.recv_sems.at[index],
                device_id=device,
                device_id_type=MESH,
            )
            for ref in (source, other_source)
        ]
        pl.when(first)(copies[0].start)
        pl.when(jnp.logical_not(first))(copies[1].start)
        self.copies.append((copies[0], None))
        return copies[0]

    def flush(self, indices):
        for index in indices:
            if self.copies[index] is not None:
                copy, when = self.copies[index]
                self.copies[index] = None
                if when is None:
                    copy.wait_send()
                else:
                    pl.when(when)(copy.wait_send)

    def drain(self):
        self.flush(range(len(self.copies)))

    def meet(self, semaphore, peers):
        for peer in peers:
            pl.semaphore_signal(semaphore, inc=1, device_id=peer, device_id_type=MESH)
        pl.semaphore_wait(semaphore, len(peers))


class Gather:
    def __init__(self, wire, full, rows, part, skew=1):
        self.w, self.full, self.rows, self.part = wire, full, rows, part
        self.size, self.skew = rows // GROUPS, skew
        self.hops, self.beside = {}, {}

    def region(self, c, t, group):
        return self.full.at[
            pl.ds(pl.multiple_of(c * self.rows + group * self.size, 16), self.size),
            pl.ds(pl.multiple_of(t * self.part, 128), self.part),
        ]

    def pass_on(self, device, c, t, group, when=None):
        spot = self.region(c, t, group)
        return self.w.send(spot, spot, device, when)

    def begin(self, group):
        w = self.w
        self.hops[group, 1] = self.pass_on(w.up, w.c, w.t, group, w.c < 3)
        self.hops[group, -1] = self.pass_on(w.down, w.c, w.t, group, w.c > 0)
        self.beside[group, 0] = self.pass_on(w.beside, w.c, w.t, group)
        self.cores = getattr(self, CORES, [])
        self.cores.append((self.pass_on(w.core, w.c, w.t, group), None))

    def steps(self):
        return itertools.chain(self.along(), self.around())

    def hop_order(self):
        events = [
            (group, sign * hop) for group in range(GROUPS) for hop in (1, 2, 3) for sign in (1, -1)
        ]
        return sorted(events, key=lambda event: (self.skew * event[0] + abs(event[1]), event[0]))

    def along(self):
        w = self.w
        for group, hop in self.hop_order():
            source = jnp.clip(w.c - hop, 0, 3)
            there = w.c >= hop if hop > 0 else w.c - hop <= 3
            pl.when(there)(self.hops[group, hop].wait_recv)
            if abs(hop) < 3:
                further = hop + (1 if hop > 0 else -1)
                ahead = w.c < 3 if hop > 0 else w.c > 0
                self.hops[group, further] = self.pass_on(
                    w.up if hop > 0 else w.down, source, w.t, group, jnp.logical_and(there, ahead)
                )
            self.beside[group, hop] = self.pass_on(w.beside, source, w.t, group, there)
            self.cores.append((self.pass_on(w.core, source, w.t, group, there), there))
            yield

    def around(self):
        w = self.w
        for group, hop in [(group, 0) for group in range(GROUPS)] + self.hop_order():
            source = jnp.clip(w.c - hop, 0, 3)
            there = None if hop == 0 else w.c >= hop if hop > 0 else w.c - hop <= 3
            copy = self.beside[group, hop]
            copy.wait_recv() if there is None else pl.when(there)(copy.wait_recv)
            self.cores.append((self.pass_on(w.core, source, w.t_y, group, there), there))
            yield
        for copy, there in self.cores:
            copy.wait_recv() if there is None else pl.when(there)(copy.wait_recv)


class DirectGather(Gather):
    def begin(self, group):
        w = self.w
        for step, place in w.others:
            self.hops[group, step] = self.pass_on({CTX: place}, w.c, w.t, group)
        self.beside[group, 0] = self.pass_on(w.beside, w.c, w.t, group)
        self.cores = getattr(self, CORES, [])
        self.cores.append((self.pass_on(w.core, w.c, w.t, group), None))

    def steps(self):
        w = self.w
        order = [(group, step) for group in range(GROUPS) for step in (1, 3, 2)]
        for group, step in order:
            source = (w.c + 4 - step) % 4
            self.hops[group, step].wait_recv()
            self.beside[group, step] = self.pass_on(w.beside, source, w.t, group)
            self.cores.append((self.pass_on(w.core, source, w.t, group), None))
            yield
        for group, step in [(group, 0) for group in range(GROUPS)] + order:
            self.beside[group, step].wait_recv()
            source = (w.c + 4 - step) % 4
            self.cores.append((self.pass_on(w.core, source, w.t_y, group), None))
            yield
        for copy, _ in self.cores:
            copy.wait_recv()


def scatter_scratch(rows, part):
    return [
        pltpu.VMEM((2, 4 * rows, part), BF16),
        pltpu.VMEM((2, 4 * rows, part), BF16),
        pltpu.VMEM((4 * rows, part), BF16),
        pltpu.VMEM((3, rows, part), BF16),
    ]


class Scatter:
    def __init__(self, wire, partial, scratch, rows, part):
        self.w, self.partial, self.rows, self.part = wire, partial, rows, part
        self.theirs, self.chip, self.from_y, self.from_far = scratch
        w = wire
        self.places = [(2, w.c_far), (1, w.c_up), (3, w.c_down), (0, w.c)]
        self.order = [
            (group, c, y)
            for group in (0, 1)
            for y in (1 - w.y, w.y)
            for _, c in self.places
        ]
        self.far, self.sent = {}, []

    def send(self, source, target, device):
        self.sent.append(len(self.w.copies))
        return self.w.send(source, target, device)

    def span(self, group, c):
        size = self.rows // 2
        return pl.ds(pl.multiple_of(c * self.rows + group * size, 16), size)

    def begin(self):
        w = self.w
        self.cores = []
        for group, c, y in self.order:
            columns = pl.ds(pl.multiple_of((2 * y + 1 - w.k) * self.part, 128), self.part)
            self.cores.append(
                self.send(
                    self.partial.at[self.span(group, c), columns],
                    self.theirs.at[y, self.span(group, c)],
                    w.core,
                )
            )

    def take(self, index):
        group, c, y = self.order[index]
        self.cores[index].wait_recv()
        rows = self.span(group, c)
        columns = pl.ds(pl.multiple_of((2 * y + self.w.k) * self.part, 128), self.part)
        return self.partial[rows, columns].astype(F32) + self.theirs[y, rows].astype(F32)

    def run(self):
        for _ in self.steps():
            pass

    def steps(self):
        w = self.w
        half = self.rows // 2
        beside = {}
        for group in (0, 1):
            for slot, (_, c) in enumerate(self.places):
                rows = self.span(group, c)
                self.chip[1 - w.y, rows] = self.take(8 * group + slot).astype(BF16)
                beside[group, slot] = self.send(
                    self.chip.at[1 - w.y, rows], self.from_y.at[rows], w.beside
                )
                yield
        for group in (0, 1):
            for slot, (step, c) in enumerate(self.places):
                rows = self.span(group, c)
                value = self.take(8 * group + 4 + slot)
                beside[group, slot].wait_recv()
                self.chip[w.y, rows] = (value + self.from_y[rows].astype(F32)).astype(BF16)
                if step:
                    self.far[group, step] = self.send(
                        self.chip.at[w.y, rows],
                        self.from_far.at[step - 1, pl.ds(group * half, half)],
                        {CTX: c},
                    )
                yield

    def total(self, group):
        half = self.rows // 2
        value = self.chip[self.w.y, self.span(group, self.w.c)].astype(F32)
        for step in (1, 3, 2):
            self.far[group, step].wait_recv()
            value += self.from_far[step - 1, pl.ds(group * half, half)].astype(F32)
        return value


def neighbours(w):
    return [{CTX: place} for _, place in w.others] + [w.beside, w.core]


def diagonal(w):
    return {TP: (w.t_core + 2) % 4}


def back_scratch(rows, part):
    return [
        pltpu.VMEM((rows, part), F32),
        pltpu.VMEM((GROUPS, 8, 128), F32),
        pltpu.VMEM((GROUPS, 3, 8, 128), F32),
    ]


def norm_back(w, scatter, blocks, scratch, rows, part, grad, sums, done, fill=iter(())):
    g_block, x_block, mean, inverse_std, gain = blocks
    d_normed, row_out, row_in = scratch
    half = rows // GROUPS
    width = 4 * part
    lane = lax.broadcasted_iota(jnp.int32, (128, 128), 1)
    sent = []
    gain_sum = jnp.zeros((1, part), F32)
    shift_sum = jnp.zeros((1, part), F32)
    for group in range(GROUPS):
        own = slice(group * half, (group + 1) * half)
        value = scatter.total(group)
        for _ in range(2):
            next(fill, None)
        d_normed[own] = value
        centered = (x_block[own].astype(F32) - mean[own]) * inverse_std[own]
        weighted = value * centered
        gain_sum += jnp.sum(weighted, axis=0, keepdims=True)
        shift_sum += jnp.sum(value, axis=0, keepdims=True)
        first = jnp.sum(value * gain[...], axis=1, keepdims=True)
        second = jnp.sum(weighted * gain[...], axis=1, keepdims=True)
        packed = jnp.where(lane == 0, first, jnp.where(lane == 1, second, 0.0))
        row_out[group] = packed.T[:8]
        sent.append(
            [
                w.send(row_out.at[group], row_in.at[group, slot], peer)
                for slot, peer in enumerate((w.beside, w.core, diagonal(w)))
            ]
        )
    sums[...] = jnp.concatenate(
        [gain_sum, shift_sum, jnp.zeros((6, part), F32)], axis=0
    )
    for group in range(GROUPS):
        own = slice(group * half, (group + 1) * half)
        next(fill, None)
        for copy in sent[group]:
            copy.wait_recv()
        rows_sum = row_out[group] + row_in[group, 0] + row_in[group, 1] + row_in[group, 2]
        columns = jnp.concatenate([rows_sum, jnp.zeros((half - 8, 128), F32)], axis=0).T
        centered = (x_block[own].astype(F32) - mean[own]) * inverse_std[own]
        scaled = d_normed[own] * gain[...]
        value = g_block[own].astype(F32) + inverse_std[own] * (
            scaled - columns[:, 0:1] / width - centered * (columns[:, 1:2] / width)
        )
        grad[own] = value.astype(BF16)
        done(group)


class Turn:
    def __init__(self, d_part, e_part, f_part):
        self.d, self.e, self.f = d_part, e_part, f_part

    def rows(self, name):
        return {QKV: self.d, OUT: self.e, UP: self.d, DOWN: self.f}[name]

    def inner(self, name, half):
        size = self.rows(name)
        return (0, size) if half is None else (half * size // 2, size // 2)

    def shard(self, name, ref, c, half=None):
        start, size = self.inner(name, half)
        if name == QKV:
            return ref.at[:, pl.ds(start, size), pl.ds(pl.multiple_of(c * self.e, 128), self.e)]
        if name == UP:
            return ref.at[pl.ds(start, size), pl.ds(pl.multiple_of(c * self.f, 128), self.f)]
        stride = self.e if name == OUT else self.f
        return ref.at[pl.ds(pl.multiple_of(c * stride + start, 16), size)]

    def turned(self, name, ref, c, half=None):
        start, size = self.inner(name, half)
        if name == QKV:
            return ref.at[:, pl.ds(pl.multiple_of(c * self.d + start, 16), size)]
        if name == UP:
            return ref.at[pl.ds(pl.multiple_of(c * self.d + start, 16), size)]
        return ref.at[pl.ds(start, size), pl.ds(pl.multiple_of(c * self.d, 128), self.d)]

    def piece_shape(self, name, halved=False):
        size = self.rows(name) // (2 if halved else 1)
        return {
            QKV: (3, size, self.e),
            OUT: (size, self.d),
            UP: (size, self.f),
            DOWN: (size, self.d),
        }[name]

    def turned_shape(self, name):
        return {
            QKV: (3, 4 * self.d, self.e),
            OUT: (self.e, 4 * self.d),
            UP: (4 * self.d, self.f),
            DOWN: (self.f, 4 * self.d),
        }[name]


NAMES = (QKV, OUT, UP, DOWN)


def everyone(w):
    return [
        {SECTION: (w.section + ds) % 2, CTX: (w.c + dc) % 4, TP: (w.t + dt) % 4}
        for ds in range(2)
        for dc in range(4)
        for dt in range(4)
        if (ds, dc, dt) != (0, 0, 0)
    ]


TILE = 256


def dot(a, b, contract=((1,), (0,))):
    return lax.dot_general(a, b, (contract, ((), ())), preferred_element_type=F32)


def tile(i, size=TILE):
    return pl.ds(pl.multiple_of(i * size, size), size)


def turn_heads(value, cosine, sine, sign):
    half = ROT // 2
    width = value.shape[1]
    lane = lax.broadcasted_iota(jnp.int32, value.shape, 1) % HD
    partner = jnp.where(
        lane < half, pltpu.roll(value, width - half, 1), pltpu.roll(value, half, 1)
    )
    return value * cosine + partner * (sine * sign)


def head_mask(shape, head):
    lane = lax.broadcasted_iota(jnp.int32, shape, 1)
    return jnp.logical_and(lane >= head * HD, lane < (head + 1) * HD)


def of_head(value, head):
    return jnp.where(head_mask(value.shape, head), value, jnp.zeros_like(value))


def allowed_keys(start, first_row, shape):
    row = lax.broadcasted_iota(jnp.int32, shape, 0) + first_row
    column = lax.broadcasted_iota(jnp.int32, shape, 1)
    return jnp.logical_and(column >= start, column <= row)


def forward_steps(r, lean=False):
    tokens, width = r.x.shape
    heads = r.att.shape[1] // HD

    def norm(i):
        rows = tile(i, 64)
        value = r.x[rows].astype(F32)
        mean = jnp.sum(value, axis=1, keepdims=True) / width
        variance = jnp.sum(value * value, axis=1, keepdims=True) / width - mean * mean
        inverse_std = lax.rsqrt(variance + EPS)
        r.mean[rows] = mean
        r.inverse_std[rows] = inverse_std
        r.normed[rows] = ((value - mean) * inverse_std * r.gain[...] + r.shift[...]).astype(BF16)

    def project(i):
        rows = tile(i)
        normed = r.normed[rows]
        for c in range(3):
            value = dot(normed, r.w_qkv[c]) + r.b_qkv[c : c + 1]
            if c < 2:
                value = turn_heads(value, r.cosine[rows], r.sine[rows], 1.0)
            r.qkv[c, rows] = value.astype(BF16)

    def attend(i):
        rows = pl.ds(i * TILE, TILE)
        keys = (i + 1) * TILE
        query, key, value = r.qkv[0, rows], r.qkv[1, :keys], r.qkv[2, :keys]
        allowed = allowed_keys(r.start[rows], i * TILE, (TILE, keys))
        total = jnp.zeros((TILE, heads * HD), F32)
        for head in range(heads):
            scores = dot(of_head(query, head), key, ((1,), (1,))) * HD ** (-0.5)
            sums = jnp.sum(jnp.where(allowed, jnp.exp(scores), 0.0), axis=1, keepdims=True)
            log_total = jnp.log(sums)
            r.lse[head, rows] = log_total
            probs = jnp.where(allowed, jnp.exp(scores - log_total), 0.0).astype(BF16)
            total += dot(probs, of_head(value, head))
        r.att[rows] = total.astype(BF16)

    def up(i):
        rows = tile(i)
        value = dot(r.normed[rows], r.w_up[...]) + r.b_up[...]
        inner = jnp.tanh(GELU_C * (value + GELU_K * value * value * value))
        r.hidden[rows] = (0.5 * value * (1.0 + inner)).astype(BF16)
        r.slope[rows] = 0.5 * (1.0 + inner) + 0.5 * value * (1.0 - inner * inner) * GELU_C * (
            1.0 + 3.0 * GELU_K * value * value
        )

    def down(i):
        rows = tile(i)
        r.partial[rows] = (
            dot(r.att[rows], r.w_out[...]) + dot(r.hidden[rows], r.w_down[...])
        ).astype(BF16)

    count = tokens // TILE
    return norm, project, attend, up, down, count


def each(count, step):
    lax.fori_loop(0, count, lambda i, _: (step(i), 0)[1], 0)


def some(begin, end, step):
    lax.fori_loop(begin, end, lambda i, _: (step(i), 0)[1], 0)


def run_forward(r):
    norm, project, attend, up, down, count = forward_steps(r)
    each(r.x.shape[0] // 64, norm)
    each(count, project)
    for i in range(count):
        attend(i)
    each(count, up)
    each(count, down)


def backward_steps(r):
    tokens, width = r.g.shape
    heads = r.att.shape[1] // HD
    count = tokens // TILE

    def start():
        r.d_b_up[...] = jnp.zeros_like(r.d_b_up)
        r.d_b_qkv[...] = jnp.zeros_like(r.d_b_qkv)
        r.d_kv[...] = jnp.zeros_like(r.d_kv)

    def open_branches(i):
        rows = tile(i)
        g = r.g[rows]
        d_pre = dot(g, r.w_down[...], ((1,), (1,))) * r.slope[rows]
        r.d_b_up[...] += jnp.sum(d_pre, axis=0, keepdims=True)
        r.d_hidden[rows] = d_pre.astype(BF16)
        r.d_att[rows] = dot(g, r.w_out[...], ((1,), (1,))).astype(BF16)

    def grad_rows(i):
        columns = tile(i)
        g = r.g[:, columns]
        r.d_w_down[:, columns] = dot(r.hidden[...], g, ((0,), (0,))).astype(BF16)
        r.d_w_out[:, columns] = dot(r.att[...], g, ((0,), (0,))).astype(BF16)

    def grad_up(i):
        rows = tile(i)
        r.d_w_up[rows] = dot(r.normed[:, rows], r.d_hidden[...], ((0,), (0,))).astype(BF16)

    def attend(i):
        rows = pl.ds(i * TILE, TILE)
        keys = (i + 1) * TILE
        query, key, value = r.qkv[0, rows], r.qkv[1, :keys], r.qkv[2, :keys]
        d_att = r.d_att[rows]
        product = d_att.astype(F32) * r.att[rows].astype(F32)
        allowed = allowed_keys(r.start[rows], i * TILE, (TILE, keys))
        d_query = jnp.zeros((TILE, heads * HD), F32)
        d_key = jnp.zeros((keys, heads * HD), F32)
        d_value = jnp.zeros((keys, heads * HD), F32)
        for head in range(heads):
            q_head, d_head = of_head(query, head), of_head(d_att, head)
            scores = dot(q_head, key, ((1,), (1,))) * HD ** (-0.5)
            probs = jnp.where(allowed, jnp.exp(scores - r.lse[head, rows]), 0.0)
            delta = jnp.sum(of_head(product, head), axis=1, keepdims=True)
            d_probs = dot(d_head, value, ((1,), (1,)))
            d_scores = (probs * (d_probs - delta) * HD ** (-0.5)).astype(BF16)
            d_query += dot(d_scores, of_head(key, head))
            d_key += dot(d_scores, q_head, ((0,), (0,)))
            d_value += dot(probs.astype(BF16), d_head, ((0,), (0,)))
        r.d_query[rows] = d_query
        r.d_kv[0, :keys] += d_key
        r.d_kv[1, :keys] += d_value

    def unrotate(i):
        rows = tile(i)
        cosine, sine = r.cosine[rows], r.sine[rows]
        parts = (
            turn_heads(r.d_query[rows], cosine, sine, -1.0),
            turn_heads(r.d_kv[0, rows], cosine, sine, -1.0),
            r.d_kv[1, rows],
        )
        for c, value in enumerate(parts):
            r.d_b_qkv[c : c + 1] += jnp.sum(value, axis=0, keepdims=True)
            r.d_qkv[c, rows] = value.astype(BF16)

    def grad_qkv(i):
        rows = tile(i)
        normed = r.normed[:, rows]
        for c in range(3):
            r.d_w_qkv[c, rows] = dot(normed, r.d_qkv[c], ((0,), (0,))).astype(BF16)

    def close(i):
        rows = tile(i)
        total = dot(r.d_hidden[rows], r.w_up[...], ((1,), (1,)))
        for c in range(3):
            total += dot(r.d_qkv[c, rows], r.w_qkv[c], ((1,), (1,)))
        r.partial[rows] = total.astype(BF16)

    return start, open_branches, grad_rows, grad_up, attend, unrotate, grad_qkv, close, count


def run_backward(r):
    start, open_branches, grad_rows, grad_up, attend, unrotate, grad_qkv, close, count = backward_steps(r)
    wide = r.g.shape[1] // TILE
    start()
    each(count, open_branches)
    each(wide, grad_rows)
    each(wide, grad_up)
    for i in range(count):
        attend(i)
    each(count, unrotate)
    each(wide, grad_qkv)
    each(count, close)


class Refs:
    def __init__(self, **refs):
        self.__dict__.update(refs)


WEIGHTS = ("w_qkv", "w_out", "w_up", "w_down", B_QKV, B_UP, GAIN, SHIFT)
TABLES = (N_START, COSINE, SINE)
SAVED = (NORMED, QKV, ATT, LSE, SLOPE, HIDDEN)


def saved_shapes(tokens, width, e, f):
    return {
        NORMED: ((tokens, width), BF16),
        QKV: ((3, tokens, e), BF16),
        ATT: ((tokens, e), BF16),
        LSE: ((e // HD, tokens, 1), F32),
        SLOPE: ((tokens, f), F32),
        HIDDEN: ((tokens, f), BF16),
    }


def scratch_shapes_back(tokens, e, f):
    return {
        "d_hidden": ((tokens, f), BF16),
        "d_att": ((tokens, e), BF16),
        "d_query": ((tokens, e), F32),
        "d_kv": ((2, tokens, e), F32),
        "d_qkv": ((3, tokens, e), BF16),
    }


def grad_shapes(width, e, f):
    return {
        "d_w_qkv": ((3, width, e), BF16),
        "d_w_out": ((e, width), BF16),
        "d_w_up": ((width, f), BF16),
        "d_w_down": ((f, width), BF16),
        "d_b_qkv": ((3, e), F32),
        "d_b_up": ((1, f), F32),
    }


def remote_call(body, name, key, inputs, outputs, scratch, copies, in_hbm=(), out_hbm=()):
    vmem = pl.BlockSpec(memory_space=pltpu.VMEM)
    hbm = pl.BlockSpec(memory_space=pl.ANY)
    keys = list(inputs) + list(outputs) + list(scratch) + ["free_sem", "local_sems", "send_sems", "recv_sems"]

    def kernel(*refs):
        body(Refs(**dict(zip(keys, refs))))

    outs = pl.pallas_call(
        kernel,
        out_shape=tuple(jax.ShapeDtypeStruct(shape, kind) for shape, kind in outputs.values()),
        in_specs=[hbm if each_in in in_hbm else vmem for each_in in inputs],
        out_specs=tuple(hbm if each_out in out_hbm else vmem for each_out in outputs),
        scratch_shapes=[pltpu.VMEM(shape, kind) for shape, kind in scratch.values()]
        + [
            pltpu.SemaphoreType.REGULAR,
            pltpu.SemaphoreType.DMA((32,)),
            pltpu.SemaphoreType.DMA((copies,)),
            pltpu.SemaphoreType.DMA((copies,)),
        ],
        compiler_params=pltpu.CompilerParams(
            collective_id=key, has_side_effects=True, vmem_limit_bytes=63 << 20
        ),
        name=name,
    )(*inputs.values())
    return dict(zip(outputs, outs))


def weight_scratch(turn):
    shapes = {W + name: (turn.turned_shape(name), BF16) for name in NAMES}
    width = 4 * turn.d
    return shapes | {
        B_QKV: ((3, turn.e), F32),
        B_UP: ((1, turn.f), F32),
        GAIN: ((1, width), F32),
        SHIFT: ((1, width), F32),
    }


def scatter_dict(rows, part):
    return {
        "theirs": ((2, 4 * rows, part), BF16),
        "chip": ((2, 4 * rows, part), BF16),
        "from_y": ((4 * rows, part), BF16),
        "from_far": ((3, rows, part), BF16),
    }


def back_dict(rows, part):
    return {
        "d_normed": ((rows, part), F32),
        "row_out": ((GROUPS, 8, 128), F32),
        "row_in": ((GROUPS, 3, 8, 128), F32),
    }


def scatter_of(w, r, partial, rows, part):
    return Scatter(w, partial, (r.theirs, r.chip, r.from_y, r.from_far), rows, part)


def small_params(w, r, layer):
    part = r.gain.shape[1] // 4
    slab = part // 4
    for t in range(4):
        for c in range(4):
            lanes = slice(t * part + c * slab, t * part + (c + 1) * slab)
            r.gain[:, lanes] = r.vectors[layer, c, t, 1:2]
            r.shift[:, lanes] = r.vectors[layer, c, t, 2:3]
    r.b_qkv[...] = r.vectors[layer, w.c, w.t, 3:6]
    for i in range(r.b_up.shape[1] // slab):
        r.b_up[:, i * slab : (i + 1) * slab] = r.vectors[layer, w.c, w.t, 6 + i : 7 + i]


def own_bias(w, r, layer):
    return jnp.concatenate([r.vectors[layer, c, w.t, 0:1] for c in range(4)], axis=1)


def own_gain(w, r, layer):
    return jnp.concatenate([r.vectors[layer, c, w.t, 1:2] for c in range(4)], axis=1)


FIRST = (OUT, QKV, UP, DOWN)
HALVES = {OUT: (None,), QKV: (None,), UP: (0, 1), DOWN: (0, 1)}


def pull(*generators, times=1):
    for _ in range(times):
        for generator in generators:
            next(generator, None)


def first_body(turn, rows, part, r):
    w = Wire(r.send_sems, r.recv_sems)
    s = w.section
    peers = everyone(w)
    w.greet(peers)
    shards = {name: getattr(r, SHARD + name) for name in NAMES}
    mine = {name: getattr(r, TURNED + name).at[s] for name in NAMES}
    bounce = {name: getattr(r, BOUNCE + name) for name in NAMES}
    swap = w.send(r.own.at[1 - s], r.other, w.across)
    r.vectors[s, w.c, w.t] = r.vector[...]
    told = [w.send(r.vector, r.vectors.at[s, w.c, w.t], peer) for peer in peers]
    local, far, across, puts = {}, {}, {name: [] for name in NAMES}, {}

    def send_along(name):
        for half in HALVES[name]:
            for step, place in w.others:
                far[name, step, half] = w.send(
                    turn.shard(name, shards[name], place, half),
                    turn.turned(name, mine[name], w.c, half),
                    {CTX: place},
                )
                yield

    def pass_across(name):
        for half in HALVES[name]:
            for step in (1, 3, 2):
                far[name, step, half].wait_recv()
                spot = turn.turned(name, mine[name], (w.c + 4 - step) % 4, half)
                across[name].append(w.send(spot, spot, w.across))
                yield

    def fetch(name):
        for copy in across[name]:
            copy.wait_recv()
        puts[name].wait()
        i = FIRST.index(name)
        copy = pltpu.make_async_copy(
            getattr(r, TURNED + name).at[0], getattr(r, W + name), r.local_sems.at[8 + i]
        )
        copy.start()
        return copy

    sending = itertools.chain(*(send_along(name) for name in FIRST))
    passing = itertools.chain(*(pass_across(name) for name in FIRST))
    pull(sending, times=6)
    for i, name in enumerate(FIRST):
        own_piece = turn.shard(name, shards[name], w.c)
        across[name].append(w.send(own_piece, turn.turned(name, mine[name], w.c), w.across))
        local[name] = pltpu.make_async_copy(own_piece, bounce[name], r.local_sems.at[i])
        local[name].start()
    swap.wait_recv()
    mine_block = r.own[s]
    r.x_block[...] = jnp.where(s == 0, mine_block, r.other[...])
    r.g_block[...] = jnp.where(s == 0, r.other[...], mine_block)
    half = rows // GROUPS
    gather_x = DirectGather(w, r.x, rows, part)
    for group in range(GROUPS):
        gather_x.region(w.c, w.t, group)[...] = r.x_block[group * half : (group + 1) * half]
        gather_x.begin(group)
    for i, name in enumerate(FIRST):
        local[name].wait()
        puts[name] = pltpu.make_async_copy(
            bounce[name], turn.turned(name, mine[name], w.c), r.local_sems.at[4 + i]
        )
        puts[name].start()
    pull(passing, times=6)
    pull(sending, times=3)
    for i, _ in enumerate(gather_x.steps()):
        if i == 5:
            pull(sending, times=3)
    for copy in told:
        copy.wait_recv()
    small_params(w, r, 0)
    norm, project, attend, up, down, count = forward_steps(r)
    each(4 * rows // 64, norm)
    ready = [fetch(OUT), fetch(QKV)]
    for copy in ready:
        copy.wait()
    each(count, project)
    pull(passing, times=3)
    pull(sending, times=3)
    attend(0)
    attend(1)
    pull(passing, times=3)
    pull(sending, times=3)
    for i in range(2, count):
        attend(i)
    fetch(UP).wait()
    each(count, up)
    for _ in passing:
        pass
    fetch(DOWN).wait()
    each(count, down)
    scatter = scatter_of(w, r, r.partial, rows, part)
    scatter.begin()
    scatter.run()
    gather = Gather(w, r.x1, rows, part)
    bias = own_bias(w, r, 0)
    for group in range(GROUPS):
        own = slice(group * half, (group + 1) * half)
        value = (r.x_block[own].astype(F32) + scatter.total(group) + bias).astype(BF16)
        r.act[own] = value
        gather.region(w.c, w.t, group)[...] = value
        gather.begin(group)
    for _ in gather.steps():
        pass
    w.drain()


def first(own, vector, tables, shards):
    _, rows, part = own.shape
    turn = Turn(shards[QKV].shape[1], shards[QKV].shape[2] // 4, shards[UP].shape[1] // 4)
    tokens, width = 4 * rows, 4 * part
    full = ((tokens, width), BF16)
    block = ((rows, part), BF16)
    outputs = {TURNED + name: ((2,) + turn.turned_shape(name), BF16) for name in NAMES}
    outputs |= {X1: full, X_BLOCK: block, G_BLOCK: block, ACT: block}
    outputs |= {VECTORS: ((2, 4, 4) + vector.shape, F32)}
    outputs |= saved_shapes(tokens, width, turn.e, turn.f)
    outputs |= {MEAN: ((tokens, 1), F32), INVERSE_STD: ((tokens, 1), F32)}
    scratch = {BOUNCE + name: (turn.piece_shape(name), BF16) for name in NAMES}
    scratch |= {"other": block, X: full, PARTIAL: full}
    scratch |= weight_scratch(turn) | scatter_dict(rows, part)
    return remote_call(
        functools.partial(first_body, turn, rows, part),
        "first",
        START,
        {"own": own, VECTOR: vector}
        | tables
        | {SHARD + name: shards[name] for name in NAMES},
        outputs,
        scratch,
        320,
        in_hbm=[SHARD + name for name in NAMES],
        out_hbm=[TURNED + name for name in NAMES],
    )


def middle_body(turn, rows, part, r):
    w = Wire(r.send_sems, r.recv_sems)
    loads = {}
    for i, name in enumerate(FIRST):
        loads[name] = pltpu.make_async_copy(
            getattr(r, TURNED + name).at[1], getattr(r, W + name), r.local_sems.at[i]
        )
        loads[name].start()
    w.greet(neighbours(w) + [diagonal(w)])
    half = rows // GROUPS
    gather_g = Gather(w, r.g, rows, part, skew=0)
    for group in range(GROUPS):
        gather_g.region(w.c, w.t, group)[...] = r.g_block[group * half : (group + 1) * half]
        gather_g.begin(group)
    arriving = gather_g.steps()
    small_params(w, r, 1)
    norm, project, attend, up, down, count = forward_steps(r)
    each(4 * rows // 64, norm)
    pull(arriving, times=4)
    loads[QKV].wait()
    each(count, project)
    attend(0)
    pull(arriving, times=4)
    attend(1)
    attend(2)
    pull(arriving, times=4)
    attend(3)
    pull(arriving, times=6)
    loads[UP].wait()
    each(count, up)
    loads[DOWN].wait()
    loads[OUT].wait()
    each(count, down)
    for _ in arriving:
        pass
    b = Refs(**dict(r.__dict__, partial=r.partial_g))
    start, open_branches, grad_rows, grad_up, attend_back, unrotate, grad_qkv, close, _ = (
        backward_steps(b)
    )
    start()
    each(count, open_branches)
    for i in range(count):
        attend_back(i)
    each(count, unrotate)
    each(count, close)

    def leftover():
        wide = 4 * part // TILE
        for step, times in ((grad_rows, wide), (grad_up, wide), (grad_qkv, wide)):
            for i in range(0, times, 2):
                some(i, i + 2, step)
                yield

    fill = leftover()
    scatter = scatter_of(w, r, r.partial_g, rows, part)
    scatter.begin()
    for i, _ in enumerate(scatter.steps()):
        if i % 2 == 1:
            pull(fill)
    gather = Gather(w, r.g1, rows, part)
    r.mean_block[...] = r.mean[pl.ds(pl.multiple_of(w.c * rows, rows), rows)]
    r.std_block[...] = r.inverse_std[pl.ds(pl.multiple_of(w.c * rows, rows), rows)]
    r.gain_block[...] = own_gain(w, r, 1)

    def done(group):
        gather.region(w.c, w.t, group)[...] = r.grad[group * half : (group + 1) * half]
        gather.begin(group)

    norm_back(
        w,
        scatter,
        (r.g_block, r.act, r.mean_block, r.std_block, r.gain_block),
        (r.d_normed, r.row_out, r.row_in),
        rows,
        part,
        r.grad,
        r.sums,
        done,
        fill,
    )
    for _ in gather.steps():
        pull(fill)
    for _ in fill:
        pass
    slab = part // 4
    columns = pl.ds(pl.multiple_of(w.t * part + w.c * slab, 128), slab)
    r.d_b_out[...] = jnp.sum(r.g[:, columns].astype(F32), axis=0, keepdims=True)
    w.drain()


def middle(made, tables, turn, rows, part):
    tokens, width = 4 * rows, 4 * part
    full = ((tokens, width), BF16)
    inputs = {X: made[X1], ACT: made[ACT], G_BLOCK: made[G_BLOCK]}
    inputs |= {VECTORS: made[VECTORS]} | tables
    inputs |= {TURNED + name: made[TURNED + name] for name in NAMES}
    outputs = grad_shapes(width, turn.e, turn.f)
    outputs |= {"d_b_out": ((1, part // 4), F32), PARTIAL: full}
    outputs |= {GRAD: ((rows, part), BF16), G1: full, SUMS: ((8, part), F32)}
    scratch = saved_shapes(tokens, width, turn.e, turn.f)
    scratch |= {MEAN: ((tokens, 1), F32), INVERSE_STD: ((tokens, 1), F32)}
    scratch |= scratch_shapes_back(tokens, turn.e, turn.f) | {"partial_g": full, G: full}
    scratch |= {MEAN_BLOCK: ((rows, 1), F32), STD_BLOCK: ((rows, 1), F32)}
    scratch |= {GAIN_BLOCK: ((1, part), F32)}
    scratch |= weight_scratch(turn) | scatter_dict(rows, part) | back_dict(rows, part)
    return remote_call(
        functools.partial(middle_body, turn, rows, part),
        "middle",
        BWD,
        inputs,
        outputs,
        scratch,
        200,
        in_hbm=[TURNED + name for name in NAMES],
    )


LATER = (DOWN, OUT, UP, QKV)


def last_body(turn, rows, part, r):
    w = Wire(r.send_sems, r.recv_sems)
    s = w.section
    half = rows // GROUPS
    loads = {}
    for i, name in enumerate(FIRST):
        loads[name] = pltpu.make_async_copy(
            getattr(r, TURNED + name).at[0], getattr(r, W + name), r.local_sems.at[i]
        )
        loads[name].start()
    moves = [(ds, dc) for ds in (0, 1) for dc in range(4) if (ds, dc) != (0, 0)]

    def away(ds, dc):
        return {SECTION: (s + ds) % 2, CTX: (w.c + dc) % 4}

    w.greet([away(*move) for move in moves] + [w.beside, w.core, diagonal(w)])
    places = [(2, w.c_far), (1, w.c_up), (3, w.c_down), (0, w.c)]
    grads0 = {name: getattr(r, D_W + name) for name in NAMES}
    grads1 = {name: getattr(r, ONE + name) for name in NAMES}
    arrived = {name: getattr(r, ARRIVED + name) for name in NAMES}
    outs = {name: getattr(r, HOME + name) for name in NAMES}
    kept = {name: getattr(r, KEPT + name) for name in NAMES}
    across, home, keeps = {}, {}, {}

    def send_across(name):
        for step, c in places:
            across[name, step] = w.send_one_of(
                s == 0,
                turn.turned(name, grads1[name], c),
                turn.turned(name, grads0[name], c),
                turn.turned(name, arrived[name], c),
                w.across,
            )

    def keep(name, c, slot):
        copy = pltpu.make_async_copy(
            turn.turned(name, grads1[name], c), kept[name].at[slot], r.local_sems.at[8 + 2 * NAMES.index(name) + slot]
        )
        copy.start()
        return copy

    def settle():
        for name in LATER:
            waiting = keep(name, places[0][1], 0)
            for i, (step, c) in enumerate(places):
                waiting.wait()
                if i < 3:
                    waiting = keep(name, places[i + 1][1], (i + 1) % 2)
                across[name, step].wait_recv()
                theirs = turn.turned(name, arrived[name], c)
                mine = jnp.where(
                    s == 0,
                    turn.turned(name, grads0[name], c)[...].astype(F32),
                    kept[name][i % 2].astype(F32),
                )
                theirs[...] = (mine + theirs[...].astype(F32)).astype(BF16)
                spot = turn.shard(name, outs[name], w.c)
                if step:
                    home[name, step] = w.send(theirs, spot, {CTX: c})
                else:
                    home[name, 0] = pltpu.make_async_copy(
                        theirs, spot, r.local_sems.at[16 + NAMES.index(name)]
                    )
                    home[name, 0].start()
                yield

    start, open_branches, grad_rows, grad_up, attend_back, unrotate, grad_qkv, close, count = (
        backward_steps(r)
    )
    wide = 4 * part // TILE
    start()
    other = scatter_of(w, r, r.partial_x, rows, part)
    other.begin()
    summing = other.steps()
    for i in range(0, wide, 2):
        some(i, i + 2, grad_rows)
        pull(summing, times=2)
    send_across(DOWN)
    send_across(OUT)
    loads[DOWN].wait()
    loads[OUT].wait()
    for i in range(count):
        some(i, i + 1, open_branches)
        pull(summing)
    for i in range(0, wide, 2):
        some(i, i + 2, grad_up)
        pull(summing)
    send_across(UP)
    settling = settle()
    for _ in summing:
        pass
    for i in range(count):
        attend_back(i)
        pull(settling)
    bias = own_bias(w, r, 1)
    r.all_acts[0] = r.act[...]
    for group in range(GROUPS):
        own = slice(group * half, (group + 1) * half)
        value = r.act[own].astype(F32) + other.total(group) + bias
        r.all_acts[1, own] = value.astype(BF16)
    r.acts[s] = r.all_acts[s]
    pairs = [w.send(r.all_acts.at[1 - s], r.acts.at[s], w.across)]
    each(count, unrotate)
    each(wide, grad_qkv)
    send_across(QKV)
    pull(settling)
    loads[QKV].wait()
    loads[UP].wait()
    each(count, close)
    slab = part // 4
    columns = pl.ds(pl.multiple_of(w.t * part + w.c * slab, 128), slab)
    n_up = r.d_b_up.shape[1] // slab
    r.small[0, 0:3] = r.d_b_qkv[...]
    r.small[1, 0:3] = r.one_b_qkv[...]
    for i in range(n_up):
        lanes = slice(i * slab, (i + 1) * slab)
        r.small[0, 3 + i : 4 + i] = r.d_b_up[:, lanes]
        r.small[1, 3 + i : 4 + i] = r.one_b_up[:, lanes]
    r.small[0, 3 + n_up : 4 + n_up] = jnp.sum(r.g[:, columns].astype(F32), axis=0, keepdims=True)
    r.small[1, 3 + n_up : 4 + n_up] = r.one_b_out[...]
    small_copy = w.send(r.small.at[1 - s], r.small_in, w.across)
    w.flush(other.sent)
    w.meet(r.free_sem, neighbours(w))
    scatter = scatter_of(w, r, r.partial, rows, part)
    scatter.begin()
    for i, _ in enumerate(scatter.steps()):
        if i % 4 == 3:
            pull(settling)
    r.mean_block[...] = r.mean[pl.ds(pl.multiple_of(w.c * rows, rows), rows)]
    r.std_block[...] = r.inverse_std[pl.ds(pl.multiple_of(w.c * rows, rows), rows)]
    r.gain_block[...] = own_gain(w, r, 0)
    norm_back(
        w,
        scatter,
        (r.grad1, r.x_block, r.mean_block, r.std_block, r.gain_block),
        (r.d_normed, r.row_out, r.row_in),
        rows,
        part,
        r.all_grads.at[0],
        r.sums0,
        lambda group: None,
        settling,
    )
    r.all_grads[1] = r.grad1[...]
    r.grads[s] = r.all_grads[s]
    pairs.append(w.send(r.all_grads.at[1 - s], r.grads.at[s], w.across))
    for layer, sums in ((0, r.sums0), (1, r.sums1)):
        for c in range(4):
            r.norm_out[layer, c] = sums[:, c * slab : (c + 1) * slab]
    told = [
        w.send(r.norm_out.at[(s + ds) % 2, (w.c + dc) % 4], r.norm_in.at[slot], away(ds, dc))
        for slot, (ds, dc) in enumerate(moves)
    ]
    for _ in settling:
        pass
    small_copy.wait_recv()
    r.small_sum[...] = r.small[s] + r.small_in[...]
    total = r.norm_out[s, w.c]
    for slot, copy in enumerate(told):
        copy.wait_recv()
        total += r.norm_in[slot]
    r.norm_sum[...] = total
    for name in LATER:
        home[name, 0].wait()
        for step in (1, 3, 2):
            home[name, step].wait_recv()
    for copy in pairs:
        copy.wait_recv()
    w.drain()


def last(made, mid, tables, turn, rows, part):
    tokens, width = 4 * rows, 4 * part
    full = ((tokens, width), BF16)
    e, f = 4 * turn.e, 4 * turn.f
    homes = {
        QKV: (3, turn.d, e),
        OUT: (e, turn.d),
        UP: (turn.d, f),
        DOWN: (f, turn.d),
    }
    inputs = {G: mid[G1], "grad1": mid[GRAD], "partial_x": mid[PARTIAL], "sums1": mid[SUMS]}
    inputs |= {key: made[key] for key in SAVED + (MEAN, INVERSE_STD, VECTORS, ACT, X_BLOCK)}
    inputs |= {ONE + name: mid[D_W + name] for name in NAMES}
    inputs |= {ONE + name: mid["d_" + name] for name in (B_QKV, B_UP, "b_out")}
    inputs |= {TURNED + name: made[TURNED + name] for name in NAMES} | tables
    pairs = ((2, rows, part), BF16)
    outputs = {HOME + name: (homes[name], BF16) for name in NAMES}
    outputs |= {ACTS: pairs, GRADS: pairs}
    outputs |= {SMALL_SUM: ((8, part // 4), F32), NORM_SUM: ((8, part // 4), F32)}
    scratch = grad_shapes(width, turn.e, turn.f) | {PARTIAL: full}
    scratch |= {ARRIVED + name: (turn.turned_shape(name), BF16) for name in NAMES}
    scratch |= {KEPT + name: ((2,) + turn.piece_shape(name), BF16) for name in NAMES}
    scratch |= scratch_shapes_back(tokens, turn.e, turn.f)
    scratch |= {W + name: (turn.turned_shape(name), BF16) for name in NAMES}
    scratch |= scatter_dict(rows, part) | back_dict(rows, part)
    scratch |= {
        MEAN_BLOCK: ((rows, 1), F32),
        STD_BLOCK: ((rows, 1), F32),
        GAIN_BLOCK: ((1, part), F32),
        "small": ((2, 8, part // 4), F32),
        "small_in": ((8, part // 4), F32),
        "sums0": ((8, part), F32),
        "norm_out": ((2, 4, 8, part // 4), F32),
        "norm_in": ((7, 8, part // 4), F32),
        "all_acts": pairs,
        "all_grads": pairs,
    }
    return remote_call(
        functools.partial(last_body, turn, rows, part),
        "last",
        LAST,
        inputs,
        outputs,
        scratch,
        140,
        in_hbm=[TURNED + name for name in NAMES] + [ONE + name for name in NAMES],
        out_hbm=[HOME + name for name in NAMES],
    )


def shards(
    boundary,
    doc_ids,
    qkv_weight,
    qkv_bias,
    out_weight,
    out_bias,
    fc1_weight,
    fc1_bias,
    fc2_weight,
    fc2_bias,
    norm_gain,
    norm_shift,
):
    section = lax.axis_index(SECTION)
    rows, part = boundary.shape[2:]
    slab = out_bias.shape[1]
    n_up = fc1_bias.shape[1] // slab
    tables = doc_tables(
        lax.dynamic_index_in_dim(doc_ids, section, 0, keepdims=False), slab // HD
    )
    vector = jnp.concatenate(
        [
            out_bias.astype(F32) + fc2_bias.astype(F32),
            norm_gain.astype(F32),
            norm_shift.astype(F32),
            qkv_bias[0].astype(F32),
            fc1_bias.astype(F32).reshape(n_up, slab),
        ]
    )
    vector = jnp.pad(vector, ((0, 16 - vector.shape[0]), (0, 0)))
    shard_of = {QKV: qkv_weight[0], OUT: out_weight[0], UP: fc1_weight[0], DOWN: fc2_weight[0]}
    turn = Turn(shard_of[QKV].shape[1], slab, shard_of[UP].shape[1] // 4)
    made = first(boundary[0], vector, tables, shard_of)
    mid = middle(made, tables, turn, rows, part)
    out = last(made, mid, tables, turn, rows, part)
    small, norms = out[SMALL_SUM], out[NORM_SUM]
    bias_out = small[3 + n_up][None]
    home = {name: out[HOME + name].astype(F32)[None] for name in NAMES}
    return (
        out[ACTS][None],
        out[GRADS][None],
        home[QKV],
        small[None, :3],
        home[OUT],
        bias_out,
        home[UP],
        small[3 : 3 + n_up].reshape(1, -1),
        home[DOWN],
        bias_out,
        norms[0:1],
        norms[1:2],
    )


def from_behind(value, axis, steps):
    count = lax.axis_size(axis)
    leading, last = (max(0, -steps), min(count, count - steps))
    return lax.ppermute(value, axis, [(source, source + steps) for source in range(leading, last)])


def gelu(value):
    inner = jnp.tanh(GELU_C * (value + GELU_K * value * value * value))
    return 0.5 * value * (1.0 + inner)


def gelu_slope(value):
    inner = jnp.tanh(GELU_C * (value + GELU_K * value * value * value))
    return 0.5 * (1.0 + inner) + 0.5 * value * (1.0 - inner * inner) * GELU_C * (
        1.0 + 3.0 * GELU_K * value * value
    )


def local_layout(ids_full, ctx_index, tokens):
    length = ids_full.shape[0]
    local_ids = lax.dynamic_slice_in_dim(ids_full, ctx_index * tokens, tokens)
    start = jnp.sum((ids_full[None, :] < local_ids[:, None]).astype(jnp.int32), axis=1)
    query_at = ctx_index * tokens + jnp.arange(tokens, dtype=jnp.int32)
    key_at = jnp.arange(length, dtype=jnp.int32)
    allowed = (key_at[None, :] <= query_at[:, None]) & (ids_full[None, :] == local_ids[:, None])
    return (query_at - start, allowed)


def score_block(query, keys):
    return jnp.einsum(SCORES_EQ, query, keys, preferred_element_type=jnp.float32) * HD ** (
        -0.5
    )


def forward_layer(layer_in, ids_full, params, ctx_index):
    w_qkv, b_qkv, w_out, b_out, w_up, b_up, w_down, b_down, gain, shift = params
    tokens = layer_in.shape[0]
    heads = w_qkv.shape[2] // HD
    wide_in = layer_in.astype(jnp.float32)
    row_sums = lax.psum((jnp.sum(wide_in, axis=1), jnp.sum(wide_in * wide_in, axis=1)), TP)
    row_mean = row_sums[0] / D
    variance = row_sums[1] / D - row_mean * row_mean
    inverse_std = lax.rsqrt(variance + EPS)
    centered = (wide_in - row_mean[:, None]) * inverse_std[:, None]
    normed_part = (centered * gain.astype(jnp.float32) + shift.astype(jnp.float32)).astype(
        jnp.bfloat16
    )
    normed = lax.all_gather(normed_part, TP, axis=1, tiled=True)
    positions, allowed = local_layout(ids_full, ctx_index, tokens)
    cosine, sine = rope_tables(positions)
    projected = (
        jnp.einsum("td,cde->cte", normed, w_qkv, preferred_element_type=jnp.float32)
        + b_qkv.astype(jnp.float32)[:, None, :]
    )
    query = rotate(projected[0].reshape(tokens, heads, HD), cosine, sine, 1.0).astype(jnp.bfloat16)
    key_rot = rotate(projected[1].reshape(tokens, heads, HD), cosine, sine, 1.0).astype(
        jnp.bfloat16
    )
    value_part = projected[2].reshape(tokens, heads, HD).astype(jnp.bfloat16)
    key_all, value_all = (
        lax.all_gather(key_rot, CTX, axis=0, tiled=True),
        lax.all_gather(value_part, CTX, axis=0, tiled=True),
    )
    scores = score_block(query, key_all)
    totals = jnp.sum(jnp.where(allowed[None], jnp.exp(scores), 0.0), axis=2)
    log_total = jnp.log(totals)
    probs = jnp.where(allowed[None], jnp.exp(scores - log_total[:, :, None]), 0.0).astype(
        jnp.bfloat16
    )
    attended = (
        jnp.einsum(HEADS_EQ, probs, value_all, preferred_element_type=jnp.float32)
        .astype(jnp.bfloat16)
        .reshape(tokens, heads * HD)
    )
    hidden_pre = jnp.dot(normed, w_up, preferred_element_type=jnp.float32) + b_up.astype(
        jnp.float32
    )
    hidden = gelu(hidden_pre).astype(jnp.bfloat16)
    summands = jnp.dot(attended, w_out, preferred_element_type=jnp.float32) + jnp.dot(
        hidden, w_down, preferred_element_type=jnp.float32
    )
    mixed = lax.psum_scatter(summands, TP, scatter_dimension=1, tiled=True)
    layer_out = (wide_in + mixed + b_out.astype(jnp.float32) + b_down.astype(jnp.float32)).astype(
        jnp.bfloat16
    )
    kept = (key_rot, value_part)
    return (
        layer_out,
        (centered, inverse_std, normed, query, kept, attended, log_total, hidden_pre, hidden),
    )


def backward_layer(incoming, saved, ids_full, params, ctx_index):
    w_qkv, b_qkv, w_out, b_out, w_up, b_up, w_down, b_down, gain, shift = params
    centered, inverse_std, normed, query, kept, attended, log_total, hidden_pre, hidden = saved
    tokens = query.shape[0]
    heads = query.shape[1]
    wide_grad = incoming.astype(jnp.float32)
    grad_rows = lax.all_gather(incoming, TP, axis=1, tiled=True)
    grad_out_bias = jnp.sum(wide_grad, axis=0)
    grad_out = jnp.einsum("tk,te->ke", attended, grad_rows, preferred_element_type=jnp.float32)
    d_attended = jnp.einsum(
        "te,ke->tk", grad_rows, w_out, preferred_element_type=jnp.float32
    ).astype(jnp.bfloat16)
    grad_down = jnp.einsum("tf,te->fe", hidden, grad_rows, preferred_element_type=jnp.float32)
    d_pre = jnp.einsum(
        "te,fe->tf", grad_rows, w_down, preferred_element_type=jnp.float32
    ) * gelu_slope(hidden_pre)
    grad_up_bias = jnp.sum(d_pre, axis=0)
    d_hidden = d_pre.astype(jnp.bfloat16)
    grad_up = jnp.einsum("td,tf->df", normed, d_hidden, preferred_element_type=jnp.float32)
    key_all, value_all = (
        lax.all_gather(kept[0], CTX, axis=0, tiled=True),
        lax.all_gather(kept[1], CTX, axis=0, tiled=True),
    )
    positions, allowed = local_layout(ids_full, ctx_index, tokens)
    cosine, sine = rope_tables(positions)
    d_heads = d_attended.reshape(tokens, heads, HD)
    out_heads = attended.reshape(tokens, heads, HD)
    delta = jnp.sum(d_heads.astype(jnp.float32) * out_heads.astype(jnp.float32), axis=2)
    scores = score_block(query, key_all)
    probs = jnp.where(allowed[None], jnp.exp(scores - log_total[:, :, None]), 0.0)
    d_probs = jnp.einsum(SCORES_EQ, d_heads, value_all, preferred_element_type=jnp.float32)
    d_scores = (probs * (d_probs - delta.T[:, :, None]) * HD ** (-0.5)).astype(jnp.bfloat16)
    d_query = jnp.einsum(HEADS_EQ, d_scores, key_all, preferred_element_type=jnp.float32)
    key_terms = jnp.einsum(KEYS_EQ, d_scores, query, preferred_element_type=jnp.float32)
    value_terms = jnp.einsum(
        KEYS_EQ, probs.astype(jnp.bfloat16), d_heads, preferred_element_type=jnp.float32
    )
    d_key, d_value = (
        lax.psum_scatter(
            key_terms.astype(jnp.bfloat16), CTX, scatter_dimension=0, tiled=True
        ).astype(jnp.float32),
        lax.psum_scatter(
            value_terms.astype(jnp.bfloat16), CTX, scatter_dimension=0, tiled=True
        ).astype(jnp.float32),
    )
    d_projected = jnp.stack(
        [rotate(d_query, cosine, sine, -1.0), rotate(d_key, cosine, sine, -1.0), d_value]
    ).reshape(3, tokens, heads * HD)
    grad_qkv_bias = jnp.sum(d_projected, axis=1)
    d_qkv = d_projected.astype(jnp.bfloat16)
    grad_qkv = jnp.einsum("td,cte->cde", normed, d_qkv, preferred_element_type=jnp.float32)
    normed_terms = jnp.einsum("cte,cde->td", d_qkv, w_qkv, preferred_element_type=jnp.float32)
    normed_terms = normed_terms + jnp.einsum(
        "tf,df->td", d_hidden, w_up, preferred_element_type=jnp.float32
    )
    d_normed = lax.psum_scatter(
        normed_terms.astype(jnp.bfloat16), TP, scatter_dimension=1, tiled=True
    ).astype(jnp.float32)
    grad_gain = jnp.sum(d_normed * centered, axis=0)
    grad_shift = jnp.sum(d_normed, axis=0)
    scaled = d_normed * gain.astype(jnp.float32)
    row_terms = lax.psum((jnp.sum(scaled, axis=1), jnp.sum(scaled * centered, axis=1)), TP)
    grad_in = wide_grad + inverse_std[:, None] * (
        scaled - row_terms[0][:, None] / D - centered * (row_terms[1][:, None] / D)
    )
    grads = (
        grad_qkv,
        grad_qkv_bias,
        grad_out,
        grad_out_bias,
        grad_up,
        grad_up_bias,
        grad_down,
        grad_out_bias,
        grad_gain,
        grad_shift,
    )
    return (grad_in.astype(jnp.bfloat16), grads)


def base_shards(
    boundary,
    doc_ids,
    qkv_weight,
    qkv_bias,
    out_weight,
    out_bias,
    fc1_weight,
    fc1_bias,
    fc2_weight,
    fc2_bias,
    norm_gain,
    norm_shift,
):
    section = lax.axis_index(SECTION)
    ctx_index = lax.axis_index(CTX)
    micro = boundary.shape[1]
    tokens = boundary.shape[2]
    width_part = boundary.shape[3]
    params = (
        lax.all_gather(qkv_weight[0], CTX, axis=1, tiled=True),
        lax.all_gather(qkv_bias[0], CTX, axis=1, tiled=True),
        lax.all_gather(out_weight[0], CTX, axis=1, tiled=True),
        lax.all_gather(out_bias[0], CTX, axis=0, tiled=True),
        lax.all_gather(fc1_weight[0], CTX, axis=0, tiled=True),
        lax.all_gather(fc1_bias[0], CTX, axis=0, tiled=True),
        lax.all_gather(fc2_weight[0], CTX, axis=1, tiled=True),
        lax.all_gather(fc2_bias[0], CTX, axis=0, tiled=True),
        lax.all_gather(norm_gain[0], CTX, axis=0, tiled=True),
        lax.all_gather(norm_shift[0], CTX, axis=0, tiled=True),
    )
    inputs = boundary[0]
    ticks = jnp.arange(micro + 1, dtype=jnp.int32)

    def forward_tick(received, tick):
        index = jnp.clip(tick - section, 0, micro - 1)
        first = lax.dynamic_index_in_dim(inputs, index, 0, keepdims=False)
        layer_in = jnp.where(section == 0, first, received)
        ids_full = lax.dynamic_index_in_dim(doc_ids, index, 0, keepdims=False)
        layer_out, saved = forward_layer(layer_in, ids_full, params, ctx_index)
        passed = from_behind(layer_out, SECTION, 1)
        return (passed, (layer_out, saved))

    start_zero = jnp.zeros((tokens, width_part), jnp.bfloat16)
    leftover, (outs_all, saved_all) = lax.scan(forward_tick, start_zero, ticks)
    held = lax.optimization_barrier(
        (
            (
                qkv_weight[0],
                qkv_bias[0],
                out_weight[0],
                out_bias[0],
                fc1_weight[0],
                fc1_bias[0],
                fc2_weight[0],
                fc2_bias[0],
                norm_gain[0],
                norm_shift[0],
            ),
            outs_all,
        )
    )[0]
    back_params = (
        lax.all_gather(held[0], CTX, axis=1, tiled=True),
        lax.all_gather(held[1], CTX, axis=1, tiled=True),
        lax.all_gather(held[2], CTX, axis=1, tiled=True),
        lax.all_gather(held[3], CTX, axis=0, tiled=True),
        lax.all_gather(held[4], CTX, axis=0, tiled=True),
        lax.all_gather(held[5], CTX, axis=0, tiled=True),
        lax.all_gather(held[6], CTX, axis=1, tiled=True),
        lax.all_gather(held[7], CTX, axis=0, tiled=True),
        lax.all_gather(held[8], CTX, axis=0, tiled=True),
        lax.all_gather(held[9], CTX, axis=0, tiled=True),
    )
    zero_grads = tuple((jnp.zeros(weight.shape, jnp.float32) for weight in params))

    def backward_tick(carry, tick):
        received, totals = carry
        raw_index = tick - (1 - section)
        valid = (raw_index >= 0) & (raw_index < micro)
        index = jnp.clip(raw_index, 0, micro - 1)
        cotangent = lax.dynamic_index_in_dim(inputs, index, 0, keepdims=False)
        incoming = jnp.where(section == 1, cotangent, received)
        incoming = jnp.where(valid, incoming, jnp.zeros_like(incoming))
        position_slot = index + section
        saved = jax.tree.map(
            lambda stacked: lax.dynamic_index_in_dim(stacked, position_slot, 0, keepdims=False),
            saved_all,
        )
        ids_full = lax.dynamic_index_in_dim(doc_ids, index, 0, keepdims=False)
        grad_in, terms = backward_layer(incoming, saved, ids_full, back_params, ctx_index)
        totals = tuple((total + term for total, term in zip(totals, terms)))
        passed = from_behind(grad_in, SECTION, -1)
        return ((passed, totals), grad_in)

    (leftover_grad, totals), grads_all = lax.scan(backward_tick, (start_zero, zero_grads), ticks)
    acts = lax.dynamic_slice_in_dim(outs_all, section, micro, 0)[None]
    input_grads = lax.dynamic_slice_in_dim(grads_all, 1 - section, micro, 0)[None]
    shares = (
        lax.psum_scatter(
            totals[0].astype(jnp.bfloat16), CTX, scatter_dimension=1, tiled=True
        ).astype(jnp.float32),
        lax.psum_scatter(
            totals[1].astype(jnp.bfloat16), CTX, scatter_dimension=1, tiled=True
        ).astype(jnp.float32),
        lax.psum_scatter(
            totals[2].astype(jnp.bfloat16), CTX, scatter_dimension=1, tiled=True
        ).astype(jnp.float32),
        lax.psum_scatter(
            totals[3].astype(jnp.bfloat16), CTX, scatter_dimension=0, tiled=True
        ).astype(jnp.float32),
        lax.psum_scatter(
            totals[4].astype(jnp.bfloat16), CTX, scatter_dimension=0, tiled=True
        ).astype(jnp.float32),
        lax.psum_scatter(
            totals[5].astype(jnp.bfloat16), CTX, scatter_dimension=0, tiled=True
        ).astype(jnp.float32),
        lax.psum_scatter(
            totals[6].astype(jnp.bfloat16), CTX, scatter_dimension=1, tiled=True
        ).astype(jnp.float32),
        lax.psum_scatter(
            totals[7].astype(jnp.bfloat16), CTX, scatter_dimension=0, tiled=True
        ).astype(jnp.float32),
        lax.psum_scatter(
            totals[8].astype(jnp.bfloat16), CTX, scatter_dimension=0, tiled=True
        ).astype(jnp.float32),
        lax.psum_scatter(
            totals[9].astype(jnp.bfloat16), CTX, scatter_dimension=0, tiled=True
        ).astype(jnp.float32),
    )
    return (
        acts,
        input_grads,
        shares[0][None],
        shares[1][None],
        shares[2][None],
        shares[3][None],
        shares[4][None],
        shares[5][None],
        shares[6][None],
        shares[7][None],
        shares[8][None],
        shares[9][None],
    )


def solution(mesh):
    specs = {
        TOKEN: P(SECTION, None, CTX, TP),
        ROWS: P(SECTION, TP, CTX),
        COLUMNS: P(SECTION, CTX, TP),
        VECTOR: P(SECTION, (TP, CTX)),
        VECTORS: P(SECTION, None, (TP, CTX)),
    }
    weights = (TOKEN, VECTORS, ROWS, VECTOR, COLUMNS, VECTOR, ROWS, VECTOR, VECTOR, VECTOR)
    placed = tuple(specs[name] for name in weights)
    heads = D // HD
    place = {SECTION: 2, CTX: 4, TP: 4}
    whole_heads = heads % (mesh.shape[TP] * mesh.shape[CTX]) == 0
    return jax.shard_map(
        shards if whole_heads and dict(mesh.shape) == place else base_shards,
        mesh=mesh,
        in_specs=(specs[TOKEN], P(), *placed),
        out_specs=(specs[TOKEN], specs[TOKEN], *placed),
        check_vma=False,
    )
```

time: 2500 us -> 632 us (0.25)
  waiting for transfers between devices: 1760 us -> 0 us
  Pallas kernels: 0 us -> 596 us
  matrix products: 354 us -> 0 us
  blocking collectives: 117 us -> 0 us
  other arithmetic: 120 us -> 14 us
  local copies, waits for them, and re-layouts: 80.9 us -> 11.2 us
    all_gather x26 -> x0, waiting for transfers between devices: 1180 us -> none  [the longest x1 149 us: shards(): lax.all_gather(fc1_weight[0], 'ctx', axis=0, tiled=True)]
    pallas_call x0 -> x3, Pallas kernels: none -> 596 us  [remote_call(): pl.pallas_call(kernel, out_shape=tuple((jax.ShapeDtypeStruct(shape, kind)...]
    reduce_scatter x16 -> x0, waiting for transfers between devices: 533 us -> none  [the longest x1 144 us: shards(): lax.psum_scatter(totals[6].astype(jnp.bfloat16), 'ctx', scatter_dimension...]
    dot_general x57 -> x0, matrix products: 354 us -> none  [the longest x3 38.8 us: backward_layer(): jnp.einsum('tf,te->fe', hidden, grad_rows, preferred_element_type=jnp.flo...]
    all_gather x7 -> x0, blocking collectives: 70.1 us -> none  [the longest x1 13.6 us: shards(): lax.all_gather(fc1_bias[0], 'ctx', axis=0, tiled=True)]
    convert_element_type x42 -> x2, other arithmetic: 44.2 us -> 0.69 us  [the longest x1 0.69 us: shards(): qkv_bias[0].astype(F32)]
    psum x6 -> x0, blocking collectives: 36.9 us -> none  [the longest x3 18.7 us: forward_layer(): lax.psum((jnp.sum(wide_in, axis=1), jnp.sum(wide_in * wide_in, axis=1)),...]
    ppermute x6 -> x0, waiting for transfers between devices: 36.8 us -> none  [from_behind(): lax.ppermute(value, axis, [(source, source + steps) for source in range(l...]
  transfers between devices with their start and end apart: 49 -> 0, of which waited for: 42 -> 0; matrix products, arithmetic and copies ran while one was open for 16% -> 0% of each run, Pallas kernels for 0% -> 0%
where the time goes in v3:
time: 632 us; the launch traced here: 623 us
  Pallas kernels  596 us (94%)
  other arithmetic  14 us (2%)
  local copies, waits for them, and re-layouts  11.2 us (2%)
    pallas_call x3, Pallas kernels, remote_call(): pl.pallas_call(kernel, out_shape=tuple((jax.ShapeDtypeStruct(shape, kind)...  596 us

profile of v3, /device:TPU:0, one launch (start us, length us, event | category | flops | bytes accessed | tf_op | source)
XLA Modules:
  0.0 622.7 jit_solution(5862659586520381885)
XLA Ops:
  0.7 0.7 convert_add_fusion
  1.5 0.7 bitcast_convert_fusion.4
  2.2 0.7 reshape.63
  2.9 0.8 concatenate.9
  3.7 0.6 pad.4.refs_1_
  4.3 0.6 convert_reduce_fusion
  5.3 1.0 copy.36.refs_3_.refs_5_.refs_27_
  6.3 1.0 copy.35.refs_2_.refs_4_.refs_26_
  7.4 1.0 copy.37.refs_4_.refs_6_.refs_28_
  8.4 274.8 %first.1 = (bf16[2,3,2048,128]{3,2,1,0:T(8,128)(2,1)}, bf16[2,128,2048]{2,1,0:T(8,128)(2,1)}, bf16[2,2048,512]{2,1,0:T(8,128)(2,1)}, bf16[2,512,2048]{2,1,0:T(8,...) custom-call(bf16[2,256,512]{2,1,0:T(8,128)(2,1)} %bitcast.35, ...), custom_call_target="tpu_custom_call" | custom-call | tf_op jit(solution)/shard_map/first/pallas_call | solution.py:748
  283.2 118.3 %middle.1 = (bf16[3,2048,128]{2,1,0:T(8,128)(2,1)}, bf16[128,2048]{1,0:T(8,128)(2,1)}, bf16[2048,512]{1,0:T(8,128)(2,1)}, bf16[512,2048]{1,0:T(8,128)(2,1)}, f32...) custom-call(bf16[1024,2048]{1,0:T(8,128)(2,1)} %get-tuple-element.48, ...), custom_call_target="tpu_custom_call" | custom-call | tf_op jit(solution)/shard_map/middle/pallas_call | solution.py:748
  401.5 203.4 %last.1 = (bf16[3,512,512]{2,1,0:T(8,128)(2,1)}, bf16[512,512]{1,0:T(8,128)(2,1)}, bf16[512,2048]{1,0:T(8,128)(2,1)}, bf16[2048,512]{1,0:T(8,128)(2,1)}, bf16[2,...) custom-call(bf16[1024,2048]{1,0:T(8,128)(2,1)} %get-tuple-element.56.refs_0_, ...), custom_call_target="tpu_custom_call" | custom-call | tf_op jit(solution)/shard_map/last/pallas_call | solution.py:748
  604.9 0.7 slice.16
  605.6 1.3 fusion.1
  606.9 1.3 slice.17
  608.1 0.7 slice_bitcast_fusion
  608.8 0.6 copy.44
  609.3 2.3 bitcast_convert_fusion.3
  611.6 3.5 bitcast_convert_fusion.2
  615.2 2.5 bitcast_convert_fusion.1
  617.7 2.6 bitcast_convert_fusion
  620.3 0.5 copy.48
  620.8 0.8 copy.49
  621.6 0.8 copy.50
  (25 shorter events, 0.7 us)
Async XLA Ops:
  0.6 3.6 copy-start
  605.6 14.7 %copy-start.6 = (f32[1,128]{1,0:T(1,128)}, f32[1,128]{1,0:T(1,128)S(1)}, u32[]{:S(2)}) copy-start(f32[1,128]{1,0:T(1,128)S(1)} %slice.16) | copy-start | bytes 1540
  609.3 5.8 copy-start.3
  615.2 2.5 copy-start.2
  615.2 7.3 %copy-start.1 = (s32[2,1024]{1,0:T(2,128)S(1)}, s32[2,1024]{1,0:T(2,128)}, u32[]{:S(2)}) copy-start(s32[2,1024]{1,0:T(2,128)} %param.13) | copy-start | bytes 24580
  617.7 3.1 copy-start.5
  617.7 3.9 copy-start.4

commit v4 on v3

--- a/solution.py
+++ b/solution.py
@@ -15,6 +15,7 @@
 GELU_C = 0.7978845608028654
 GELU_K = 0.044715
 ACT = "act"
+ACT1 = "act1"
 ACTS = "acts"
 ARRIVED = "arrived_"
 ATT = "att"
@@ -27,6 +28,10 @@
 CTX = "ctx"
 DOWN = "down"
 D_W = "d_w_"
+D_W_DOWN = "d_w_down"
+D_W_OUT = "d_w_out"
+D_W_QKV = "d_w_qkv"
+D_W_UP = "d_w_up"
 G = "g"
 G1 = "g1"
 GAIN = "gain"
@@ -34,6 +39,7 @@
 GRAD = "grad"
 GRADS = "grads"
 G_BLOCK = "g_block"
+HBM = "hbm_"
 HEADS_EQ = "hts,shd->thd"
 HIDDEN = "hidden"
 HOME = "home_"
@@ -67,7 +73,6 @@
 VECTOR = "vector"
 VECTORS = "vectors"
 W = "w_"
-X = "x"
 X1 = "x1"
 X_BLOCK = "x_block"
 BF16 = jnp.bfloat16
@@ -151,6 +156,22 @@
         self.copies.append((copy, when))
         return copy
 
+    def pick(self, *values):
+        chosen = values[3]
+        for c in (2, 1, 0):
+            chosen = jnp.where(self.c == c, values[c], chosen)
+        return chosen
+
+    def step_copy(self, base, step, source, target):
+        return pltpu.make_async_remote_copy(
+            src_ref=source,
+            dst_ref=target,
+            send_sem=self.send_sems.at[base + step - 1],
+            recv_sem=self.recv_sems.at[base + step - 1],
+            device_id={CTX: (self.c + step) % 4},
+            device_id_type=MESH,
+        )
+
     def send_one_of(self, first, source, other_source, target, device):
         index = len(self.copies)
         copies = [
@@ -308,18 +329,19 @@
         size = self.rows // 2
         return pl.ds(pl.multiple_of(c * self.rows + group * size, 16), size)
 
-    def begin(self):
+    def begin(self, compute):
         w = self.w
-        self.cores = []
-        for group, c, y in self.order:
-            columns = pl.ds(pl.multiple_of((2 * y + 1 - w.k) * self.part, 128), self.part)
-            self.cores.append(
-                self.send(
-                    self.partial.at[self.span(group, c), columns],
-                    self.theirs.at[y, self.span(group, c)],
-                    w.core,
-                )
-            )
+        self.cores = [None] * len(self.order)
+        for _, place in self.places:
+            compute(place)
+            for index, (group, c, y) in enumerate(self.order):
+                if c is place:
+                    columns = pl.ds(pl.multiple_of((2 * y + 1 - w.k) * self.part, 128), self.part)
+                    self.cores[index] = self.send(
+                        self.partial.at[self.span(group, c), columns],
+                        self.theirs.at[y, self.span(group, c)],
+                        w.core,
+                    )
 
     def take(self, index):
         group, c, y = self.order[index]
@@ -728,19 +750,28 @@
 
 def grad_shapes(width, e, f):
     return {
-        "d_w_qkv": ((3, width, e), BF16),
-        "d_w_out": ((e, width), BF16),
-        "d_w_up": ((width, f), BF16),
-        "d_w_down": ((f, width), BF16),
+        D_W_QKV: ((3, width, e), BF16),
+        D_W_OUT: ((e, width), BF16),
+        D_W_UP: ((width, f), BF16),
+        D_W_DOWN: ((f, width), BF16),
         "d_b_qkv": ((3, e), F32),
         "d_b_up": ((1, f), F32),
     }
 
 
-def remote_call(body, name, key, inputs, outputs, scratch, copies, in_hbm=(), out_hbm=()):
+STAGED = (NORMED, QKV, ATT, SLOPE, HIDDEN)
+
+
+def remote_call(
+    body, name, key, inputs, outputs, scratch, copies, in_hbm=(), out_hbm=(), staged=()
+):
+    scratch = scratch | {each_in: (inputs[each_in].shape, inputs[each_in].dtype) for each_in in staged if each_in in inputs}
+    scratch |= {each_out: outputs[each_out] for each_out in staged if each_out in outputs}
+    in_hbm, out_hbm = (*in_hbm, *staged), (*out_hbm, *staged)
     vmem = pl.BlockSpec(memory_space=pltpu.VMEM)
     hbm = pl.BlockSpec(memory_space=pl.ANY)
-    keys = list(inputs) + list(outputs) + list(scratch) + ["free_sem", "local_sems", "send_sems", "recv_sems"]
+    given = [HBM + ref if ref in staged else ref for ref in (*inputs, *outputs)]
+    keys = given + list(scratch) + ["free_sem", "local_sems", "send_sems", "recv_sems"]
 
     def kernel(*refs):
         body(Refs(**dict(zip(keys, refs))))
@@ -765,6 +796,17 @@
     return dict(zip(outputs, outs))
 
 
+def stage(r, names, first_sem, out=False):
+    copies = {}
+    for i, name in enumerate(names):
+        ends = (getattr(r, HBM + name), getattr(r, name))
+        copies[name] = pltpu.make_async_copy(
+            *(ends[::-1] if out else ends), r.local_sems.at[first_sem + i]
+        )
+        copies[name].start()
+    return copies
+
+
 def weight_scratch(turn):
     shapes = {W + name: (turn.turned_shape(name), BF16) for name in NAMES}
     width = 4 * turn.d
@@ -841,20 +883,31 @@
     told = [w.send(r.vector, r.vectors.at[s, w.c, w.t], peer) for peer in peers]
     local, far, across, puts = {}, {}, {name: [] for name in NAMES}, {}
 
+    leave = (w.pick(3, 2, 2, 1), w.pick(2, 3, 1, 2), w.pick(1, 1, 3, 3))
+    enter = (w.pick(1, 2, 2, 3), w.pick(2, 1, 3, 2), w.pick(3, 3, 1, 1))
+
+    def along_copy(name, half, base, step):
+        place = (w.c + step) % 4
+        return w.step_copy(
+            base,
+            step,
+            turn.shard(name, shards[name], place, half),
+            turn.turned(name, mine[name], w.c, half),
+        )
+
     def send_along(name):
         for half in HALVES[name]:
-            for step, place in w.others:
-                far[name, step, half] = w.send(
-                    turn.shard(name, shards[name], place, half),
-                    turn.turned(name, mine[name], w.c, half),
-                    {CTX: place},
-                )
+            base = far[name, half] = len(w.copies)
+            for step in leave:
+                copy = along_copy(name, half, base, step)
+                copy.start()
+                w.copies.append((copy, None))
                 yield
 
     def pass_across(name):
         for half in HALVES[name]:
-            for step in (1, 3, 2):
-                far[name, step, half].wait_recv()
+            for step in enter:
+                along_copy(name, half, far[name, half], step).wait_recv()
                 spot = turn.turned(name, mine[name], (w.c + 4 - step) % 4, half)
                 across[name].append(w.send(spot, spot, w.across))
                 yield
@@ -917,12 +970,12 @@
         attend(i)
     fetch(UP).wait()
     each(count, up)
+    stores = stage(r, STAGED, 12, True)
     for _ in passing:
         pass
     fetch(DOWN).wait()
-    each(count, down)
     scatter = scatter_of(w, r, r.partial, rows, part)
-    scatter.begin()
+    scatter.begin(down)
     scatter.run()
     gather = Gather(w, r.x1, rows, part)
     bias = own_bias(w, r, 0)
@@ -934,6 +987,8 @@
         gather.begin(group)
     for _ in gather.steps():
         pass
+    for copy in stores.values():
+        copy.wait()
     w.drain()
 
 
@@ -949,7 +1004,7 @@
     outputs |= saved_shapes(tokens, width, turn.e, turn.f)
     outputs |= {MEAN: ((tokens, 1), F32), INVERSE_STD: ((tokens, 1), F32)}
     scratch = {BOUNCE + name: (turn.piece_shape(name), BF16) for name in NAMES}
-    scratch |= {"other": block, X: full, PARTIAL: full}
+    scratch |= {"other": block, "x": full, PARTIAL: full}
     scratch |= weight_scratch(turn) | scatter_dict(rows, part)
     return remote_call(
         functools.partial(first_body, turn, rows, part),
@@ -963,11 +1018,15 @@
         320,
         in_hbm=[SHARD + name for name in NAMES],
         out_hbm=[TURNED + name for name in NAMES],
+        staged=STAGED,
     )
 
 
 def middle_body(turn, rows, part, r):
     w = Wire(r.send_sems, r.recv_sems)
+    load_x = pltpu.make_async_copy(r.x1, r.normed, r.local_sems.at[4])
+    load_x.start()
+    r.x = r.normed
     loads = {}
     for i, name in enumerate(FIRST):
         loads[name] = pltpu.make_async_copy(
@@ -983,6 +1042,7 @@
     arriving = gather_g.steps()
     small_params(w, r, 1)
     norm, project, attend, up, down, count = forward_steps(r)
+    load_x.wait()
     each(4 * rows // 64, norm)
     pull(arriving, times=4)
     loads[QKV].wait()
@@ -998,7 +1058,9 @@
     each(count, up)
     loads[DOWN].wait()
     loads[OUT].wait()
-    each(count, down)
+    other = Scatter(w, r.partial, (r.theirs_x, r.chip_x, r.from_y_x, r.from_far_x), rows, part)
+    other.begin(down)
+    summing = other.steps()
     for _ in arriving:
         pass
     b = Refs(**dict(r.__dict__, partial=r.partial_g))
@@ -1006,22 +1068,34 @@
         backward_steps(b)
     )
     start()
-    each(count, open_branches)
+    pull(summing, times=2)
+    some(0, 2, open_branches)
+    pull(summing, times=2)
+    some(2, count, open_branches)
+    pull(summing, times=4)
     for i in range(count):
         attend_back(i)
+        pull(summing)
     each(count, unrotate)
-    each(count, close)
 
     def leftover():
         wide = 4 * part // TILE
-        for step, times in ((grad_rows, wide), (grad_up, wide), (grad_qkv, wide)):
-            for i in range(0, times, 2):
+        for slot, step, made in (
+            (8, grad_rows, (D_W_DOWN, D_W_OUT)),
+            (10, grad_up, (D_W_UP,)),
+            (11, grad_qkv, (D_W_QKV,)),
+        ):
+            for i in range(0, wide, 2):
                 some(i, i + 2, step)
                 yield
-
+            stores.update(stage(r, made, slot, True))
+
+    stores = {}
     fill = leftover()
     scatter = scatter_of(w, r, r.partial_g, rows, part)
-    scatter.begin()
+    scatter.begin(close)
+    for _ in summing:
+        pass
     for i, _ in enumerate(scatter.steps()):
         if i % 2 == 1:
             pull(fill)
@@ -1050,24 +1124,32 @@
         pull(fill)
     for _ in fill:
         pass
+    bias = own_bias(w, r, 1)
+    for group in range(GROUPS):
+        own = slice(group * half, (group + 1) * half)
+        value = r.act[own].astype(F32) + other.total(group) + bias
+        r.act1[own] = value.astype(BF16)
     slab = part // 4
     columns = pl.ds(pl.multiple_of(w.t * part + w.c * slab, 128), slab)
     r.d_b_out[...] = jnp.sum(r.g[:, columns].astype(F32), axis=0, keepdims=True)
+    for copy in stores.values():
+        copy.wait()
     w.drain()
 
 
 def middle(made, tables, turn, rows, part):
     tokens, width = 4 * rows, 4 * part
     full = ((tokens, width), BF16)
-    inputs = {X: made[X1], ACT: made[ACT], G_BLOCK: made[G_BLOCK]}
+    inputs = {X1: made[X1], ACT: made[ACT], G_BLOCK: made[G_BLOCK]}
     inputs |= {VECTORS: made[VECTORS]} | tables
     inputs |= {TURNED + name: made[TURNED + name] for name in NAMES}
     outputs = grad_shapes(width, turn.e, turn.f)
-    outputs |= {"d_b_out": ((1, part // 4), F32), PARTIAL: full}
+    outputs |= {"d_b_out": ((1, part // 4), F32), ACT1: ((rows, part), BF16)}
     outputs |= {GRAD: ((rows, part), BF16), G1: full, SUMS: ((8, part), F32)}
     scratch = saved_shapes(tokens, width, turn.e, turn.f)
     scratch |= {MEAN: ((tokens, 1), F32), INVERSE_STD: ((tokens, 1), F32)}
-    scratch |= scratch_shapes_back(tokens, turn.e, turn.f) | {"partial_g": full, G: full}
+    scratch |= scratch_shapes_back(tokens, turn.e, turn.f) | {"partial_g": full, G: full, PARTIAL: full}
+    scratch |= {key + "_x": value for key, value in scatter_dict(rows, part).items()}
     scratch |= {MEAN_BLOCK: ((rows, 1), F32), STD_BLOCK: ((rows, 1), F32)}
     scratch |= {GAIN_BLOCK: ((1, part), F32)}
     scratch |= weight_scratch(turn) | scatter_dict(rows, part) | back_dict(rows, part)
@@ -1078,18 +1160,23 @@
         inputs,
         outputs,
         scratch,
-        200,
-        in_hbm=[TURNED + name for name in NAMES],
-    )
-
-
-LATER = (DOWN, OUT, UP, QKV)
+        240,
+        in_hbm=[X1] + [TURNED + name for name in NAMES],
+        staged=[D_W + name for name in NAMES],
+    )
+
+
+LATER = (OUT, DOWN, UP, QKV)
+
+
+ENTERING = (G, HIDDEN, ATT, SLOPE, NORMED, QKV, COSINE, SINE)
 
 
 def last_body(turn, rows, part, r):
     w = Wire(r.send_sems, r.recv_sems)
     s = w.section
     half = rows // GROUPS
+    brought = stage(r, ENTERING, 20)
     loads = {}
     for i, name in enumerate(FIRST):
         loads[name] = pltpu.make_async_copy(
@@ -1157,35 +1244,26 @@
     )
     wide = 4 * part // TILE
     start()
-    other = scatter_of(w, r, r.partial_x, rows, part)
-    other.begin()
-    summing = other.steps()
-    for i in range(0, wide, 2):
-        some(i, i + 2, grad_rows)
-        pull(summing, times=2)
+    for name in ENTERING[:3]:
+        brought[name].wait()
+    each(wide, grad_rows)
+    for name in ENTERING[3:]:
+        brought[name].wait()
+    send_across(OUT)
     send_across(DOWN)
-    send_across(OUT)
+    settling = settle()
     loads[DOWN].wait()
     loads[OUT].wait()
-    for i in range(count):
-        some(i, i + 1, open_branches)
-        pull(summing)
-    for i in range(0, wide, 2):
-        some(i, i + 2, grad_up)
-        pull(summing)
+    each(count, open_branches)
+    pull(settling)
+    each(wide, grad_up)
     send_across(UP)
-    settling = settle()
-    for _ in summing:
-        pass
+    pull(settling)
     for i in range(count):
         attend_back(i)
         pull(settling)
-    bias = own_bias(w, r, 1)
     r.all_acts[0] = r.act[...]
-    for group in range(GROUPS):
-        own = slice(group * half, (group + 1) * half)
-        value = r.act[own].astype(F32) + other.total(group) + bias
-        r.all_acts[1, own] = value.astype(BF16)
+    r.all_acts[1] = r.act1[...]
     r.acts[s] = r.all_acts[s]
     pairs = [w.send(r.all_acts.at[1 - s], r.acts.at[s], w.across)]
     each(count, unrotate)
@@ -1194,7 +1272,8 @@
     pull(settling)
     loads[QKV].wait()
     loads[UP].wait()
-    each(count, close)
+    scatter = scatter_of(w, r, r.partial, rows, part)
+    scatter.begin(close)
     slab = part // 4
     columns = pl.ds(pl.multiple_of(w.t * part + w.c * slab, 128), slab)
     n_up = r.d_b_up.shape[1] // slab
@@ -1207,10 +1286,6 @@
     r.small[0, 3 + n_up : 4 + n_up] = jnp.sum(r.g[:, columns].astype(F32), axis=0, keepdims=True)
     r.small[1, 3 + n_up : 4 + n_up] = r.one_b_out[...]
     small_copy = w.send(r.small.at[1 - s], r.small_in, w.across)
-    w.flush(other.sent)
-    w.meet(r.free_sem, neighbours(w))
-    scatter = scatter_of(w, r, r.partial, rows, part)
-    scatter.begin()
     for i, _ in enumerate(scatter.steps()):
         if i % 4 == 3:
             pull(settling)
@@ -1267,7 +1342,7 @@
         UP: (turn.d, f),
         DOWN: (f, turn.d),
     }
-    inputs = {G: mid[G1], "grad1": mid[GRAD], "partial_x": mid[PARTIAL], "sums1": mid[SUMS]}
+    inputs = {G: mid[G1], "grad1": mid[GRAD], ACT1: mid[ACT1], "sums1": mid[SUMS]}
     inputs |= {key: made[key] for key in SAVED + (MEAN, INVERSE_STD, VECTORS, ACT, X_BLOCK)}
     inputs |= {ONE + name: mid[D_W + name] for name in NAMES}
     inputs |= {ONE + name: mid["d_" + name] for name in (B_QKV, B_UP, "b_out")}
@@ -1304,6 +1379,7 @@
         140,
         in_hbm=[TURNED + name for name in NAMES] + [ONE + name for name in NAMES],
         out_hbm=[HOME + name for name in NAMES],
+        staged=ENTERING,
     )
 
 

time: 632 us -> 610 us (0.965)
  Pallas kernels: 596 us -> 577 us
    pallas_call x3, Pallas kernels: 596 us -> 577 us  [remote_call(): pl.pallas_call(kernel, out_shape=tuple((jax.ShapeDtypeStruct(shape, kind)...]
where the time goes in v4:
time: 610 us; the launch traced here: 603 us
  Pallas kernels  577 us (95%)
  other arithmetic  14 us (2%)
  local copies, waits for them, and re-layouts  11.2 us (2%)
    pallas_call x3, Pallas kernels, remote_call(): pl.pallas_call(kernel, out_shape=tuple((jax.ShapeDtypeStruct(shape, kind)...  577 us

profile of v4, /device:TPU:0, one launch (start us, length us, event | category | flops | bytes accessed | tf_op | source)
XLA Modules:
  0.0 603.5 jit_solution(12426262422695341232)
XLA Ops:
  0.7 0.7 convert_add_fusion
  1.5 0.7 bitcast_convert_fusion.4
  2.2 0.7 reshape.63
  2.9 0.8 concatenate.9
  3.7 0.6 pad.4.refs_1_
  4.3 0.6 convert_reduce_fusion
  5.3 1.0 copy.36.refs_3_.refs_5_.refs_27_
  6.3 1.0 copy.35.refs_2_.refs_4_.refs_26_
  7.4 1.0 copy.37.refs_4_.refs_6_.refs_28_
  8.4 263.0 %first.1 = (bf16[2,3,2048,128]{3,2,1,0:T(8,128)(2,1)}, bf16[2,128,2048]{2,1,0:T(8,128)(2,1)}, bf16[2,2048,512]{2,1,0:T(8,128)(2,1)}, bf16[2,512,2048]{2,1,0:T(8,...) custom-call(bf16[2,256,512]{2,1,0:T(8,128)(2,1)} %bitcast.35, ...), custom_call_target="tpu_custom_call" | custom-call | tf_op jit(solution)/shard_map/first/pallas_call | solution.py:779
  271.4 126.7 %middle.1 = (bf16[3,2048,128]{2,1,0:T(8,128)(2,1)}, bf16[128,2048]{1,0:T(8,128)(2,1)}, bf16[2048,512]{1,0:T(8,128)(2,1)}, bf16[512,2048]{1,0:T(8,128)(2,1)}, f32...) custom-call(bf16[1024,2048]{1,0:T(8,128)(2,1)} %get-tuple-element.48, ...), custom_call_target="tpu_custom_call" | custom-call | tf_op jit(solution)/shard_map/middle/pallas_call | solution.py:779
  398.1 187.4 %last.1 = (bf16[3,512,512]{2,1,0:T(8,128)(2,1)}, bf16[512,512]{1,0:T(8,128)(2,1)}, bf16[512,2048]{1,0:T(8,128)(2,1)}, bf16[2048,512]{1,0:T(8,128)(2,1)}, bf16[2,...) custom-call(bf16[1024,2048]{1,0:T(8,128)(2,1)} %get-tuple-element.56.refs_0_, ...), custom_call_target="tpu_custom_call" | custom-call | tf_op jit(solution)/shard_map/last/pallas_call | solution.py:779
  585.5 0.7 slice.16
  586.2 1.3 fusion.1
  587.5 1.3 slice.17
  588.7 0.7 slice_bitcast_fusion
  589.4 0.6 copy.44
  590.0 2.3 bitcast_convert_fusion.3
  592.3 3.5 bitcast_convert_fusion.2
  595.8 2.5 bitcast_convert_fusion.1
  598.3 2.6 bitcast_convert_fusion
  600.9 0.5 copy.48
  601.5 0.8 copy.49
  602.2 0.8 copy.50
  (25 shorter events, 0.7 us)
Async XLA Ops:
  0.6 3.6 copy-start
  586.2 14.7 %copy-start.6 = (f32[1,128]{1,0:T(1,128)}, f32[1,128]{1,0:T(1,128)S(1)}, u32[]{:S(2)}) copy-start(f32[1,128]{1,0:T(1,128)S(1)} %slice.16) | copy-start | bytes 1540
  590.0 5.8 copy-start.3
  595.8 2.5 copy-start.2
  595.8 7.3 %copy-start.1 = (s32[2,1024]{1,0:T(2,128)S(1)}, s32[2,1024]{1,0:T(2,128)}, u32[]{:S(2)}) copy-start(s32[2,1024]{1,0:T(2,128)} %param.13) | copy-start | bytes 24580
  598.3 3.1 copy-start.5
  598.3 3.9 copy-start.4

commit v5 on v4

--- a/solution.py
+++ b/solution.py
@@ -20,6 +20,7 @@
 ARRIVED = "arrived_"
 ATT = "att"
 BOUNCE = "bounce_"
+B_OUT = "b_out"
 B_QKV = "b_qkv"
 B_UP = "b_up"
 COLUMNS = "columns"
@@ -51,6 +52,7 @@
 MEAN_BLOCK = "mean_block"
 NORMED = "normed"
 NORM_SUM = "norm_sum"
+N_RAW = "raw_"
 N_START = "start"
 ONE = "one_"
 OUT = "out"
@@ -462,7 +464,10 @@
 
     def inner(self, name, half):
         size = self.rows(name)
-        return (0, size) if half is None else (half * size // 2, size // 2)
+        if half is None:
+            return (0, size)
+        index, count = half
+        return (index * size // count, size // count)
 
     def shard(self, name, ref, c, half=None):
         start, size = self.inner(name, half)
@@ -861,7 +866,12 @@
 
 
 FIRST = (OUT, QKV, UP, DOWN)
-HALVES = {OUT: (None,), QKV: (None,), UP: (0, 1), DOWN: (0, 1)}
+HALVES = {
+    OUT: (None,),
+    QKV: (None,),
+    UP: ((0, 2), (1, 2)),
+    DOWN: ((0, 4), (1, 4), (2, 4), (3, 4)),
+}
 
 
 def pull(*generators, times=1):
@@ -879,6 +889,13 @@
     mine = {name: getattr(r, TURNED + name).at[s] for name in NAMES}
     bounce = {name: getattr(r, BOUNCE + name) for name in NAMES}
     swap = w.send(r.own.at[1 - s], r.other, w.across)
+    raw = [getattr(r, N_RAW + name)[...].astype(F32) for name in RAW]
+    slab = raw[0].shape[1]
+    r.vector[...] = jnp.zeros_like(r.vector)
+    r.vector[0:1] = raw[0] + raw[1]
+    r.vector[1:2], r.vector[2:3], r.vector[3:6] = raw[2], raw[3], raw[4]
+    for i in range(raw[5].shape[1] // slab):
+        r.vector[6 + i : 7 + i] = raw[5][:, i * slab : (i + 1) * slab]
     r.vectors[s, w.c, w.t] = r.vector[...]
     told = [w.send(r.vector, r.vectors.at[s, w.c, w.t], peer) for peer in peers]
     local, far, across, puts = {}, {}, {name: [] for name in NAMES}, {}
@@ -961,11 +978,11 @@
         copy.wait()
     each(count, project)
     pull(passing, times=3)
-    pull(sending, times=3)
+    pull(sending, times=6)
     attend(0)
     attend(1)
     pull(passing, times=3)
-    pull(sending, times=3)
+    pull(sending, times=6)
     for i in range(2, count):
         attend(i)
     fetch(UP).wait()
@@ -992,7 +1009,10 @@
     w.drain()
 
 
-def first(own, vector, tables, shards):
+RAW = (B_OUT, "b_down", GAIN, SHIFT, B_QKV, B_UP)
+
+
+def first(own, vectors, tables, shards):
     _, rows, part = own.shape
     turn = Turn(shards[QKV].shape[1], shards[QKV].shape[2] // 4, shards[UP].shape[1] // 4)
     tokens, width = 4 * rows, 4 * part
@@ -1000,17 +1020,18 @@
     block = ((rows, part), BF16)
     outputs = {TURNED + name: ((2,) + turn.turned_shape(name), BF16) for name in NAMES}
     outputs |= {X1: full, X_BLOCK: block, G_BLOCK: block, ACT: block}
-    outputs |= {VECTORS: ((2, 4, 4) + vector.shape, F32)}
+    outputs |= {VECTORS: ((2, 4, 4, 16, turn.e), F32)}
     outputs |= saved_shapes(tokens, width, turn.e, turn.f)
     outputs |= {MEAN: ((tokens, 1), F32), INVERSE_STD: ((tokens, 1), F32)}
     scratch = {BOUNCE + name: (turn.piece_shape(name), BF16) for name in NAMES}
-    scratch |= {"other": block, "x": full, PARTIAL: full}
+    scratch |= {"other": block, "x": full, PARTIAL: full, VECTOR: ((16, turn.e), F32)}
     scratch |= weight_scratch(turn) | scatter_dict(rows, part)
     return remote_call(
         functools.partial(first_body, turn, rows, part),
         "first",
         START,
-        {"own": own, VECTOR: vector}
+        {"own": own}
+        | {N_RAW + name: vector for name, vector in zip(RAW, vectors)}
         | tables
         | {SHARD + name: shards[name] for name in NAMES},
         outputs,
@@ -1345,7 +1366,7 @@
     inputs = {G: mid[G1], "grad1": mid[GRAD], ACT1: mid[ACT1], "sums1": mid[SUMS]}
     inputs |= {key: made[key] for key in SAVED + (MEAN, INVERSE_STD, VECTORS, ACT, X_BLOCK)}
     inputs |= {ONE + name: mid[D_W + name] for name in NAMES}
-    inputs |= {ONE + name: mid["d_" + name] for name in (B_QKV, B_UP, "b_out")}
+    inputs |= {ONE + name: mid["d_" + name] for name in (B_QKV, B_UP, B_OUT)}
     inputs |= {TURNED + name: made[TURNED + name] for name in NAMES} | tables
     pairs = ((2, rows, part), BF16)
     outputs = {HOME + name: (homes[name], BF16) for name in NAMES}
@@ -1404,19 +1425,10 @@
     tables = doc_tables(
         lax.dynamic_index_in_dim(doc_ids, section, 0, keepdims=False), slab // HD
     )
-    vector = jnp.concatenate(
-        [
-            out_bias.astype(F32) + fc2_bias.astype(F32),
-            norm_gain.astype(F32),
-            norm_shift.astype(F32),
-            qkv_bias[0].astype(F32),
-            fc1_bias.astype(F32).reshape(n_up, slab),
-        ]
-    )
-    vector = jnp.pad(vector, ((0, 16 - vector.shape[0]), (0, 0)))
+    vectors = (out_bias, fc2_bias, norm_gain, norm_shift, qkv_bias[0], fc1_bias)
     shard_of = {QKV: qkv_weight[0], OUT: out_weight[0], UP: fc1_weight[0], DOWN: fc2_weight[0]}
     turn = Turn(shard_of[QKV].shape[1], slab, shard_of[UP].shape[1] // 4)
-    made = first(boundary[0], vector, tables, shard_of)
+    made = first(boundary[0], vectors, tables, shard_of)
     mid = middle(made, tables, turn, rows, part)
     out = last(made, mid, tables, turn, rows, part)
     small, norms = out[SMALL_SUM], out[NORM_SUM]

time: 610 us -> 604 us (level)
  no operation moved by 1% of the time
where the time goes in v5:
time: 604 us; the launch traced here: 601 us
  Pallas kernels  578 us (96%)
  other arithmetic  11.9 us (2%)
  local copies, waits for them, and re-layouts  10.3 us (2%)
    pallas_call x3, Pallas kernels, remote_call(): pl.pallas_call(kernel, out_shape=tuple((jax.ShapeDtypeStruct(shape, kind)...  578 us

profile of v5, /device:TPU:0, one launch (start us, length us, event | category | flops | bytes accessed | tf_op | source)
XLA Modules:
  0.0 600.8 jit_solution(9787911963249547734)
XLA Ops:
  0.7 0.1 pad.5.clone
  0.8 0.1 pad.2.clone
  0.8 0.5 copy-done
  1.4 0.6 convert_reduce_fusion
  1.9 0.3 fusion
  2.2 0.1 maximum_maximum_fusion
  2.4 1.0 copy.36.refs_8_.refs_5_.refs_27_
  3.4 1.0 copy.35.refs_7_.refs_4_.refs_26_
  4.5 1.0 copy.37.refs_9_.refs_6_.refs_28_
  5.5 262.6 %first.1 = (bf16[2,3,2048,128]{3,2,1,0:T(8,128)(2,1)}, bf16[2,128,2048]{2,1,0:T(8,128)(2,1)}, bf16[2,2048,512]{2,1,0:T(8,128)(2,1)}, bf16[2,512,2048]{2,1,0:T(8,...) custom-call(bf16[2,256,512]{2,1,0:T(8,128)(2,1)} %bitcast.32, ...), custom_call_target="tpu_custom_call" | custom-call | tf_op jit(solution)/shard_map/first/pallas_call | solution.py:784
  268.1 127.5 %middle.1 = (bf16[3,2048,128]{2,1,0:T(8,128)(2,1)}, bf16[128,2048]{1,0:T(8,128)(2,1)}, bf16[2048,512]{1,0:T(8,128)(2,1)}, bf16[512,2048]{1,0:T(8,128)(2,1)}, f32...) custom-call(bf16[1024,2048]{1,0:T(8,128)(2,1)} %get-tuple-element.48, ...), custom_call_target="tpu_custom_call" | custom-call | tf_op jit(solution)/shard_map/middle/pallas_call | solution.py:784
  395.5 187.5 %last.1 = (bf16[3,512,512]{2,1,0:T(8,128)(2,1)}, bf16[512,512]{1,0:T(8,128)(2,1)}, bf16[512,2048]{1,0:T(8,128)(2,1)}, bf16[2048,512]{1,0:T(8,128)(2,1)}, bf16[2,...) custom-call(bf16[1024,2048]{1,0:T(8,128)(2,1)} %get-tuple-element.56.refs_0_, ...), custom_call_target="tpu_custom_call" | custom-call | tf_op jit(solution)/shard_map/last/pallas_call | solution.py:784
  583.0 0.7 slice.16
  583.7 1.3 fusion.1
  585.0 1.3 slice.17
  586.2 0.7 slice_bitcast_fusion
  586.9 0.6 copy.44
  587.5 2.3 bitcast_convert_fusion.3
  589.8 3.5 bitcast_convert_fusion.2
  593.3 2.5 bitcast_convert_fusion.1
  595.8 2.6 bitcast_convert_fusion
  598.4 0.5 copy.48
  598.9 0.8 copy.49
  599.7 0.8 copy.50
  (20 shorter events, 0.1 us)
Async XLA Ops:
  0.6 0.7 copy-start
  583.7 14.7 %copy-start.6 = (f32[1,128]{1,0:T(1,128)}, f32[1,128]{1,0:T(1,128)S(1)}, u32[]{:S(2)}) copy-start(f32[1,128]{1,0:T(1,128)S(1)} %slice.16) | copy-start | bytes 1540
  587.5 5.8 copy-start.3
  593.3 2.5 copy-start.2
  593.3 7.3 %copy-start.1 = (s32[2,1024]{1,0:T(2,128)S(1)}, s32[2,1024]{1,0:T(2,128)}, u32[]{:S(2)}) copy-start(s32[2,1024]{1,0:T(2,128)} %param.13) | copy-start | bytes 24580
  595.8 3.1 copy-start.5
  595.8 3.9 copy-start.4
